TPU v7x, 32 devices: a whole 2x2x4 slice. The times are simulated.
32 devices in a mesh: gx: 2 (over x), gy: 4 (over z), gz: 4 (over y, core).
Axes of the slice: x: 2, y: 2, z: 4, core: 2. Of those that a mesh axis runs over, the one named last changes fastest.
Arguments:
- right_side: float32 [48, 96, 512], P('gx', 'gy', 'gz'), may hold values from -6 to 6
- reaction: float32 [48, 96, 512], P('gx', 'gy', 'gz'), may hold values from 0.05 to 2
- basis_x: float32 [40, 40], replicated, may hold values from -1 to 1
- basis_y: float32 [40, 40], replicated, may hold values from -1 to 1
- basis_z: float32 [144, 144], replicated, may hold values from -0.5 to 0.5
- eigen_x: float32 [40], replicated, may hold values from 0.5 to 6
- eigen_y: float32 [40], replicated, may hold values from 0.5 to 6
- eigen_z: float32 [144], replicated, may hold values from 0.5 to 6
Outputs:
- solution: float32 [48, 96, 512], P('gx', 'gy', 'gz')
All inputs are finite; a program needn't handle non-finite values.
Results may differ from a plain program's by a relative error of at most 0.0003.
Values sent between devices are 32-bit elements; how exact they have to be, the bound alone decides.
No kernel may reach another device: no remote copies, remote signals or barrier semaphores. Data moves between devices by JAX's collectives and lax.ppermute only.
A program may use at most 64 MiB of HBM per device.

v0:
```python
import functools
import math

import jax
import jax.numpy as jnp
from jax import lax
from jax.experimental import pallas as pl
from jax.experimental.pallas import tpu as pltpu
from jax.sharding import PartitionSpec as P

LANES = 128
RING = 256
F32 = jnp.float32
BF16 = jnp.bfloat16


def pairs(count, first):
    swaps = {}
    for low in range(first, count - 1, 2):
        swaps[low], swaps[low + 1] = low + 1, low
    return [(i, swaps.get(i, i)) for i in range(count)]


def swap(one, two, axis):
    count = lax.axis_size(axis)
    return lax.ppermute(one, axis, pairs(count, 0)), lax.ppermute(two, axis, pairs(count, 1))


def call(kernel, outs, *args, scratch=(), smem=1, after=()):
    vmem = pl.BlockSpec(memory_space=pltpu.VMEM)
    specs = [pl.BlockSpec(memory_space=pltpu.SMEM)] * smem + [vmem] * (len(args) - smem)
    specs += [pl.BlockSpec(memory_space=pl.ANY)] * len(after)
    used = len(args)
    held = sum(math.prod(s.shape) * 4 for s in scratch)

    def body(*refs):
        kernel(*refs[:used], *refs[used + len(after) :])

    return pl.pallas_call(
        body,
        out_shape=[jax.ShapeDtypeStruct(s, F32) for s in outs],
        in_specs=specs,
        out_specs=[vmem] * len(outs),
        scratch_shapes=list(scratch),
        compiler_params=pltpu.CompilerParams(vmem_limit_bytes=held + 6 * 1024 * 1024),
    )(*args, *after)


class Side:
    def __init__(self, index, count):
        self.even = index % 2 == 0
        self.has_below = index > 0
        self.has_above = index < count - 1
        self.one_valid = jnp.where(self.even, self.has_above, self.has_below)
        self.two_valid = jnp.where(self.even, self.has_below, self.has_above)

    def one(self, above, below):
        return jnp.where(self.even, above, below)

    def two(self, above, below):
        return jnp.where(self.even, below, above)


def rows_of(start, size):
    return pl.ds(pl.multiple_of(start, 8), size)


def lane_of(shape):
    return lax.broadcasted_iota(jnp.int32, shape, 1)


def group_of(count, width):
    return -(-count // (LANES // width))


def pack(load, count, rows, width, src, out):
    each = group_of(count, width)
    lane = lane_of((rows, LANES))

    def member(j, carry):
        value = jnp.zeros((rows, LANES), F32)
        for g in range(-(-count // each)):
            x = jnp.minimum(g * each + j, count - 1)
            turned = pltpu.roll(load(x), (g * width - src + LANES) % LANES, 1)
            value = jnp.where((lane >= g * width) & (lane < (g + 1) * width), turned, value)
        out[rows_of(j * rows, rows), :] = value
        return carry

    lax.fori_loop(0, each, member, 0, unroll=each <= 3)


def unpack(ref, x, count, rows, width, dst, valid):
    each = group_of(count, width)
    g, j = x // each, x % each
    turned = pltpu.roll(ref[rows_of(j * rows, rows), :], (dst - g * width + LANES) % LANES, 1)
    away = (lane_of((rows, LANES)) - dst + LANES) % LANES
    return jnp.where((away < width) & valid, turned, 0.0)


def split(value):
    high = value.astype(BF16)
    return high, (value - high.astype(F32)).astype(BF16)


def stack_rows(value):
    high, low = split(value)
    return jnp.concatenate([high, high, low], axis=0)


def dot(a, b):
    return jnp.dot(a, b, preferred_element_type=F32)


def dot_nt(a, b):
    return lax.dot_general(a, b, (((1,), (1,)), ((), ())), preferred_element_type=F32)


def first_slabs(info, *refs, ny, ov):
    parts, (one, two) = refs[:-2], refs[-2:]
    side = Side(info[1], ny)
    cx, cy, _ = parts[0].shape
    for k, part in enumerate(parts):
        one[k * cx : (k + 1) * cx] = part[:, rows_of(side.one(cy - ov, 0), ov), :]
        two[k * cx : (k + 1) * cx] = part[:, rows_of(side.two(cy - ov, 0), ov), :]


def second_slabs(info, *refs, ny, nz, ov):
    parts, (got_one, got_two, field, one, two) = refs[:-5], refs[-5:]
    side, along = Side(info[1], ny), Side(info[2], nz)
    cx, cy, cz = parts[0].shape
    ey = cy + 2 * ov
    count = len(parts) * cx
    for k, part in enumerate(parts):

        def place(x, carry, k=k, part=part):
            a = got_one[k * cx + x]
            b = got_two[k * cx + x]
            row = (k * cx + x) * ey
            above = jnp.where(side.even, a, b)
            below = jnp.where(side.even, b, a)
            field[rows_of(row, ov), :] = jnp.where(side.has_below, below, 0.0)
            field[rows_of(row + ov, cy), :] = part[x]
            field[rows_of(row + ov + cy, ov), :] = jnp.where(side.has_above, above, 0.0)
            return carry

        lax.fori_loop(0, cx, place, 0)

    def load(x):
        return field[rows_of(x * ey, ey), :]

    pack(load, count, ey, ov, along.one(cz - ov, 0), one)
    pack(load, count, ey, ov, along.two(cz - ov, 0), two)


def extended(field, got_one, got_two, x, count, ey, ov, along):
    halo = unpack(got_one, x, count, ey, ov, along.one(0, LANES - ov), along.one_valid)
    halo = halo + unpack(got_two, x, count, ey, ov, along.two(0, LANES - ov), along.two_valid)
    return jnp.concatenate([field[rows_of(x * ey, ey), :], halo], axis=1)


def turn(value):
    group = LANES // 8
    row = lax.broadcasted_iota(jnp.int32, (8, LANES), 0)
    column = lane_of((8, LANES)) // group
    for bit in (4, 2, 1):
        up = pltpu.roll(pltpu.roll(value, 8 - bit, 0), bit * group, 1)
        down = pltpu.roll(pltpu.roll(value, bit, 0), LANES - bit * group, 1)
        moved = jnp.where((row & bit) == 0, up, down)
        value = jnp.where((row & bit) == (column & bit), value, moved)
    return value


def solve(source, store, tables, state, count, back, ey):
    zt, y_on, y_back, x_on, x_back, recip = tables
    s0, s1 = state
    z_high, z_low = split(zt[...])
    modes = recip.shape[1]
    group = LANES // 8
    lane = lane_of((ey, LANES))
    octs = ey // 8
    nothing = jnp.zeros((ey, LANES), F32)

    def times_y(table, core, side):
        two = 2 * ey
        first = dot(table[...], stack_rows(jnp.concatenate([core[:two], core[two : 2 * two]], axis=1)))
        second = dot(table[...], stack_rows(jnp.concatenate([core[2 * two : 3 * two], core[3 * two :]], axis=1)))
        third = dot(table[...], stack_rows(jnp.concatenate([side, nothing], axis=0)))
        return jnp.concatenate([first[:, :LANES], first[:, LANES:], second[:, :LANES], second[:, LANES:]], axis=0), third[:ey]

    def on(k, carry):
        high, low = split(jnp.concatenate([source(8 * k + j) for j in range(8)], axis=0))
        value = dot(high, z_high) + (dot(high, z_low) + dot(low, z_high))
        side = nothing
        for j in range(8):
            turned = pltpu.roll(value[j * ey : (j + 1) * ey, LANES:], j * group, 1)
            side = jnp.where(lane // group == j, turned, side)
        core, side = times_y(y_on, value[:, :LANES], side)
        s0[rows_of(k * 8 * ey, 8 * ey), :] = core
        for q in range(octs):
            s1[rows_of(q * count + k * 8, 8), :] = turn(side[q * 8 : (q + 1) * 8])
        return carry

    lax.fori_loop(0, count // 8, on, 0, unroll=2)

    def times_x(value, factor):
        value = dot(x_on[...], stack_rows(value))
        value = jnp.concatenate([value[i * modes : (i + 1) * modes] * factor for i in range(value.shape[0] // modes)], axis=0)
        return dot(x_back[...], stack_rows(value))[:back]

    def middle(h, carry):
        q = 2 * h
        value = [s0[pl.ds(q + i, count, stride=ey), :] for i in range(2)]
        value = times_x(jnp.concatenate(value, axis=1), jnp.concatenate([recip[q], recip[q + 1]], axis=1))
        for i in range(2):
            s0[pl.ds(q + i, back, stride=ey), :] = value[:, i * LANES : (i + 1) * LANES]
        return carry

    for q in range(octs):
        value = times_x(s1[q * count : (q + 1) * count, :], recip[ey + q])
        s1[q * count : q * count + back, :] = value
    lax.fori_loop(0, ey // 2, middle, 0, unroll=4)

    def off(k, carry):
        side = jnp.concatenate([turn(s1[rows_of(q * count + k * 8, 8), :]) for q in range(octs)], axis=0)
        core, side = times_y(y_back, s0[rows_of(k * 8 * ey, 8 * ey), :], side)
        side = jnp.concatenate([side] + [pltpu.roll(side, LANES - j * group, 1) for j in range(1, 8)], axis=0)
        high, low = split(jnp.concatenate([core, side], axis=1))
        value = dot_nt(high, z_high) + (dot_nt(high, z_low) + dot_nt(low, z_high))
        for j in range(8):
            store(8 * k + j, value[j * ey : (j + 1) * ey])
        return carry

    lax.fori_loop(0, back // 8, off, 0, unroll=2 if back % 16 == 0 else 1)


def merged(core, halo, low):
    lane = lane_of(core.shape)
    return jnp.where((lane < LANES // 2) == low, core, halo)


def first_solve(info, field, got_one, got_two, zt, y_on, y_back, x_on, x_back, recip, u, block, one, two, s0, s1, *, nz, ov, ey, cz):
    along = Side(info[2], nz)
    count = field.shape[0] // ey
    w = 2 * ov + 1

    def source(x):
        value = extended(field, got_one, got_two, x, count, ey, ov, along)
        block[rows_of(x * ey, ey), :] = value
        return value

    def store(x, value):
        u[rows_of(x * ey, ey), :] = value

    solve(source, store, (zt, y_on, y_back, x_on, x_back, recip), (s0, s1), count, count, ey)

    for out, low in ((one, ~along.even), (two, along.even)):

        def load(x, low=low):
            rows = rows_of(x * ey, ey)
            return merged(u[rows, :LANES], u[rows, LANES:], low)

        pack(load, count, ey, w, jnp.where(low, LANES - ov, cz - ov - 1), out)


def sum_z(info, u, got_one, got_two, v, one, two, *, ny, nz, ov, ey, cz):
    side, along = Side(info[1], ny), Side(info[2], nz)
    count = u.shape[0] // ey
    w = 2 * ov + 1
    lane = lane_of((ey, LANES))
    inside = ((lane <= ov) & along.has_above) | ((lane >= LANES - ov - 1) & along.has_below)

    def add(x, carry):
        rows = rows_of(x * ey, ey)
        core, rest = u[rows, :LANES], u[rows, LANES:]
        for got, low, valid in ((got_one, ~along.even, along.one_valid), (got_two, along.even, along.two_valid)):
            part = unpack(got, x, count, ey, w, jnp.where(low, LANES - ov - 1, cz - ov), valid)
            mine = (lane < LANES // 2) == low
            core, rest = core + jnp.where(mine, part, 0.0), rest + jnp.where(mine, 0.0, part)
        v[rows, :LANES] = core
        v[rows, LANES:] = jnp.where(inside, rest, 0.0)
        return carry

    lax.fori_loop(0, count, add, 0, unroll=4)
    tall, halo = 2 * ov, 2 * (ov + 1)
    each = group_of(count, halo)
    for out, start, odd in (
        (one, side.one(ey - tall, 0), side.even),
        (two, side.two(ey - tall, 0), ~side.even),
    ):

        def main(x, carry, out=out, start=start):
            out[rows_of(x * tall, tall), :] = v[rows_of(x * ey + start, tall), :LANES]
            return carry

        lax.fori_loop(0, count, main, 0)
        base = count * tall

        def load(x, start=start):
            return v[rows_of(x * ey + start, tall), LANES:]

        pack(load, count, tall, halo, LANES - ov - 1, out.at[base : base + each * tall])
        base = base + each * tall
        for x in range(count):
            last, next_ = v[x * ey + ey - tall - 1 : x * ey + ey - tall, :], v[x * ey + tall : x * ey + tall + 1, :]
            row = jnp.where(odd, last, next_)
            out[base + x : base + x + 1, :] = row[:, :LANES]
            out[base + count + x : base + count + x + 1, :] = row[:, LANES:]


def second_solve(info, v, got_one, got_two, block, coef, c_one, c_two, zt, y_on, y_back, x_on, x_back, recip, u, first, one, two, s0, s1, side_part, resid, *, nx, ny, nz, ov, ey, cx, cz):
    side, along = Side(info[1], ny), Side(info[2], nz)
    count = coef.shape[0] // ey
    tall, halo = 2 * ov, 2 * (ov + 1)
    each = group_of(count, halo)
    cy = ey - 2 * ov
    main_rows = count * tall
    odd_rows = main_rows + each * tall

    def slab(ref, x, valid):
        core = ref[rows_of(x * tall, tall), :]
        extra = unpack(ref.at[main_rows:odd_rows], x, count, tall, halo, LANES - ov - 1, True)
        return jnp.where(valid, jnp.concatenate([core, extra], axis=1), 0.0)

    def odd(ref, x, valid):
        row = jnp.concatenate([ref[pl.ds(odd_rows + x, 1), :], ref[pl.ds(odd_rows + count + x, 1), :]], axis=1)
        return jnp.where(valid, row, 0.0)

    def gather(x, carry):
        a, b = slab(got_one, x, side.one_valid), slab(got_two, x, side.two_valid)
        above, below = jnp.where(side.even, a, b), jnp.where(side.even, b, a)
        value = v[rows_of(x * ey, ey), :]
        value = jnp.concatenate([value[:tall] + below, value[tall : ey - tall], value[ey - tall :] + above], axis=0)
        y = lax.broadcasted_iota(jnp.int32, (ey, RING), 0)
        value = jnp.where(((y >= ov) | side.has_below) & ((y < ey - ov) | side.has_above), value, 0.0)
        a, b = odd(got_one, x, side.one_valid), odd(got_two, x, side.two_valid)
        near = lax.broadcasted_iota(jnp.int32, (8, RING), 0)
        under = jnp.where(near == 7, jnp.where(side.even, b, a), 0.0)
        over = jnp.where(near == 0, jnp.where(side.even, a, b), 0.0)
        center = value
        full = jnp.concatenate([under, value, over], axis=0)
        sum_y = full[7 : 7 + ey] + full[9 : 9 + ey]

        @pl.when(x < cx)
        def _():
            first[rows_of(x * cy, cy), :] = center[ov : ov + cy, :LANES]

        p = sum_y + pltpu.roll(center, 1, 1) + pltpu.roll(center, RING - 1, 1)
        q = pltpu.roll(sum_y, 1, 1) + pltpu.roll(sum_y, RING - 1, 1)
        f = block[rows_of(x * ey, ey), :]
        c = extended(coef, c_one, c_two, x, count, ey, ov, along)
        rows = rows_of(x * ey, ey)
        side_part[rows, :] = 0.5 * center + 0.125 * p + 0.0625 * q
        resid[rows, :] = f - (c + 5.0) * center + (0.5 * p + 0.125 * q)
        return carry

    lax.fori_loop(0, count, gather, 0, unroll=2)

    lane = lane_of((ey, RING))
    y = lax.broadcasted_iota(jnp.int32, (ey, RING), 0)
    inside = (lane < cz) | ((lane < cz + ov) & along.has_above) | ((lane >= RING - ov) & along.has_below)
    inside = inside & ((y >= ov) | side.has_below) & ((y < ey - ov) | side.has_above)

    def plane(x):
        at = (info[0] * cx + x) % count
        value = resid[rows_of(x * ey, ey), :]
        before = side_part[rows_of((x + count - 1) % count * ey, ey), :]
        after = side_part[rows_of((x + 1) % count * ey, ey), :]
        value = value + jnp.where(at > 0, before, 0.0) + jnp.where(at < count - 1, after, 0.0)
        return jnp.where(inside, value, 0.0)

    def store(x, value):
        rows = rows_of(x * ey, ey)
        u[rows, :] = value[:, :LANES]
        resid[rows, :LANES] = value[:, LANES:]

    solve(plane, store, (zt, y_on, y_back, x_on, x_back, recip), (s0, s1), count, cx, ey)

    def load(x):
        return resid[rows_of(x * ey, ey), :LANES]

    pack(load, cx, ey, ov, along.one(0, LANES - ov), one)
    pack(load, cx, ey, ov, along.two(0, LANES - ov), two)


def last_sum_z(info, u, got_one, got_two, v, one, two, *, ny, nz, ov, ey, cx, cz):
    side, along = Side(info[1], ny), Side(info[2], nz)

    def add(x, carry):
        rows = rows_of(x * ey, ey)
        value = u[rows, :]
        value = value + unpack(got_one, x, cx, ey, ov, along.one(cz - ov, 0), along.one_valid)
        value = value + unpack(got_two, x, cx, ey, ov, along.two(cz - ov, 0), along.two_valid)
        v[rows, :] = value
        one[rows_of(x * ov, ov), :] = v[rows_of(x * ey + side.one(ey - ov, 0), ov), :]
        two[rows_of(x * ov, ov), :] = v[rows_of(x * ey + side.two(ey - ov, 0), ov), :]
        return carry

    lax.fori_loop(0, cx, add, 0)


def last_sum_y(info, v, got_one, got_two, first, out, *, ny, ov, ey, cx):
    side = Side(info[1], ny)
    cy = ey - 2 * ov

    def add(x, carry):
        a, b = got_one[rows_of(x * ov, ov), :], got_two[rows_of(x * ov, ov), :]
        above, below = jnp.where(side.even, a, b), jnp.where(side.even, b, a)
        above, below = jnp.where(side.has_above, above, 0.0), jnp.where(side.has_below, below, 0.0)
        value = v[rows_of(x * ey + ov, cy), :] + first[rows_of(x * cy, cy), :]
        out[x] = jnp.concatenate([value[:ov] + below, value[ov : cy - ov], value[cy - ov :] + above], axis=0)
        return carry

    lax.fori_loop(0, cx, add, 0)


def reciprocals(eigen_x, rest, out):
    def row(q, carry):
        out[q] = 1.0 / (eigen_x[...] + rest[pl.ds(q, 1), :])
        return carry

    lax.fori_loop(0, out.shape[0], row, 0, unroll=5)


def gather_x(block):
    count = lax.axis_size("gx")
    return [block] + [lax.ppermute(block, "gx", [((i + shift) % count, i) for i in range(count)]) for shift in range(1, count)]


def columns(table):
    high = lax.reduce_precision(table, 8, 7)
    return jnp.concatenate([high, table - high, high], axis=1).astype(BF16)


def local(right_side, reaction, basis_x, basis_y, basis_z, eigen_x, eigen_y, eigen_z):
    cx, cy, cz = right_side.shape
    ex, ey, ez = basis_x.shape[0], basis_y.shape[0], basis_z.shape[0]
    ov = (ex - cx) // 2
    nx, ny, nz = lax.axis_size("gx"), lax.axis_size("gy"), lax.axis_size("gz")
    ix, iy, iz = lax.axis_index("gx"), lax.axis_index("gy"), lax.axis_index("gz")
    count = nx * cx
    info = jnp.stack([ix, iy, iz]).astype(jnp.int32)
    w, tall, halo = 2 * ov + 1, 2 * ov, 2 * (ov + 1)
    at = dict(ov=ov, ey=ey, cz=cz)

    f_parts = gather_x(right_side)
    c_parts = gather_x(lax.optimization_barrier((reaction, f_parts[-1]))[0])

    blocks = [jnp.pad(basis_x.T, ((0, 0), (i * cx, (nx - 1 - i) * cx)))[:, ov : ov + count] for i in range(nx)]
    table = jnp.concatenate(blocks, axis=0)
    table = lax.dynamic_slice_in_dim(jnp.concatenate([table, table], axis=1), ix * cx, count, axis=1)
    zero = jnp.zeros((ey, ey), F32)
    double = jnp.concatenate([jnp.concatenate([basis_y, zero], axis=1), jnp.concatenate([zero, basis_y], axis=1)], axis=0)
    zt = jnp.concatenate([basis_z[ov:], jnp.zeros((RING - ez, ez), F32), basis_z[:ov]], axis=0)
    zt = jnp.pad(zt, ((0, 0), (0, RING - ez)))
    rest = eigen_y[:, None] + eigen_z[None, :]
    rest = jnp.concatenate([rest[:, :LANES], rest[:, LANES:].reshape(-1, LANES)], axis=0)
    recip = call(reciprocals, [(rest.shape[0], ex, LANES)], jnp.broadcast_to(eigen_x[:, None], (ex, LANES)), rest, smem=0)[0]
    tables = (zt, columns(double.T), columns(double), columns(table), columns(table.T), recip)

    def y_slabs(parts, after=()):
        return call(functools.partial(first_slabs, ny=ny, ov=ov), [(count, ov, cz)] * 2, info, *parts, after=after)

    def z_slabs(parts, got, after=()):
        small = (group_of(count, ov) * ey, LANES)
        return call(functools.partial(second_slabs, ny=ny, nz=nz, ov=ov), [(count * ey, cz), small, small], info, *parts, *got, after=after)

    f, *slabs = z_slabs(f_parts, swap(*y_slabs(f_parts), "gy"))
    c_slabs = y_slabs(c_parts, after=slabs[:1])
    got, c_got = swap(*slabs, "gz"), swap(*c_slabs, "gy")
    state = [pltpu.VMEM((count * ey, LANES), F32), pltpu.VMEM((ey // 8 * count, LANES), F32)]
    small = (group_of(count, w) * ey, LANES)
    u, block, *slabs = call(
        functools.partial(first_solve, nz=nz, **at), [(count * ey, RING)] * 2 + [small, small], info, f, *got, *tables, scratch=state, after=c_slabs[:1]
    )
    c, *c_slabs = z_slabs(c_parts, c_got, after=slabs[:1])
    got, c_got = swap(*slabs, "gz"), swap(*c_slabs, "gz")
    tall_rows = (count * tall + group_of(count, halo) * tall + 2 * count, LANES)
    v, *slabs = call(functools.partial(sum_z, ny=ny, nz=nz, **at), [(count * ey, RING), tall_rows, tall_rows], info, u, *got, after=c_slabs[:1])
    got = swap(*slabs, "gy")
    small = (group_of(cx, ov) * ey, LANES)
    state = state + [pltpu.VMEM((count * ey, RING), F32)] * 2
    u, first, *slabs = call(
        functools.partial(second_solve, nx=nx, ny=ny, nz=nz, cx=cx, **at),
        [(cx * ey, LANES), (cx * cy, LANES), small, small], info, v, *got, block, c, *c_got, *tables, scratch=state,
    )
    got = swap(*slabs, "gz")
    v, *slabs = call(functools.partial(last_sum_z, ny=ny, nz=nz, cx=cx, **at), [(cx * ey, LANES)] + [(cx * ov, LANES)] * 2, info, u, *got)
    got = swap(*slabs, "gy")
    return call(functools.partial(last_sum_y, ny=ny, ov=ov, ey=ey, cx=cx), [(cx, cy, cz)], info, v, *got, first)[0]


def solution(mesh):
    return jax.shard_map(
        local,
        mesh=mesh,
        in_specs=(P("gx", "gy", "gz"), P("gx", "gy", "gz"), P(), P(), P(), P(), P(), P()),
        out_specs=P("gx", "gy", "gz"),
        check_vma=False,
    )
```

profile of v0, /device:TPU:1, one launch (start us, length us, event | category | flops | bytes accessed | tf_op | source)
XLA Modules:
  0.0 98.5 jit_solution(9939020190717783766)
XLA Ops:
  0.0 2.0 %collective-permute-start = (f32[24,24,128]{2,1,0:T(8,128)}, f32[24,24,128]{2,1,0:T(8,128)S(1)}, u32[]{:S(2)}, u32[]{:S(2)}) collective-permute-start(f32[24,24,128]{2,1,0:T(8,128)} %refs_1_.3), channel_id=1, source_target_pairs={{16,0},{0,16},{17,1},{1,17},{18,2},{2,18},{19,3},{3,19},{20,4},{4,... | collective-permute-start | bytes 884744 | tf_op jit(solution)/shard_map/ppermute | solution.py:426
  2.0 0.8 pad_slice_fusion.1
  2.8 0.1 fusion.3
  3.0 0.8 broadcast_add_fusion
  3.7 0.9 fusion
  4.6 0.9 fusion.1
  5.5 0.9 slice.18
  6.4 0.7 slice.19
  7.1 0.1 reshape.6
  7.2 0.1 pad.38.clone
  7.3 0.1 pad_maximum_fusion.4.refs_8_.refs_12_
  7.4 0.1 pad_maximum_fusion.2.refs_6_.refs_10_
  7.5 1.5 %collective-permute-done.refs_2_ = f32[24,24,128]{2,1,0:T(8,128)S(1)} collective-permute-done((f32[24,24,128]{2,1,0:T(8,128)}, f32[24,24,128]{2,1,0:T(8,128)S(1)}, u32[]{:S(2)}, u32[]{:S(2)}) %collective-permute-start) | collective-permute-done | bytes 294944 | tf_op jit(solution)/shard_map/ppermute | solution.py:426
  9.0 1.1 %collective-permute-start.5 = (f32[24,24,128]{2,1,0:T(8,128)}, f32[24,24,128]{2,1,0:T(8,128)S(1)}, u32[]{:S(2)}, u32[]{:S(2)}) collective-permute-start(f32[24,24,128]{2,1,0:T(8,128)} %refs_1_.5), channel_id=1, source_target_pairs={{16,0},{0,16},{17,1},{1,17},{18,2},{2,18},{19,3},{3,19},{20,4},{4,... | collective-permute-start | bytes 884744 | tf_op jit(solution)/shard_map/ppermute | solution.py:426
  10.1 0.1 pad_add_fusion.refs_0_
  10.2 1.0 copy-done
  11.2 0.6 shard_map.82
  11.8 1.4 %collective-permute-start.1 = (f32[48,8,128]{2,1,0:T(8,128)S(1)}, f32[48,8,128]{2,1,0:T(8,128)S(1)}, u32[]{:S(2)}, u32[]{:S(2)}) collective-permute-start(f32[48,8,128]{2,1,0:T(8,128)S(1)} %get-tuple-element.30), channel_id=1, source_target_pairs={{0,4},{4,0},{8,12},{12,8},{1,5},{5,1},{9,13},{13,9},{2,6},{6,2},{1... | collective-permute-start | bytes 589832 | tf_op jit(solution)/shard_map/ppermute | solution.py:26
  13.1 0.7 collective-permute-start.2
  13.8 0.1 pad_maximum_fusion
  13.9 2.7 %collective-permute-done.1.refs_3_ = f32[48,8,128]{2,1,0:T(8,128)S(1)} collective-permute-done((f32[48,8,128]{2,1,0:T(8,128)S(1)}, f32[48,8,128]{2,1,0:T(8,128)S(1)}, u32[]{:S(2)}, u32[]{:S(2)}) %collective-permute-start.1) | collective-permute-done | bytes 196640 | tf_op jit(solution)/shard_map/ppermute | solution.py:26
  16.6 0.0 collective-permute-done.2.refs_4_
  16.6 0.0 copy-done.1
  16.6 1.5 %shard_map.83 = (f32[1920,128]{1,0:T(8,128)S(1)}, f32[120,128]{1,0:T(8,128)S(1)}, f32[120,128]{1,0:T(8,128)S(1)}) custom-call(s32[3]{0:T(128)S(1)} %pad_add_fusion.refs_0_, f32[24,24,128]{2,1,0:T(8,128)S(1)} %copy-done.1, f32[24,24,128]{2,1,0:T(8,128)S(1)} %collective-permute-done.refs_2_, f32[48,8,128]{2,1,0:T(8,128)S(1)} %collective-permute-done.1.refs_3_, ...), custom_call_target="tpu_custom_call" | custom-call | tf_op jit(solution)/shard_map/pallas_call | solution.py:39
  18.2 2.7 %collective-permute-start.3 = (f32[120,128]{1,0:T(8,128)S(1)}, f32[120,128]{1,0:T(8,128)S(1)}, u32[]{:S(2)}, u32[]{:S(2)}) collective-permute-start(f32[120,128]{1,0:T(8,128)S(1)} %get-tuple-element.33.refs_3_), channel_id=1, source_target_pairs={{0,1},{1,0},{2,3},{3,2},{4,5},{5,4},{6,7},{7,6},{8,9},{9,8},{10,11... | collective-permute-start | bytes 184328 | tf_op jit(solution)/shard_map/ppermute | solution.py:26
  20.9 3.0 %collective-permute-start.4 = (f32[120,128]{1,0:T(8,128)S(1)}, f32[120,128]{1,0:T(8,128)S(1)}, u32[]{:S(2)}, u32[]{:S(2)}) collective-permute-start(f32[120,128]{1,0:T(8,128)S(1)} %get-tuple-element.34), channel_id=1, source_target_pairs={{0,0},{1,2},{2,1},{3,3},{4,4},{5,6},{6,5},{7,7},{8,8},{9,10},{10,9... | collective-permute-start | bytes 184328 | tf_op jit(solution)/shard_map/ppermute | solution.py:26
  23.9 0.0 collective-permute-done.5.refs_2_
  24.0 0.6 shard_map.85
  24.5 4.4 %collective-permute-start.8 = (f32[48,8,128]{2,1,0:T(8,128)S(1)}, f32[48,8,128]{2,1,0:T(8,128)S(1)}, u32[]{:S(2)}, u32[]{:S(2)}) collective-permute-start(f32[48,8,128]{2,1,0:T(8,128)S(1)} %get-tuple-element.36.refs_10_), channel_id=1, source_target_pairs={{0,4},{4,0},{8,12},{12,8},{1,5},{5,1},{9,13},{13,9},{2,6},{6,2},{1... | collective-permute-start | bytes 589832 | tf_op jit(solution)/shard_map/ppermute | solution.py:26
  28.9 0.7 collective-permute-start.9
  29.6 0.1 copy.14.refs_7_.refs_11_
  29.7 0.1 copy.13.refs_5_.refs_9_
  29.8 0.1 broadcast_in_dim.5.refs_0_
  29.9 0.2 shard_map.84.refs_9_.refs_13_
  30.1 0.0 collective-permute-done.3.refs_2_
  30.1 0.0 collective-permute-done.4.refs_3_
  30.1 12.3 %shard_map.86 = (f32[1920,256]{1,0:T(8,128)S(1)}, f32[1920,256]{1,0:T(8,128)S(1)}, f32[280,128]{1,0:T(8,128)S(1)}, f32[280,128]{1,0:T(8,128)S(1)}) custom-call(s32[3]{0:T(128)S(1)} %pad_add_fusion.refs_0_, f32[1920,128]{1,0:T(8,128)S(1)} %get-tuple-element.32.refs_1_, f32[120,128]{1,0:T(8,128)S(1)} %collective-permute-done.3.refs_2_, ...), custom_call_target="tpu_custom_call" | custom-call | tf_op jit(solution)/shard_map/pallas_call | solution.py:39
  42.4 0.1 collective-permute-start.6
  42.5 2.8 %collective-permute-start.7 = (f32[280,128]{1,0:T(8,128)S(1)}, f32[280,128]{1,0:T(8,128)S(1)}, u32[]{:S(2)}, u32[]{:S(2)}) collective-permute-start(f32[280,128]{1,0:T(8,128)S(1)} %get-tuple-element.39), channel_id=1, source_target_pairs={{0,0},{1,2},{2,1},{3,3},{4,4},{5,6},{6,5},{7,7},{8,8},{9,10},{10,9... | collective-permute-start | bytes 430088 | tf_op jit(solution)/shard_map/ppermute | solution.py:26
  45.3 0.0 collective-permute-done.8.refs_3_
  45.3 0.0 collective-permute-done.9.refs_4_
  45.3 1.5 %shard_map.87 = (f32[1920,128]{1,0:T(8,128)S(1)}, f32[120,128]{1,0:T(8,128)S(1)}, f32[120,128]{1,0:T(8,128)S(1)}) custom-call(s32[3]{0:T(128)S(1)} %pad_add_fusion.refs_0_, f32[24,24,128]{2,1,0:T(8,128)S(1)} %copy-done.2, f32[24,24,128]{2,1,0:T(8,128)S(1)} %collective-permute-done.5.refs_2_, f32[48,8,128]{2,1,0:T(8,128)S(1)} %collective-permute-done.8.refs_3_, ...), custom_call_target="tpu_custom_call" | custom-call | tf_op jit(solution)/shard_map/pallas_call | solution.py:39
  46.8 0.0 collective-permute-done.6.refs_2_
  46.8 2.1 %collective-permute-done.7.refs_3_ = f32[280,128]{1,0:T(8,128)S(1)} collective-permute-done((f32[280,128]{1,0:T(8,128)S(1)}, f32[280,128]{1,0:T(8,128)S(1)}, u32[]{:S(2)}, u32[]{:S(2)}) %collective-permute-start.7) | collective-permute-done | bytes 143392 | tf_op jit(solution)/shard_map/ppermute | solution.py:26
  48.9 4.1 %shard_map.88 = (f32[1920,256]{1,0:T(8,128)S(1)}, f32[976,128]{1,0:T(8,128)S(1)}, f32[976,128]{1,0:T(8,128)S(1)}) custom-call(s32[3]{0:T(128)S(1)} %pad_add_fusion.refs_0_, f32[1920,256]{1,0:T(8,128)S(1)} %get-tuple-element.37.refs_1_, f32[280,128]{1,0:T(8,128)S(1)} %collective-permute-done.6.refs_2_, f32[280,128]{1,0:T(8,128)S(1)} %collective-permute-done.7.refs_3_, ...), custom_call_target="tpu_custom_call" | custom-call | tf_op jit(solution)/shard_map/pallas_call | solution.py:39
  53.0 3.1 %collective-permute-start.10 = (f32[976,128]{1,0:T(8,128)S(1)}, f32[976,128]{1,0:T(8,128)S(1)}, u32[]{:S(2)}, u32[]{:S(2)}) collective-permute-start(f32[976,128]{1,0:T(8,128)S(1)} %get-tuple-element.43), channel_id=1, source_target_pairs={{0,4},{4,0},{8,12},{12,8},{1,5},{5,1},{9,13},{13,9},{2,6},{6,2},{1... | collective-permute-start | bytes 1499144 | tf_op jit(solution)/shard_map/ppermute | solution.py:26
  56.0 0.7 collective-permute-start.11
  56.7 0.1 collective-permute-start.12
  56.8 3.1 %collective-permute-start.13 = (f32[120,128]{1,0:T(8,128)S(1)}, f32[120,128]{1,0:T(8,128)S(1)}, u32[]{:S(2)}, u32[]{:S(2)}) collective-permute-start(f32[120,128]{1,0:T(8,128)S(1)} %get-tuple-element.47), channel_id=1, source_target_pairs={{0,0},{1,2},{2,1},{3,3},{4,4},{5,6},{6,5},{7,7},{8,8},{9,10},{10,9... | collective-permute-start | bytes 184328 | tf_op jit(solution)/shard_map/ppermute | solution.py:26
  59.9 0.0 collective-permute-done.12.refs_6_
  59.9 2.5 %collective-permute-done.13.refs_7_ = f32[120,128]{1,0:T(8,128)S(1)} collective-permute-done((f32[120,128]{1,0:T(8,128)S(1)}, f32[120,128]{1,0:T(8,128)S(1)}, u32[]{:S(2)}, u32[]{:S(2)}) %collective-permute-start.13) | collective-permute-done | bytes 61472 | tf_op jit(solution)/shard_map/ppermute | solution.py:26
  62.3 1.8 %collective-permute-done.10.refs_2_ = f32[976,128]{1,0:T(8,128)S(1)} collective-permute-done((f32[976,128]{1,0:T(8,128)S(1)}, f32[976,128]{1,0:T(8,128)S(1)}, u32[]{:S(2)}, u32[]{:S(2)}) %collective-permute-start.10) | collective-permute-done | bytes 499744 | tf_op jit(solution)/shard_map/ppermute | solution.py:26
  64.2 0.0 collective-permute-done.11.refs_3_
  64.2 18.8 %shard_map.89 = (f32[960,128]{1,0:T(8,128)S(1)}, f32[576,128]{1,0:T(8,128)S(1)}, f32[80,128]{1,0:T(8,128)S(1)}, f32[80,128]{1,0:T(8,128)S(1)}) custom-call(s32[3]{0:T(128)S(1)} %pad_add_fusion.refs_0_, f32[1920,256]{1,0:T(8,128)S(1)} %get-tuple-element.42.refs_1_, f32[976,128]{1,0:T(8,128)S(1)} %collective-permute-done.10.refs_2_, ...), custom_call_target="tpu_custom_call" | custom-call | tf_op jit(solution)/shard_map/pallas_call | solution.py:39
  83.0 0.1 collective-permute-start.14
  83.1 2.8 %collective-permute-start.15 = (f32[80,128]{1,0:T(8,128)S(1)}, f32[80,128]{1,0:T(8,128)S(1)}, u32[]{:S(2)}, u32[]{:S(2)}) collective-permute-start(f32[80,128]{1,0:T(8,128)S(1)} %get-tuple-element.50), channel_id=1, source_target_pairs={{0,0},{1,2},{2,1},{3,3},{4,4},{5,6},{6,5},{7,7},{8,8},{9,10},{10,9... | collective-permute-start | bytes 122888 | tf_op jit(solution)/shard_map/ppermute | solution.py:26
  85.9 0.0 collective-permute-done.14.refs_2_
  85.9 2.5 %collective-permute-done.15.refs_3_ = f32[80,128]{1,0:T(8,128)S(1)} collective-permute-done((f32[80,128]{1,0:T(8,128)S(1)}, f32[80,128]{1,0:T(8,128)S(1)}, u32[]{:S(2)}, u32[]{:S(2)}) %collective-permute-start.15) | collective-permute-done | bytes 40992 | tf_op jit(solution)/shard_map/ppermute | solution.py:26
  88.4 2.8 %shard_map.90 = (f32[960,128]{1,0:T(8,128)S(1)}, f32[192,128]{1,0:T(8,128)S(1)}, f32[192,128]{1,0:T(8,128)S(1)}) custom-call(s32[3]{0:T(128)S(1)} %pad_add_fusion.refs_0_, f32[960,128]{1,0:T(8,128)S(1)} %get-tuple-element.48.refs_1_, f32[80,128]{1,0:T(8,128)S(1)} %collective-permute-done.14.refs_2_, f32[80,128]{1,0:T(8,128)S(1)} %collective-permute-done.15.refs_3_), custom_call_target="tpu_custom_call" | custom-call | tf_op jit(solution)/shard_map/pallas_call | solution.py:39
  91.3 3.7 %collective-permute-start.16 = (f32[192,128]{1,0:T(8,128)S(1)}, f32[192,128]{1,0:T(8,128)S(1)}, u32[]{:S(2)}, u32[]{:S(2)}) collective-permute-start(f32[192,128]{1,0:T(8,128)S(1)} %get-tuple-element.52), channel_id=1, source_target_pairs={{0,4},{4,0},{8,12},{12,8},{1,5},{5,1},{9,13},{13,9},{2,6},{6,2},{1... | collective-permute-start | bytes 294920 | tf_op jit(solution)/shard_map/ppermute | solution.py:26
  95.0 0.7 collective-permute-start.17
  95.6 1.3 %collective-permute-done.16.refs_2_ = f32[192,128]{1,0:T(8,128)S(1)} collective-permute-done((f32[192,128]{1,0:T(8,128)S(1)}, f32[192,128]{1,0:T(8,128)S(1)}, u32[]{:S(2)}, u32[]{:S(2)}) %collective-permute-start.16) | collective-permute-done | bytes 98336 | tf_op jit(solution)/shard_map/ppermute | solution.py:26
  97.0 0.0 collective-permute-done.17.refs_3_
  97.0 1.5 %shard_map.91 = f32[24,24,128]{2,1,0:T(8,128)} custom-call(s32[3]{0:T(128)S(1)} %pad_add_fusion.refs_0_, f32[960,128]{1,0:T(8,128)S(1)} %get-tuple-element.51.refs_1_, f32[192,128]{1,0:T(8,128)S(1)} %collective-permute-done.16.refs_2_, f32[192,128]{1,0:T(8,128)S(1)} %collective-permute-done.17.refs_3_, f32[576,128]{1,0:T(8,128)S(1)} %get-tuple-element.54.refs_4_), custom_call_target="tpu_custom_call" | custom-call | tf_op jit(solution)/shard_map/pallas_call | solution.py:39
  (15 shorter events, 0.1 us)
Async XLA Ops:
  0.0 16.6 %copy-start.1 = (f32[24,24,128]{2,1,0:T(8,128)S(1)}, f32[24,24,128]{2,1,0:T(8,128)}, u32[]{:S(2)}) copy-start(f32[24,24,128]{2,1,0:T(8,128)} %refs_1_.3) | copy-start | bytes 884740
  0.0 23.9 %copy-start.2 = (f32[24,24,128]{2,1,0:T(8,128)S(1)}, f32[24,24,128]{2,1,0:T(8,128)}, u32[]{:S(2)}) copy-start(f32[24,24,128]{2,1,0:T(8,128)} %refs_1_.5) | copy-start | bytes 884740
  0.0 9.0 %collective-permute-start = (f32[24,24,128]{2,1,0:T(8,128)}, f32[24,24,128]{2,1,0:T(8,128)S(1)}, u32[]{:S(2)}, u32[]{:S(2)}) collective-permute-start(f32[24,24,128]{2,1,0:T(8,128)} %refs_1_.3), channel_id=1, source_target_pairs={{16,0},{0,16},{17,1},{1,17},{18,2},{2,18},{19,3},{3,19},{20,4},{4,... | collective-permute-start | bytes 884744 | tf_op jit(solution)/shard_map/ppermute | solution.py:426
  5.5 24.3 %copy-start.3 = (f32[40]{0:T(128)S(1)}, f32[40]{0:T(128)}, u32[]{:S(2)}) copy-start(f32[40]{0:T(128)} %param.13) | copy-start | bytes 484
  9.0 14.9 %collective-permute-start.5 = (f32[24,24,128]{2,1,0:T(8,128)}, f32[24,24,128]{2,1,0:T(8,128)S(1)}, u32[]{:S(2)}, u32[]{:S(2)}) collective-permute-start(f32[24,24,128]{2,1,0:T(8,128)} %refs_1_.5), channel_id=1, source_target_pairs={{16,0},{0,16},{17,1},{1,17},{18,2},{2,18},{19,3},{3,19},{20,4},{4,... | collective-permute-start | bytes 884744 | tf_op jit(solution)/shard_map/ppermute | solution.py:426
  10.2 1.0 copy-start
  11.8 4.9 %collective-permute-start.1 = (f32[48,8,128]{2,1,0:T(8,128)S(1)}, f32[48,8,128]{2,1,0:T(8,128)S(1)}, u32[]{:S(2)}, u32[]{:S(2)}) collective-permute-start(f32[48,8,128]{2,1,0:T(8,128)S(1)} %get-tuple-element.30), channel_id=1, source_target_pairs={{0,4},{4,0},{8,12},{12,8},{1,5},{5,1},{9,13},{13,9},{2,6},{6,2},{1... | collective-permute-start | bytes 589832 | tf_op jit(solution)/shard_map/ppermute | solution.py:26
  13.1 3.5 %collective-permute-start.2 = (f32[48,8,128]{2,1,0:T(8,128)S(1)}, f32[48,8,128]{2,1,0:T(8,128)S(1)}, u32[]{:S(2)}, u32[]{:S(2)}) collective-permute-start(f32[48,8,128]{2,1,0:T(8,128)S(1)} %get-tuple-element.31), channel_id=1, source_target_pairs={{0,0},{4,8},{8,4},{12,12},{1,1},{5,9},{9,5},{13,13},{2,2},{6,10},{... | collective-permute-start | bytes 589832 | tf_op jit(solution)/shard_map/ppermute | solution.py:26
  18.2 12.0 %collective-permute-start.3 = (f32[120,128]{1,0:T(8,128)S(1)}, f32[120,128]{1,0:T(8,128)S(1)}, u32[]{:S(2)}, u32[]{:S(2)}) collective-permute-start(f32[120,128]{1,0:T(8,128)S(1)} %get-tuple-element.33.refs_3_), channel_id=1, source_target_pairs={{0,1},{1,0},{2,3},{3,2},{4,5},{5,4},{6,7},{7,6},{8,9},{9,8},{10,11... | collective-permute-start | bytes 184328 | tf_op jit(solution)/shard_map/ppermute | solution.py:26
  20.9 9.3 %collective-permute-start.4 = (f32[120,128]{1,0:T(8,128)S(1)}, f32[120,128]{1,0:T(8,128)S(1)}, u32[]{:S(2)}, u32[]{:S(2)}) collective-permute-start(f32[120,128]{1,0:T(8,128)S(1)} %get-tuple-element.34), channel_id=1, source_target_pairs={{0,0},{1,2},{2,1},{3,3},{4,4},{5,6},{6,5},{7,7},{8,8},{9,10},{10,9... | collective-permute-start | bytes 184328 | tf_op jit(solution)/shard_map/ppermute | solution.py:26
  24.5 20.7 %collective-permute-start.8 = (f32[48,8,128]{2,1,0:T(8,128)S(1)}, f32[48,8,128]{2,1,0:T(8,128)S(1)}, u32[]{:S(2)}, u32[]{:S(2)}) collective-permute-start(f32[48,8,128]{2,1,0:T(8,128)S(1)} %get-tuple-element.36.refs_10_), channel_id=1, source_target_pairs={{0,4},{4,0},{8,12},{12,8},{1,5},{5,1},{9,13},{13,9},{2,6},{6,2},{1... | collective-permute-start | bytes 589832 | tf_op jit(solution)/shard_map/ppermute | solution.py:26
  28.9 16.4 %collective-permute-start.9 = (f32[48,8,128]{2,1,0:T(8,128)S(1)}, f32[48,8,128]{2,1,0:T(8,128)S(1)}, u32[]{:S(2)}, u32[]{:S(2)}) collective-permute-start(f32[48,8,128]{2,1,0:T(8,128)S(1)} %get-tuple-element.40), channel_id=1, source_target_pairs={{0,0},{4,8},{8,4},{12,12},{1,1},{5,9},{9,5},{13,13},{2,2},{6,10},{... | collective-permute-start | bytes 589832 | tf_op jit(solution)/shard_map/ppermute | solution.py:26
  42.4 4.4 %collective-permute-start.6 = (f32[280,128]{1,0:T(8,128)S(1)}, f32[280,128]{1,0:T(8,128)S(1)}, u32[]{:S(2)}, u32[]{:S(2)}) collective-permute-start(f32[280,128]{1,0:T(8,128)S(1)} %get-tuple-element.38.refs_5_), channel_id=1, source_target_pairs={{0,1},{1,0},{2,3},{3,2},{4,5},{5,4},{6,7},{7,6},{8,9},{9,8},{10,11... | collective-permute-start | bytes 430088 | tf_op jit(solution)/shard_map/ppermute | solution.py:26
  42.5 6.4 %collective-permute-start.7 = (f32[280,128]{1,0:T(8,128)S(1)}, f32[280,128]{1,0:T(8,128)S(1)}, u32[]{:S(2)}, u32[]{:S(2)}) collective-permute-start(f32[280,128]{1,0:T(8,128)S(1)} %get-tuple-element.39), channel_id=1, source_target_pairs={{0,0},{1,2},{2,1},{3,3},{4,4},{5,6},{6,5},{7,7},{8,8},{9,10},{10,9... | collective-permute-start | bytes 430088 | tf_op jit(solution)/shard_map/ppermute | solution.py:26
  53.0 11.2 %collective-permute-start.10 = (f32[976,128]{1,0:T(8,128)S(1)}, f32[976,128]{1,0:T(8,128)S(1)}, u32[]{:S(2)}, u32[]{:S(2)}) collective-permute-start(f32[976,128]{1,0:T(8,128)S(1)} %get-tuple-element.43), channel_id=1, source_target_pairs={{0,4},{4,0},{8,12},{12,8},{1,5},{5,1},{9,13},{13,9},{2,6},{6,2},{1... | collective-permute-start | bytes 1499144 | tf_op jit(solution)/shard_map/ppermute | solution.py:26
  56.0 8.1 %collective-permute-start.11 = (f32[976,128]{1,0:T(8,128)S(1)}, f32[976,128]{1,0:T(8,128)S(1)}, u32[]{:S(2)}, u32[]{:S(2)}) collective-permute-start(f32[976,128]{1,0:T(8,128)S(1)} %get-tuple-element.44), channel_id=1, source_target_pairs={{0,0},{4,8},{8,4},{12,12},{1,1},{5,9},{9,5},{13,13},{2,2},{6,10},{... | collective-permute-start | bytes 1499144 | tf_op jit(solution)/shard_map/ppermute | solution.py:26
  56.7 3.1 %collective-permute-start.12 = (f32[120,128]{1,0:T(8,128)S(1)}, f32[120,128]{1,0:T(8,128)S(1)}, u32[]{:S(2)}, u32[]{:S(2)}) collective-permute-start(f32[120,128]{1,0:T(8,128)S(1)} %get-tuple-element.41.refs_4_), channel_id=1, source_target_pairs={{0,1},{1,0},{2,3},{3,2},{4,5},{5,4},{6,7},{7,6},{8,9},{9,8},{10,11... | collective-permute-start | bytes 184328 | tf_op jit(solution)/shard_map/ppermute | solution.py:26
  56.8 5.5 %collective-permute-start.13 = (f32[120,128]{1,0:T(8,128)S(1)}, f32[120,128]{1,0:T(8,128)S(1)}, u32[]{:S(2)}, u32[]{:S(2)}) collective-permute-start(f32[120,128]{1,0:T(8,128)S(1)} %get-tuple-element.47), channel_id=1, source_target_pairs={{0,0},{1,2},{2,1},{3,3},{4,4},{5,6},{6,5},{7,7},{8,8},{9,10},{10,9... | collective-permute-start | bytes 184328 | tf_op jit(solution)/shard_map/ppermute | solution.py:26
  83.0 2.9 %collective-permute-start.14 = (f32[80,128]{1,0:T(8,128)S(1)}, f32[80,128]{1,0:T(8,128)S(1)}, u32[]{:S(2)}, u32[]{:S(2)}) collective-permute-start(f32[80,128]{1,0:T(8,128)S(1)} %get-tuple-element.49), channel_id=1, source_target_pairs={{0,1},{1,0},{2,3},{3,2},{4,5},{5,4},{6,7},{7,6},{8,9},{9,8},{10,11... | collective-permute-start | bytes 122888 | tf_op jit(solution)/shard_map/ppermute | solution.py:26
  83.1 5.3 %collective-permute-start.15 = (f32[80,128]{1,0:T(8,128)S(1)}, f32[80,128]{1,0:T(8,128)S(1)}, u32[]{:S(2)}, u32[]{:S(2)}) collective-permute-start(f32[80,128]{1,0:T(8,128)S(1)} %get-tuple-element.50), channel_id=1, source_target_pairs={{0,0},{1,2},{2,1},{3,3},{4,4},{5,6},{6,5},{7,7},{8,8},{9,10},{10,9... | collective-permute-start | bytes 122888 | tf_op jit(solution)/shard_map/ppermute | solution.py:26
  91.3 5.7 %collective-permute-start.16 = (f32[192,128]{1,0:T(8,128)S(1)}, f32[192,128]{1,0:T(8,128)S(1)}, u32[]{:S(2)}, u32[]{:S(2)}) collective-permute-start(f32[192,128]{1,0:T(8,128)S(1)} %get-tuple-element.52), channel_id=1, source_target_pairs={{0,4},{4,0},{8,12},{12,8},{1,5},{5,1},{9,13},{13,9},{2,6},{6,2},{1... | collective-permute-start | bytes 294920 | tf_op jit(solution)/shard_map/ppermute | solution.py:26
  95.0 2.0 %collective-permute-start.17 = (f32[192,128]{1,0:T(8,128)S(1)}, f32[192,128]{1,0:T(8,128)S(1)}, u32[]{:S(2)}, u32[]{:S(2)}) collective-permute-start(f32[192,128]{1,0:T(8,128)S(1)} %get-tuple-element.53), channel_id=1, source_target_pairs={{0,0},{4,8},{8,4},{12,12},{1,1},{5,9},{9,5},{13,13},{2,2},{6,10},{... | collective-permute-start | bytes 294920 | tf_op jit(solution)/shard_map/ppermute | solution.py:26
where the time goes:
time: 100 us; the launch traced here: 98.5 us
  Pallas kernels  43.8 us (44%)
  starting transfers between devices  32.9 us (33%)
  waiting for transfers between devices  14.5 us (14%)
  local copies, waits for them, and re-layouts  3.83 us (4%)
  other arithmetic  3.01 us (3%)
    pallas_call x10, Pallas kernels, call(): pl.pallas_call(body, out_shape=[jax.ShapeDtypeStruct(s, F32) for s in out...  43.8 us
    ppermute x8, starting transfers between devices, swap(): lax.ppermute(one, axis, pairs(count, 0))  15.4 us
    ppermute x8, starting transfers between devices, swap(): lax.ppermute(two, axis, pairs(count, 1))  14.3 us
    ppermute x8, waiting for transfers between devices, swap(): lax.ppermute(two, axis, pairs(count, 1))  7.07 us
    ppermute x8, waiting for transfers between devices, swap(): lax.ppermute(one, axis, pairs(count, 0))  5.94 us
    ppermute x2, starting transfers between devices, gather_x(): lax.ppermute(block, 'gx', [((i + shift) % count, i) for i in range(count)])  3.14 us
  transfers between devices with their start and end apart: 18, of which 7 were waited for; matrix products, arithmetic and copies ran while one was open for 6% of the time, Pallas kernels for 17%

commit v1 on v0

--- a/solution.py
+++ b/solution.py
@@ -7,6 +7,7 @@
 from jax.experimental import pallas as pl
 from jax.experimental.pallas import tpu as pltpu
 from jax.sharding import PartitionSpec as P
+
 
 LANES = 128
 RING = 256
@@ -86,7 +87,7 @@
         out[rows_of(j * rows, rows), :] = value
         return carry
 
-    lax.fori_loop(0, each, member, 0, unroll=each <= 3)
+    lax.fori_loop(0, each, member, 0, unroll=min(each, 8))
 
 
 def unpack(ref, x, count, rows, width, dst, valid):
@@ -125,31 +126,36 @@
 
 
 def second_slabs(info, *refs, ny, nz, ov):
-    parts, (got_one, got_two, field, one, two) = refs[:-5], refs[-5:]
+    parts, (got_one, got_two, field, coef, one, two) = refs[:-6], refs[-6:]
     side, along = Side(info[1], ny), Side(info[2], nz)
     cx, cy, cz = parts[0].shape
     ey = cy + 2 * ov
-    count = len(parts) * cx
+    count = (len(parts) - 1) * cx
     for k, part in enumerate(parts):
-
-        def place(x, carry, k=k, part=part):
+        out, first = (coef, 0) if k == len(parts) - 1 else (field, k * cx)
+
+        def place(x, carry, k=k, part=part, out=out, first=first):
             a = got_one[k * cx + x]
             b = got_two[k * cx + x]
-            row = (k * cx + x) * ey
+            row = (first + x) * ey
             above = jnp.where(side.even, a, b)
             below = jnp.where(side.even, b, a)
-            field[rows_of(row, ov), :] = jnp.where(side.has_below, below, 0.0)
-            field[rows_of(row + ov, cy), :] = part[x]
-            field[rows_of(row + ov + cy, ov), :] = jnp.where(side.has_above, above, 0.0)
+            out[rows_of(row, ov), :] = jnp.where(side.has_below, below, 0.0)
+            out[rows_of(row + ov, cy), :] = part[x]
+            out[rows_of(row + ov + cy, ov), :] = jnp.where(side.has_above, above, 0.0)
             return carry
 
-        lax.fori_loop(0, cx, place, 0)
-
-    def load(x):
-        return field[rows_of(x * ey, ey), :]
-
-    pack(load, count, ey, ov, along.one(cz - ov, 0), one)
-    pack(load, count, ey, ov, along.two(cz - ov, 0), two)
+        lax.fori_loop(0, cx, place, 0, unroll=8)
+
+    edge = group_of(count, ov) * ey
+    for ref, planes, first in ((field, count, 0), (coef, cx, edge)):
+
+        def load(x, ref=ref):
+            return ref[rows_of(x * ey, ey), :]
+
+        last = first + group_of(planes, ov) * ey
+        pack(load, planes, ey, ov, along.one(cz - ov, 0), one.at[first:last])
+        pack(load, planes, ey, ov, along.two(cz - ov, 0), two.at[first:last])
 
 
 def extended(field, got_one, got_two, x, count, ey, ov, along):
@@ -200,7 +206,7 @@
             s1[rows_of(q * count + k * 8, 8), :] = turn(side[q * 8 : (q + 1) * 8])
         return carry
 
-    lax.fori_loop(0, count // 8, on, 0, unroll=2)
+    lax.fori_loop(0, count // 8, on, 0, unroll=3)
 
     def times_x(value, factor):
         value = dot(x_on[...], stack_rows(value))
@@ -218,7 +224,7 @@
     for q in range(octs):
         value = times_x(s1[q * count : (q + 1) * count, :], recip[ey + q])
         s1[q * count : q * count + back, :] = value
-    lax.fori_loop(0, ey // 2, middle, 0, unroll=4)
+    lax.fori_loop(0, ey // 2, middle, 0, unroll=10)
 
     def off(k, carry):
         side = jnp.concatenate([turn(s1[rows_of(q * count + k * 8, 8), :]) for q in range(octs)], axis=0)
@@ -230,7 +236,7 @@
             store(8 * k + j, value[j * ey : (j + 1) * ey])
         return carry
 
-    lax.fori_loop(0, back // 8, off, 0, unroll=2 if back % 16 == 0 else 1)
+    lax.fori_loop(0, back // 8, off, 0, unroll=2 if back % 16 == 0 else 3)
 
 
 def merged(core, halo, low):
@@ -238,10 +244,13 @@
     return jnp.where((lane < LANES // 2) == low, core, halo)
 
 
-def first_solve(info, field, got_one, got_two, zt, y_on, y_back, x_on, x_back, recip, u, block, one, two, s0, s1, *, nz, ov, ey, cz):
+def first_solve(info, field, got_one, got_two, zt, y_on, y_back, x_on, x_back, recip, u, block, rest, one, two, s0, s1, *, nz, ov, ey, cz):
     along = Side(info[2], nz)
     count = field.shape[0] // ey
     w = 2 * ov + 1
+    edge, half = group_of(count, ov) * ey, rest.shape[0] // 2
+    rest[:half] = got_one[edge:]
+    rest[half:] = got_two[edge:]
 
     def source(x):
         value = extended(field, got_one, got_two, x, count, ey, ov, along)
@@ -262,7 +271,7 @@
         pack(load, count, ey, w, jnp.where(low, LANES - ov, cz - ov - 1), out)
 
 
-def sum_z(info, u, got_one, got_two, v, one, two, *, ny, nz, ov, ey, cz):
+def sum_z(info, u, got_one, got_two, core_out, rest_out, one, two, *, ny, nz, ov, ey, cz):
     side, along = Side(info[1], ny), Side(info[2], nz)
     count = u.shape[0] // ey
     w = 2 * ov + 1
@@ -276,84 +285,89 @@
             part = unpack(got, x, count, ey, w, jnp.where(low, LANES - ov - 1, cz - ov), valid)
             mine = (lane < LANES // 2) == low
             core, rest = core + jnp.where(mine, part, 0.0), rest + jnp.where(mine, 0.0, part)
-        v[rows, :LANES] = core
-        v[rows, LANES:] = jnp.where(inside, rest, 0.0)
-        return carry
-
-    lax.fori_loop(0, count, add, 0, unroll=4)
+        core_out[rows, :] = core
+        rest_out[rows, :] = jnp.where(inside, rest, 0.0)
+        return carry
+
+    lax.fori_loop(0, count, add, 0, unroll=8)
     tall, halo = 2 * ov, 2 * (ov + 1)
     each = group_of(count, halo)
-    for out, start, odd in (
-        (one, side.one(ey - tall, 0), side.even),
-        (two, side.two(ey - tall, 0), ~side.even),
-    ):
+    for out, high in ((one, side.even), (two, ~side.even)):
+        start = jnp.where(high, ey - tall, 0)
+        odd = pl.ds(jnp.where(high, ey - tall - 1, tall), count, stride=ey)
 
         def main(x, carry, out=out, start=start):
-            out[rows_of(x * tall, tall), :] = v[rows_of(x * ey + start, tall), :LANES]
+            out[rows_of(x * tall, tall), :] = core_out[rows_of(x * ey + start, tall), :]
             return carry
 
-        lax.fori_loop(0, count, main, 0)
+        lax.fori_loop(0, count, main, 0, unroll=8)
         base = count * tall
 
         def load(x, start=start):
-            return v[rows_of(x * ey + start, tall), LANES:]
+            return rest_out[rows_of(x * ey + start, tall), :]
 
         pack(load, count, tall, halo, LANES - ov - 1, out.at[base : base + each * tall])
         base = base + each * tall
-        for x in range(count):
-            last, next_ = v[x * ey + ey - tall - 1 : x * ey + ey - tall, :], v[x * ey + tall : x * ey + tall + 1, :]
-            row = jnp.where(odd, last, next_)
-            out[base + x : base + x + 1, :] = row[:, :LANES]
-            out[base + count + x : base + count + x + 1, :] = row[:, LANES:]
-
-
-def second_solve(info, v, got_one, got_two, block, coef, c_one, c_two, zt, y_on, y_back, x_on, x_back, recip, u, first, one, two, s0, s1, side_part, resid, *, nx, ny, nz, ov, ey, cx, cz):
+        out[base : base + count, :] = core_out[odd, :]
+        out[base + count : base + 2 * count, :] = rest_out[odd, :]
+
+
+def coefficients(info, *refs, nz, ov, ey):
+    parts, out = refs[:-1], refs[-1]
+    along = Side(info[2], nz)
+    half = len(parts) // 2
+    cx = parts[0].shape[0] // ey
+    for k in range(half):
+        core, rest = parts[k], parts[half + k]
+        edge = rest.shape[0] // 2
+
+        def plane(x, carry, k=k, core=core, rest=rest, edge=edge):
+            value = extended(core, rest.at[:edge], rest.at[edge:], x, cx, ey, ov, along)
+            out[rows_of((k * cx + x) * ey, ey), :] = value + 5.0
+            return carry
+
+        lax.fori_loop(0, cx, plane, 0, unroll=4)
+
+
+def second_solve(info, core_in, rest_in, got_one, got_two, block, coef, zt, y_on, y_back, x_on, x_back, recip, u, first, one, two, s0, s1, core_v, rest_v, far, *, ny, nz, ov, ey, cx, cz):
     side, along = Side(info[1], ny), Side(info[2], nz)
     count = coef.shape[0] // ey
     tall, halo = 2 * ov, 2 * (ov + 1)
     each = group_of(count, halo)
+    room = ey + 2 * ov
     cy = ey - 2 * ov
     main_rows = count * tall
     odd_rows = main_rows + each * tall
 
-    def slab(ref, x, valid):
-        core = ref[rows_of(x * tall, tall), :]
-        extra = unpack(ref.at[main_rows:odd_rows], x, count, tall, halo, LANES - ov - 1, True)
-        return jnp.where(valid, jnp.concatenate([core, extra], axis=1), 0.0)
-
-    def odd(ref, x, valid):
-        row = jnp.concatenate([ref[pl.ds(odd_rows + x, 1), :], ref[pl.ds(odd_rows + count + x, 1), :]], axis=1)
-        return jnp.where(valid, row, 0.0)
+    def sides(a, b):
+        a, b = jnp.where(side.one_valid, a, 0.0), jnp.where(side.two_valid, b, 0.0)
+        return jnp.where(side.even, b, a), jnp.where(side.even, a, b)
 
     def gather(x, carry):
-        a, b = slab(got_one, x, side.one_valid), slab(got_two, x, side.two_valid)
-        above, below = jnp.where(side.even, a, b), jnp.where(side.even, b, a)
-        value = v[rows_of(x * ey, ey), :]
-        value = jnp.concatenate([value[:tall] + below, value[tall : ey - tall], value[ey - tall :] + above], axis=0)
-        y = lax.broadcasted_iota(jnp.int32, (ey, RING), 0)
-        value = jnp.where(((y >= ov) | side.has_below) & ((y < ey - ov) | side.has_above), value, 0.0)
-        a, b = odd(got_one, x, side.one_valid), odd(got_two, x, side.two_valid)
-        near = lax.broadcasted_iota(jnp.int32, (8, RING), 0)
-        under = jnp.where(near == 7, jnp.where(side.even, b, a), 0.0)
-        over = jnp.where(near == 0, jnp.where(side.even, a, b), 0.0)
-        center = value
-        full = jnp.concatenate([under, value, over], axis=0)
-        sum_y = full[7 : 7 + ey] + full[9 : 9 + ey]
-
-        @pl.when(x < cx)
-        def _():
-            first[rows_of(x * cy, cy), :] = center[ov : ov + cy, :LANES]
-
-        p = sum_y + pltpu.roll(center, 1, 1) + pltpu.roll(center, RING - 1, 1)
-        q = pltpu.roll(sum_y, 1, 1) + pltpu.roll(sum_y, RING - 1, 1)
-        f = block[rows_of(x * ey, ey), :]
-        c = extended(coef, c_one, c_two, x, count, ey, ov, along)
-        rows = rows_of(x * ey, ey)
-        side_part[rows, :] = 0.5 * center + 0.125 * p + 0.0625 * q
-        resid[rows, :] = f - (c + 5.0) * center + (0.5 * p + 0.125 * q)
-        return carry
-
-    lax.fori_loop(0, count, gather, 0, unroll=2)
+        rows, slab = rows_of(x * ey, ey), rows_of(x * tall, tall)
+        for source, out, (a, b) in (
+            (core_in, core_v, (got_one[slab, :], got_two[slab, :])),
+            (
+                rest_in,
+                rest_v,
+                [unpack(got.at[main_rows:odd_rows], x, count, tall, halo, LANES - ov - 1, True) for got in (got_one, got_two)],
+            ),
+        ):
+            below, above = sides(a, b)
+            value = source[rows, :]
+            low, high = value[:tall] + below, value[ey - tall :] + above
+            out[rows_of(x * room + ov, ov), :] = jnp.where(side.has_below, low[:ov], 0.0)
+            out[rows_of(x * room + tall, ov), :] = low[ov:]
+            out[rows_of(x * room + ov + tall, ey - 2 * tall), :] = value[tall : ey - tall]
+            out[rows_of(x * room + ov + ey - tall, ov), :] = high[:ov]
+            out[rows_of(x * room + ey, ov), :] = jnp.where(side.has_above, high[ov:], 0.0)
+        return carry
+
+    lax.fori_loop(0, count, gather, 0, unroll=4)
+    for out, start in ((core_v, odd_rows), (rest_v, odd_rows + count)):
+        below, above = sides(got_one[start : start + count, :], got_two[start : start + count, :])
+        out[pl.ds(ov - 1, count, stride=room), :] = below
+        out[pl.ds(ov + ey, count, stride=room), :] = above
 
     lane = lane_of((ey, RING))
     y = lax.broadcasted_iota(jnp.int32, (ey, RING), 0)
@@ -362,24 +376,38 @@
 
     def plane(x):
         at = (info[0] * cx + x) % count
-        value = resid[rows_of(x * ey, ey), :]
-        before = side_part[rows_of((x + count - 1) % count * ey, ey), :]
-        after = side_part[rows_of((x + 1) % count * ey, ey), :]
-        value = value + jnp.where(at > 0, before, 0.0) + jnp.where(at < count - 1, after, 0.0)
+        before, after = jnp.where(at > 0, 1.0, 0.0), jnp.where(at < count - 1, 1.0, 0.0)
+        spots = [(x + shift) % count * room + ov for shift in (0, count - 1, 1)]
+        halves = []
+        for ref in (core_v, rest_v):
+            mid, left, right = [ref[rows_of(spot, ey), :] for spot in spots]
+            mid_y, left_y, right_y = [ref[pl.ds(spot - 1, ey), :] + ref[pl.ds(spot + 1, ey), :] for spot in spots]
+            across, corner = before * left + after * right, before * left_y + after * right_y
+            faces = mid_y + across
+            halves.append((mid, 0.5 * faces + 0.125 * corner, 0.5 * mid + 0.125 * faces + 0.0625 * corner))
+        mid, flat, slope = [jnp.concatenate(pair, axis=1) for pair in zip(*halves)]
+        rows = rows_of(x * ey, ey)
+        value = block[rows, :] - coef[rows, :] * mid + flat + (pltpu.roll(slope, 1, 1) + pltpu.roll(slope, RING - 1, 1))
         return jnp.where(inside, value, 0.0)
 
     def store(x, value):
         rows = rows_of(x * ey, ey)
         u[rows, :] = value[:, :LANES]
-        resid[rows, :LANES] = value[:, LANES:]
+        far[rows, :] = value[:, LANES:]
 
     solve(plane, store, (zt, y_on, y_back, x_on, x_back, recip), (s0, s1), count, cx, ey)
 
     def load(x):
-        return resid[rows_of(x * ey, ey), :LANES]
+        return far[rows_of(x * ey, ey), :]
 
     pack(load, cx, ey, ov, along.one(0, LANES - ov), one)
     pack(load, cx, ey, ov, along.two(0, LANES - ov), two)
+
+    def keep(x, carry):
+        first[rows_of(x * cy, cy), :] = core_v[rows_of(x * room + 2 * ov, cy), :]
+        return carry
+
+    lax.fori_loop(0, cx, keep, 0, unroll=8)
 
 
 def last_sum_z(info, u, got_one, got_two, v, one, two, *, ny, nz, ov, ey, cx, cz):
@@ -395,7 +423,7 @@
         two[rows_of(x * ov, ov), :] = v[rows_of(x * ey + side.two(ey - ov, 0), ov), :]
         return carry
 
-    lax.fori_loop(0, cx, add, 0)
+    lax.fori_loop(0, cx, add, 0, unroll=8)
 
 
 def last_sum_y(info, v, got_one, got_two, first, out, *, ny, ov, ey, cx):
@@ -410,7 +438,7 @@
         out[x] = jnp.concatenate([value[:ov] + below, value[ov : cy - ov], value[cy - ov :] + above], axis=0)
         return carry
 
-    lax.fori_loop(0, cx, add, 0)
+    lax.fori_loop(0, cx, add, 0, unroll=8)
 
 
 def reciprocals(eigen_x, rest, out):
@@ -423,7 +451,10 @@
 
 def gather_x(block):
     count = lax.axis_size("gx")
-    return [block] + [lax.ppermute(block, "gx", [((i + shift) % count, i) for i in range(count)]) for shift in range(1, count)]
+    parts = [block]
+    for shift in range(1, count):
+        parts.append(lax.ppermute(block, "gx", [((i + shift) % count, i) for i in range(count)]))
+    return parts
 
 
 def columns(table):
@@ -443,7 +474,6 @@
     at = dict(ov=ov, ey=ey, cz=cz)
 
     f_parts = gather_x(right_side)
-    c_parts = gather_x(lax.optimization_barrier((reaction, f_parts[-1]))[0])
 
     blocks = [jnp.pad(basis_x.T, ((0, 0), (i * cx, (nx - 1 - i) * cx)))[:, ov : ov + count] for i in range(nx)]
     table = jnp.concatenate(blocks, axis=0)
@@ -457,31 +487,31 @@
     recip = call(reciprocals, [(rest.shape[0], ex, LANES)], jnp.broadcast_to(eigen_x[:, None], (ex, LANES)), rest, smem=0)[0]
     tables = (zt, columns(double.T), columns(double), columns(table), columns(table.T), recip)
 
-    def y_slabs(parts, after=()):
-        return call(functools.partial(first_slabs, ny=ny, ov=ov), [(count, ov, cz)] * 2, info, *parts, after=after)
-
-    def z_slabs(parts, got, after=()):
-        small = (group_of(count, ov) * ey, LANES)
-        return call(functools.partial(second_slabs, ny=ny, nz=nz, ov=ov), [(count * ey, cz), small, small], info, *parts, *got, after=after)
-
-    f, *slabs = z_slabs(f_parts, swap(*y_slabs(f_parts), "gy"))
-    c_slabs = y_slabs(c_parts, after=slabs[:1])
-    got, c_got = swap(*slabs, "gz"), swap(*c_slabs, "gy")
+    slabs = call(functools.partial(first_slabs, ny=ny, ov=ov), [(count + cx, ov, cz)] * 2, info, *f_parts, reaction)
+    got = swap(*slabs, "gy")
+    edge = group_of(cx, ov) * ey
+    small = (group_of(count, ov) * ey + edge, LANES)
+    f, c, *slabs = call(
+        functools.partial(second_slabs, ny=ny, nz=nz, ov=ov), [(count * ey, cz), (cx * ey, cz), small, small], info, *f_parts, reaction, *got
+    )
+    got = swap(*slabs, "gz")
+    c_parts = gather_x(c)
     state = [pltpu.VMEM((count * ey, LANES), F32), pltpu.VMEM((ey // 8 * count, LANES), F32)]
     small = (group_of(count, w) * ey, LANES)
-    u, block, *slabs = call(
-        functools.partial(first_solve, nz=nz, **at), [(count * ey, RING)] * 2 + [small, small], info, f, *got, *tables, scratch=state, after=c_slabs[:1]
+    u, block, rest, *slabs = call(
+        functools.partial(first_solve, nz=nz, **at), [(count * ey, RING)] * 2 + [(2 * edge, LANES), small, small], info, f, *got, *tables, scratch=state
     )
-    c, *c_slabs = z_slabs(c_parts, c_got, after=slabs[:1])
-    got, c_got = swap(*slabs, "gz"), swap(*c_slabs, "gz")
+    got = swap(*slabs, "gz")
+    c_parts += gather_x(rest)
     tall_rows = (count * tall + group_of(count, halo) * tall + 2 * count, LANES)
-    v, *slabs = call(functools.partial(sum_z, ny=ny, nz=nz, **at), [(count * ey, RING), tall_rows, tall_rows], info, u, *got, after=c_slabs[:1])
+    core, rest, *slabs = call(functools.partial(sum_z, ny=ny, nz=nz, **at), [(count * ey, LANES)] * 2 + [tall_rows, tall_rows], info, u, *got)
     got = swap(*slabs, "gy")
+    c = call(functools.partial(coefficients, nz=nz, ov=ov, ey=ey), [(count * ey, RING)], info, *c_parts, after=slabs[:1])[0]
     small = (group_of(cx, ov) * ey, LANES)
-    state = state + [pltpu.VMEM((count * ey, RING), F32)] * 2
+    state += [pltpu.VMEM((count * (ey + 2 * ov), LANES), F32)] * 2 + [pltpu.VMEM((cx * ey, LANES), F32)]
     u, first, *slabs = call(
-        functools.partial(second_solve, nx=nx, ny=ny, nz=nz, cx=cx, **at),
-        [(cx * ey, LANES), (cx * cy, LANES), small, small], info, v, *got, block, c, *c_got, *tables, scratch=state,
+        functools.partial(second_solve, ny=ny, nz=nz, cx=cx, **at),
+        [(cx * ey, LANES), (cx * cy, LANES), small, small], info, core, rest, *got, block, c, *tables, scratch=state,
     )
     got = swap(*slabs, "gz")
     v, *slabs = call(functools.partial(last_sum_z, ny=ny, nz=nz, cx=cx, **at), [(cx * ey, LANES)] + [(cx * ov, LANES)] * 2, info, u, *got)

time: 100 us -> 87.8 us (0.88)
  Pallas kernels: 43.8 us -> 29.4 us
  waiting for transfers between devices: 14.5 us -> 26.4 us
  starting transfers between devices: 32.9 us -> 24.9 us
    pallas_call x10 -> x9, Pallas kernels: 43.8 us -> 29.4 us  [call(): pl.pallas_call(body, out_shape=[jax.ShapeDtypeStruct(s, F32) for s in out...]
    ppermute x2 -> x3, waiting for transfers between devices: 1.51 us -> 10.8 us  [gather_x(): lax.ppermute(block, 'gx', [((i + shift) % count, i) for i in range(count)])]
    ppermute x8 -> x6, starting transfers between devices: 15.4 us -> 10.7 us  [swap(): lax.ppermute(one, axis, pairs(count, 0))]
    ppermute x8 -> x6, starting transfers between devices: 14.3 us -> 10.6 us  [swap(): lax.ppermute(two, axis, pairs(count, 1))]
    ppermute x8 -> x6, waiting for transfers between devices: 7.07 us -> 9.01 us  [swap(): lax.ppermute(two, axis, pairs(count, 1))]
    ppermute x8 -> x6, waiting for transfers between devices: 5.94 us -> 6.62 us  [swap(): lax.ppermute(one, axis, pairs(count, 0))]
    ppermute x2 -> x3, starting transfers between devices: 3.14 us -> 3.63 us  [gather_x(): lax.ppermute(block, 'gx', [((i + shift) % count, i) for i in range(count)])]
  transfers between devices with their start and end apart: 18 -> 15, of which waited for: 7 -> 7; matrix products, arithmetic and copies ran while one was open for 6% -> 6% of each run, Pallas kernels for 17% -> 3%
where the time goes in v1:
time: 87.8 us; the launch traced here: 86.1 us
  Pallas kernels  29.4 us (33%)
  waiting for transfers between devices  26.4 us (30%)
  starting transfers between devices  24.9 us (28%)
  local copies, waits for them, and re-layouts  2.87 us (3%)
  other arithmetic  2.21 us (3%)
    pallas_call x9, Pallas kernels, call(): pl.pallas_call(body, out_shape=[jax.ShapeDtypeStruct(s, F32) for s in out...  29.4 us
    ppermute x3, waiting for transfers between devices, gather_x(): lax.ppermute(block, 'gx', [((i + shift) % count, i) for i in range(count)])  10.8 us
    ppermute x6, starting transfers between devices, swap(): lax.ppermute(one, axis, pairs(count, 0))  10.7 us
    ppermute x6, starting transfers between devices, swap(): lax.ppermute(two, axis, pairs(count, 1))  10.6 us
    ppermute x6, waiting for transfers between devices, swap(): lax.ppermute(two, axis, pairs(count, 1))  9.01 us
    ppermute x6, waiting for transfers between devices, swap(): lax.ppermute(one, axis, pairs(count, 0))  6.62 us
    ppermute x3, starting transfers between devices, gather_x(): lax.ppermute(block, 'gx', [((i + shift) % count, i) for i in range(count)])  3.63 us
  transfers between devices with their start and end apart: 15, of which 7 were waited for; matrix products, arithmetic and copies ran while one was open for 6% of the time, Pallas kernels for 3%

profile of v1, /device:TPU:1, one launch (start us, length us, event | category | flops | bytes accessed | tf_op | source)
XLA Modules:
  0.0 86.1 jit_solution(1215108606858185381)
XLA Ops:
  0.0 0.0 copy-start
  0.0 0.0 copy-start.2
  0.0 0.0 copy-start.3
  0.0 0.0 copy-start.1
  0.0 2.1 %collective-permute-start = (f32[24,24,128]{2,1,0:T(8,128)}, f32[24,24,128]{2,1,0:T(8,128)S(1)}, u32[]{:S(2)}, u32[]{:S(2)}) collective-permute-start(f32[24,24,128]{2,1,0:T(8,128)} %refs_1_.3), channel_id=1, source_target_pairs={{16,0},{0,16},{17,1},{1,17},{18,2},{2,18},{19,3},{3,19},{20,4},{4,... | collective-permute-start | bytes 884744 | tf_op jit(solution)/shard_map/ppermute | solution.py:456
  2.1 0.8 broadcast_add_fusion
  2.9 0.9 %slice.18 = f32[136,144]{1,0:T(8,128)S(1)} slice(f32[144,144]{1,0:T(8,128)} %param.12), slice={[8:144], [0:144]} | slice | bytes 156672 | tf_op jit(solution)/shard_map/slice | solution.py:483
  3.8 0.7 slice.19
  4.5 0.8 pad_slice_fusion.1
  5.3 0.1 fusion.3
  5.4 0.1 copy.14.refs_7_.refs_10_
  5.5 0.1 reshape.6
  5.6 0.9 %fusion = (bf16[80,80]{0,1:T(8,128)(2,1)S(1)}, bf16[80,80]{0,1:T(8,128)(2,1)S(1)}) fusion(f32[40,40]{1,0:T(8,128)} %param.11), kind=kLoop, calls=%fused_computation.10 | loop fusion | flops 57600 | bytes 32000 | tf_op jit(solution)/shard_map/convert.10
  6.5 0.1 copy.13.refs_5_.refs_8_
  6.6 0.1 pad.38.clone
  6.7 0.1 pad_maximum_fusion
  6.8 0.0 copy-done.3
  6.9 0.1 broadcast_in_dim.5.refs_0_
  6.9 0.2 shard_map.84.refs_9_.refs_12_
  7.1 0.1 pad_add_fusion.refs_0_
  7.2 0.0 copy-done.2
  7.2 0.1 fusion.1
  7.3 1.7 %collective-permute-done.refs_2_ = f32[24,24,128]{2,1,0:T(8,128)S(1)} collective-permute-done((f32[24,24,128]{2,1,0:T(8,128)}, f32[24,24,128]{2,1,0:T(8,128)S(1)}, u32[]{:S(2)}, u32[]{:S(2)}) %collective-permute-start) | collective-permute-done | bytes 294944 | tf_op jit(solution)/shard_map/ppermute | solution.py:456
  9.0 0.0 copy-done
  9.0 0.0 copy-done.1
  9.0 0.6 shard_map.82
  9.6 1.3 %collective-permute-start.1 = (f32[72,8,128]{2,1,0:T(8,128)S(1)}, f32[72,8,128]{2,1,0:T(8,128)S(1)}, u32[]{:S(2)}, u32[]{:S(2)}) collective-permute-start(f32[72,8,128]{2,1,0:T(8,128)S(1)} %get-tuple-element.27), channel_id=1, source_target_pairs={{0,4},{4,0},{8,12},{12,8},{1,5},{5,1},{9,13},{13,9},{2,6},{6,2},{1... | collective-permute-start | bytes 884744 | tf_op jit(solution)/shard_map/ppermute | solution.py:27
  11.0 0.7 collective-permute-start.2
  11.6 0.1 pad_maximum_fusion.2.refs_6_.refs_9_
  11.8 5.3 %collective-permute-done.1.refs_4_ = f32[72,8,128]{2,1,0:T(8,128)S(1)} collective-permute-done((f32[72,8,128]{2,1,0:T(8,128)S(1)}, f32[72,8,128]{2,1,0:T(8,128)S(1)}, u32[]{:S(2)}, u32[]{:S(2)}) %collective-permute-start.1) | collective-permute-done | bytes 294944 | tf_op jit(solution)/shard_map/ppermute | solution.py:27
  17.0 0.0 collective-permute-done.2.refs_5_
  17.0 1.5 %shard_map.83 = (f32[1920,128]{1,0:T(8,128)S(1)}, f32[960,128]{1,0:T(8,128)S(1)}, f32[200,128]{1,0:T(8,128)S(1)}, f32[200,128]{1,0:T(8,128)S(1)}) custom-call(s32[3]{0:T(128)S(1)} %pad_add_fusion.refs_0_, f32[24,24,128]{2,1,0:T(8,128)S(1)} %copy-done, f32[24,24,128]{2,1,0:T(8,128)S(1)} %collective-permute-done.refs_2_, f32[24,24,128]{2,1,0:T(8,128)S(1)} %copy-done.1, ...), custom_call_target="tpu_custom_call" | custom-call | tf_op jit(solution)/shard_map/pallas_call | solution.py:40
  18.6 2.2 %collective-permute-start.3 = (f32[200,128]{1,0:T(8,128)S(1)}, f32[200,128]{1,0:T(8,128)S(1)}, u32[]{:S(2)}, u32[]{:S(2)}) collective-permute-start(f32[200,128]{1,0:T(8,128)S(1)} %get-tuple-element.30), channel_id=1, source_target_pairs={{0,1},{1,0},{2,3},{3,2},{4,5},{5,4},{6,7},{7,6},{8,9},{9,8},{10,11... | collective-permute-start | bytes 307208 | tf_op jit(solution)/shard_map/ppermute | solution.py:27
  20.7 3.0 %collective-permute-start.4 = (f32[200,128]{1,0:T(8,128)S(1)}, f32[200,128]{1,0:T(8,128)S(1)}, u32[]{:S(2)}, u32[]{:S(2)}) collective-permute-start(f32[200,128]{1,0:T(8,128)S(1)} %get-tuple-element.31), channel_id=1, source_target_pairs={{0,0},{1,2},{2,1},{3,3},{4,4},{5,6},{6,5},{7,7},{8,8},{9,10},{10,9... | collective-permute-start | bytes 307208 | tf_op jit(solution)/shard_map/ppermute | solution.py:27
  23.8 0.1 pad_maximum_fusion.4.refs_8_.refs_11_
  23.8 0.0 collective-permute-done.3.refs_2_
  23.9 2.8 %collective-permute-done.4.refs_3_ = f32[200,128]{1,0:T(8,128)S(1)} collective-permute-done((f32[200,128]{1,0:T(8,128)S(1)}, f32[200,128]{1,0:T(8,128)S(1)}, u32[]{:S(2)}, u32[]{:S(2)}) %collective-permute-start.4) | collective-permute-done | bytes 102432 | tf_op jit(solution)/shard_map/ppermute | solution.py:27
  26.7 9.8 %shard_map.85 = (f32[1920,256]{1,0:T(8,128)S(1)}, f32[1920,256]{1,0:T(8,128)S(1)}, f32[160,128]{1,0:T(8,128)S(1)}, f32[280,128]{1,0:T(8,128)S(1)}, f32[280,128]{1,0:T(8,128)S(1)}) custom-call(s32[3]{0:T(128)S(1)} %pad_add_fusion.refs_0_, f32[1920,128]{1,0:T(8,128)S(1)} %get-tuple-element.29.refs_1_, f32[200,128]{1,0:T(8,128)S(1)} %collective-permute-done.3.refs_2_, ...), custom_call_target="tpu_custom_call" | custom-call | tf_op jit(solution)/shard_map/pallas_call | solution.py:40
  36.5 0.1 collective-permute-start.5
  36.5 3.0 %collective-permute-start.6 = (f32[280,128]{1,0:T(8,128)S(1)}, f32[280,128]{1,0:T(8,128)S(1)}, u32[]{:S(2)}, u32[]{:S(2)}) collective-permute-start(f32[280,128]{1,0:T(8,128)S(1)} %get-tuple-element.34), channel_id=1, source_target_pairs={{0,0},{1,2},{2,1},{3,3},{4,4},{5,6},{6,5},{7,7},{8,8},{9,10},{10,9... | collective-permute-start | bytes 430088 | tf_op jit(solution)/shard_map/ppermute | solution.py:27
  39.6 0.0 collective-permute-done.5.refs_2_
  39.6 3.4 %collective-permute-done.6.refs_3_ = f32[280,128]{1,0:T(8,128)S(1)} collective-permute-done((f32[280,128]{1,0:T(8,128)S(1)}, f32[280,128]{1,0:T(8,128)S(1)}, u32[]{:S(2)}, u32[]{:S(2)}) %collective-permute-start.6) | collective-permute-done | bytes 143392 | tf_op jit(solution)/shard_map/ppermute | solution.py:27
  43.0 2.1 %shard_map.86 = (f32[1920,128]{1,0:T(8,128)S(1)}, f32[1920,128]{1,0:T(8,128)S(1)}, f32[976,128]{1,0:T(8,128)S(1)}, f32[976,128]{1,0:T(8,128)S(1)}) custom-call(s32[3]{0:T(128)S(1)} %pad_add_fusion.refs_0_, f32[1920,256]{1,0:T(8,128)S(1)} %get-tuple-element.32.refs_1_, f32[280,128]{1,0:T(8,128)S(1)} %collective-permute-done.5.refs_2_, ...), custom_call_target="tpu_custom_call" | custom-call | tf_op jit(solution)/shard_map/pallas_call | solution.py:40
  45.1 4.3 %collective-permute-start.7 = (f32[976,128]{1,0:T(8,128)S(1)}, f32[976,128]{1,0:T(8,128)S(1)}, u32[]{:S(2)}, u32[]{:S(2)}) collective-permute-start(f32[976,128]{1,0:T(8,128)S(1)} %get-tuple-element.37.refs_5_), channel_id=1, source_target_pairs={{0,4},{4,0},{8,12},{12,8},{1,5},{5,1},{9,13},{13,9},{2,6},{6,2},{1... | collective-permute-start | bytes 1499144 | tf_op jit(solution)/shard_map/ppermute | solution.py:27
  49.4 0.7 collective-permute-start.8
  50.1 1.3 %collective-permute-start.9 = (f32[960,128]{1,0:T(8,128)S(1)}, f32[960,128]{1,0:T(8,128)S(1)}, u32[]{:S(2)}, u32[]{:S(2)}) collective-permute-start(f32[960,128]{1,0:T(8,128)S(1)} %get-tuple-element.40.refs_1_), channel_id=1, source_target_pairs={{16,0},{0,16},{17,1},{1,17},{18,2},{2,18},{19,3},{3,19},{20,4},{4,... | collective-permute-start | bytes 1474568 | tf_op jit(solution)/shard_map/ppermute | solution.py:456
  51.4 0.3 collective-permute-start.10
  51.7 9.1 %collective-permute-done.10.refs_4_ = f32[160,128]{1,0:T(8,128)S(1)} collective-permute-done((f32[160,128]{1,0:T(8,128)S(1)}, f32[160,128]{1,0:T(8,128)S(1)}, u32[]{:S(2)}, u32[]{:S(2)}) %collective-permute-start.10) | collective-permute-done | bytes 81952 | tf_op jit(solution)/shard_map/ppermute | solution.py:456
  60.7 0.0 collective-permute-done.9.refs_2_
  60.7 2.0 %shard_map.87.refs_6_ = f32[1920,256]{1,0:T(8,128)S(1)} custom-call(s32[3]{0:T(128)S(1)} %pad_add_fusion.refs_0_, f32[960,128]{1,0:T(8,128)S(1)} %get-tuple-element.40.refs_1_, f32[960,128]{1,0:T(8,128)S(1)} %collective-permute-done.9.refs_2_, f32[160,128]{1,0:T(8,128)S(1)} %get-tuple-element.41.refs_3_, f32[160,128]{1,0:T(8,128)S(1)} %collective-permute-done.10.refs_4_, ...), custom_call_target="tpu_custom_call" | custom-call | tf_op jit(solution)/shard_map/pallas_call | solution.py:40
  62.8 0.0 collective-permute-done.7.refs_3_
  62.8 0.0 collective-permute-done.8.refs_4_
  62.8 10.7 %shard_map.88 = (f32[960,128]{1,0:T(8,128)S(1)}, f32[576,128]{1,0:T(8,128)S(1)}, f32[80,128]{1,0:T(8,128)S(1)}, f32[80,128]{1,0:T(8,128)S(1)}) custom-call(s32[3]{0:T(128)S(1)} %pad_add_fusion.refs_0_, f32[1920,128]{1,0:T(8,128)S(1)} %get-tuple-element.35.refs_1_, f32[1920,128]{1,0:T(8,128)S(1)} %get-tuple-element.36.refs_2_, ...), custom_call_target="tpu_custom_call" | custom-call | tf_op jit(solution)/shard_map/pallas_call | solution.py:40
  73.5 0.1 collective-permute-start.11
  73.6 2.5 %collective-permute-start.12 = (f32[80,128]{1,0:T(8,128)S(1)}, f32[80,128]{1,0:T(8,128)S(1)}, u32[]{:S(2)}, u32[]{:S(2)}) collective-permute-start(f32[80,128]{1,0:T(8,128)S(1)} %get-tuple-element.44), channel_id=1, source_target_pairs={{0,0},{1,2},{2,1},{3,3},{4,4},{5,6},{6,5},{7,7},{8,8},{9,10},{10,9... | collective-permute-start | bytes 122888 | tf_op jit(solution)/shard_map/ppermute | solution.py:27
  76.1 0.0 collective-permute-done.11.refs_2_
  76.1 2.8 %collective-permute-done.12.refs_3_ = f32[80,128]{1,0:T(8,128)S(1)} collective-permute-done((f32[80,128]{1,0:T(8,128)S(1)}, f32[80,128]{1,0:T(8,128)S(1)}, u32[]{:S(2)}, u32[]{:S(2)}) %collective-permute-start.12) | collective-permute-done | bytes 40992 | tf_op jit(solution)/shard_map/ppermute | solution.py:27
  78.9 1.1 %shard_map.89 = (f32[960,128]{1,0:T(8,128)S(1)}, f32[192,128]{1,0:T(8,128)S(1)}, f32[192,128]{1,0:T(8,128)S(1)}) custom-call(s32[3]{0:T(128)S(1)} %pad_add_fusion.refs_0_, f32[960,128]{1,0:T(8,128)S(1)} %get-tuple-element.42.refs_1_, f32[80,128]{1,0:T(8,128)S(1)} %collective-permute-done.11.refs_2_, f32[80,128]{1,0:T(8,128)S(1)} %collective-permute-done.12.refs_3_), custom_call_target="tpu_custom_call" | custom-call | tf_op jit(solution)/shard_map/pallas_call | solution.py:40
  80.0 2.7 %collective-permute-start.13 = (f32[192,128]{1,0:T(8,128)S(1)}, f32[192,128]{1,0:T(8,128)S(1)}, u32[]{:S(2)}, u32[]{:S(2)}) collective-permute-start(f32[192,128]{1,0:T(8,128)S(1)} %get-tuple-element.46), channel_id=1, source_target_pairs={{0,4},{4,0},{8,12},{12,8},{1,5},{5,1},{9,13},{13,9},{2,6},{6,2},{1... | collective-permute-start | bytes 294920 | tf_op jit(solution)/shard_map/ppermute | solution.py:27
  82.8 0.7 collective-permute-start.14
  83.4 1.3 %collective-permute-done.13.refs_2_ = f32[192,128]{1,0:T(8,128)S(1)} collective-permute-done((f32[192,128]{1,0:T(8,128)S(1)}, f32[192,128]{1,0:T(8,128)S(1)}, u32[]{:S(2)}, u32[]{:S(2)}) %collective-permute-start.13) | collective-permute-done | bytes 98336 | tf_op jit(solution)/shard_map/ppermute | solution.py:27
  84.8 0.0 collective-permute-done.14.refs_3_
  84.8 1.3 %shard_map.90 = f32[24,24,128]{2,1,0:T(8,128)} custom-call(s32[3]{0:T(128)S(1)} %pad_add_fusion.refs_0_, f32[960,128]{1,0:T(8,128)S(1)} %get-tuple-element.45.refs_1_, f32[192,128]{1,0:T(8,128)S(1)} %collective-permute-done.13.refs_2_, f32[192,128]{1,0:T(8,128)S(1)} %collective-permute-done.14.refs_3_, f32[576,128]{1,0:T(8,128)S(1)} %get-tuple-element.48.refs_4_), custom_call_target="tpu_custom_call" | custom-call | tf_op jit(solution)/shard_map/pallas_call | solution.py:40
  (9 shorter events, 0.1 us)
Async XLA Ops:
  0.0 9.0 %copy-start = (f32[24,24,128]{2,1,0:T(8,128)S(1)}, f32[24,24,128]{2,1,0:T(8,128)}, u32[]{:S(2)}) copy-start(f32[24,24,128]{2,1,0:T(8,128)} %refs_1_.3) | copy-start | bytes 884740
  0.0 7.2 %copy-start.2 = (f32[40,40]{1,0:T(8,128)S(1)}, f32[40,40]{1,0:T(8,128)}, u32[]{:S(2)}) copy-start(f32[40,40]{1,0:T(8,128)} %param.11) | copy-start | bytes 19204
  0.0 6.8 %copy-start.3 = (f32[40]{0:T(128)S(1)}, f32[40]{0:T(128)}, u32[]{:S(2)}) copy-start(f32[40]{0:T(128)} %param.13) | copy-start | bytes 484
  0.0 9.0 %copy-start.1 = (f32[24,24,128]{2,1,0:T(8,128)S(1)}, f32[24,24,128]{2,1,0:T(8,128)}, u32[]{:S(2)}) copy-start(f32[24,24,128]{2,1,0:T(8,128)} %refs_3_.3) | copy-start | bytes 884740
  0.0 9.0 %collective-permute-start = (f32[24,24,128]{2,1,0:T(8,128)}, f32[24,24,128]{2,1,0:T(8,128)S(1)}, u32[]{:S(2)}, u32[]{:S(2)}) collective-permute-start(f32[24,24,128]{2,1,0:T(8,128)} %refs_1_.3), channel_id=1, source_target_pairs={{16,0},{0,16},{17,1},{1,17},{18,2},{2,18},{19,3},{3,19},{20,4},{4,... | collective-permute-start | bytes 884744 | tf_op jit(solution)/shard_map/ppermute | solution.py:456
  9.6 7.4 %collective-permute-start.1 = (f32[72,8,128]{2,1,0:T(8,128)S(1)}, f32[72,8,128]{2,1,0:T(8,128)S(1)}, u32[]{:S(2)}, u32[]{:S(2)}) collective-permute-start(f32[72,8,128]{2,1,0:T(8,128)S(1)} %get-tuple-element.27), channel_id=1, source_target_pairs={{0,4},{4,0},{8,12},{12,8},{1,5},{5,1},{9,13},{13,9},{2,6},{6,2},{1... | collective-permute-start | bytes 884744 | tf_op jit(solution)/shard_map/ppermute | solution.py:27
  11.0 6.1 %collective-permute-start.2 = (f32[72,8,128]{2,1,0:T(8,128)S(1)}, f32[72,8,128]{2,1,0:T(8,128)S(1)}, u32[]{:S(2)}, u32[]{:S(2)}) collective-permute-start(f32[72,8,128]{2,1,0:T(8,128)S(1)} %get-tuple-element.28), channel_id=1, source_target_pairs={{0,0},{4,8},{8,4},{12,12},{1,1},{5,9},{9,5},{13,13},{2,2},{6,10},{... | collective-permute-start | bytes 884744 | tf_op jit(solution)/shard_map/ppermute | solution.py:27
  18.6 5.3 %collective-permute-start.3 = (f32[200,128]{1,0:T(8,128)S(1)}, f32[200,128]{1,0:T(8,128)S(1)}, u32[]{:S(2)}, u32[]{:S(2)}) collective-permute-start(f32[200,128]{1,0:T(8,128)S(1)} %get-tuple-element.30), channel_id=1, source_target_pairs={{0,1},{1,0},{2,3},{3,2},{4,5},{5,4},{6,7},{7,6},{8,9},{9,8},{10,11... | collective-permute-start | bytes 307208 | tf_op jit(solution)/shard_map/ppermute | solution.py:27
  20.7 6.0 %collective-permute-start.4 = (f32[200,128]{1,0:T(8,128)S(1)}, f32[200,128]{1,0:T(8,128)S(1)}, u32[]{:S(2)}, u32[]{:S(2)}) collective-permute-start(f32[200,128]{1,0:T(8,128)S(1)} %get-tuple-element.31), channel_id=1, source_target_pairs={{0,0},{1,2},{2,1},{3,3},{4,4},{5,6},{6,5},{7,7},{8,8},{9,10},{10,9... | collective-permute-start | bytes 307208 | tf_op jit(solution)/shard_map/ppermute | solution.py:27
  36.5 3.1 %collective-permute-start.5 = (f32[280,128]{1,0:T(8,128)S(1)}, f32[280,128]{1,0:T(8,128)S(1)}, u32[]{:S(2)}, u32[]{:S(2)}) collective-permute-start(f32[280,128]{1,0:T(8,128)S(1)} %get-tuple-element.33), channel_id=1, source_target_pairs={{0,1},{1,0},{2,3},{3,2},{4,5},{5,4},{6,7},{7,6},{8,9},{9,8},{10,11... | collective-permute-start | bytes 430088 | tf_op jit(solution)/shard_map/ppermute | solution.py:27
  36.5 6.4 %collective-permute-start.6 = (f32[280,128]{1,0:T(8,128)S(1)}, f32[280,128]{1,0:T(8,128)S(1)}, u32[]{:S(2)}, u32[]{:S(2)}) collective-permute-start(f32[280,128]{1,0:T(8,128)S(1)} %get-tuple-element.34), channel_id=1, source_target_pairs={{0,0},{1,2},{2,1},{3,3},{4,4},{5,6},{6,5},{7,7},{8,8},{9,10},{10,9... | collective-permute-start | bytes 430088 | tf_op jit(solution)/shard_map/ppermute | solution.py:27
  45.1 17.7 %collective-permute-start.7 = (f32[976,128]{1,0:T(8,128)S(1)}, f32[976,128]{1,0:T(8,128)S(1)}, u32[]{:S(2)}, u32[]{:S(2)}) collective-permute-start(f32[976,128]{1,0:T(8,128)S(1)} %get-tuple-element.37.refs_5_), channel_id=1, source_target_pairs={{0,4},{4,0},{8,12},{12,8},{1,5},{5,1},{9,13},{13,9},{2,6},{6,2},{1... | collective-permute-start | bytes 1499144 | tf_op jit(solution)/shard_map/ppermute | solution.py:27
  49.4 13.3 %collective-permute-start.8 = (f32[976,128]{1,0:T(8,128)S(1)}, f32[976,128]{1,0:T(8,128)S(1)}, u32[]{:S(2)}, u32[]{:S(2)}) collective-permute-start(f32[976,128]{1,0:T(8,128)S(1)} %get-tuple-element.38), channel_id=1, source_target_pairs={{0,0},{4,8},{8,4},{12,12},{1,1},{5,9},{9,5},{13,13},{2,2},{6,10},{... | collective-permute-start | bytes 1499144 | tf_op jit(solution)/shard_map/ppermute | solution.py:27
  50.1 10.6 %collective-permute-start.9 = (f32[960,128]{1,0:T(8,128)S(1)}, f32[960,128]{1,0:T(8,128)S(1)}, u32[]{:S(2)}, u32[]{:S(2)}) collective-permute-start(f32[960,128]{1,0:T(8,128)S(1)} %get-tuple-element.40.refs_1_), channel_id=1, source_target_pairs={{16,0},{0,16},{17,1},{1,17},{18,2},{2,18},{19,3},{3,19},{20,4},{4,... | collective-permute-start | bytes 1474568 | tf_op jit(solution)/shard_map/ppermute | solution.py:456
  51.4 9.3 %collective-permute-start.10 = (f32[160,128]{1,0:T(8,128)S(1)}, f32[160,128]{1,0:T(8,128)S(1)}, u32[]{:S(2)}, u32[]{:S(2)}) collective-permute-start(f32[160,128]{1,0:T(8,128)S(1)} %get-tuple-element.41.refs_3_), channel_id=1, source_target_pairs={{16,0},{0,16},{17,1},{1,17},{18,2},{2,18},{19,3},{3,19},{20,4},{4,... | collective-permute-start | bytes 245768 | tf_op jit(solution)/shard_map/ppermute | solution.py:456
  73.5 2.6 %collective-permute-start.11 = (f32[80,128]{1,0:T(8,128)S(1)}, f32[80,128]{1,0:T(8,128)S(1)}, u32[]{:S(2)}, u32[]{:S(2)}) collective-permute-start(f32[80,128]{1,0:T(8,128)S(1)} %get-tuple-element.43), channel_id=1, source_target_pairs={{0,1},{1,0},{2,3},{3,2},{4,5},{5,4},{6,7},{7,6},{8,9},{9,8},{10,11... | collective-permute-start | bytes 122888 | tf_op jit(solution)/shard_map/ppermute | solution.py:27
  73.6 5.3 %collective-permute-start.12 = (f32[80,128]{1,0:T(8,128)S(1)}, f32[80,128]{1,0:T(8,128)S(1)}, u32[]{:S(2)}, u32[]{:S(2)}) collective-permute-start(f32[80,128]{1,0:T(8,128)S(1)} %get-tuple-element.44), channel_id=1, source_target_pairs={{0,0},{1,2},{2,1},{3,3},{4,4},{5,6},{6,5},{7,7},{8,8},{9,10},{10,9... | collective-permute-start | bytes 122888 | tf_op jit(solution)/shard_map/ppermute | solution.py:27
  80.0 4.8 %collective-permute-start.13 = (f32[192,128]{1,0:T(8,128)S(1)}, f32[192,128]{1,0:T(8,128)S(1)}, u32[]{:S(2)}, u32[]{:S(2)}) collective-permute-start(f32[192,128]{1,0:T(8,128)S(1)} %get-tuple-element.46), channel_id=1, source_target_pairs={{0,4},{4,0},{8,12},{12,8},{1,5},{5,1},{9,13},{13,9},{2,6},{6,2},{1... | collective-permute-start | bytes 294920 | tf_op jit(solution)/shard_map/ppermute | solution.py:27
  82.8 2.0 %collective-permute-start.14 = (f32[192,128]{1,0:T(8,128)S(1)}, f32[192,128]{1,0:T(8,128)S(1)}, u32[]{:S(2)}, u32[]{:S(2)}) collective-permute-start(f32[192,128]{1,0:T(8,128)S(1)} %get-tuple-element.47), channel_id=1, source_target_pairs={{0,0},{4,8},{8,4},{12,12},{1,1},{5,9},{9,5},{13,13},{2,2},{6,10},{... | collective-permute-start | bytes 294920 | tf_op jit(solution)/shard_map/ppermute | solution.py:27

commit v2 on v1

--- a/solution.py
+++ b/solution.py
@@ -39,7 +39,7 @@
 
     return pl.pallas_call(
         body,
-        out_shape=[jax.ShapeDtypeStruct(s, F32) for s in outs],
+        out_shape=[jax.ShapeDtypeStruct(s[:2], BF16) if BF16 in s else jax.ShapeDtypeStruct(s, F32) for s in outs],
         in_specs=specs,
         out_specs=[vmem] * len(outs),
         scratch_shapes=list(scratch),
@@ -110,10 +110,6 @@
 
 def dot(a, b):
     return jnp.dot(a, b, preferred_element_type=F32)
-
-
-def dot_nt(a, b):
-    return lax.dot_general(a, b, (((1,), (1,)), ((), ())), preferred_element_type=F32)
 
 
 def first_slabs(info, *refs, ny, ov):
@@ -176,37 +172,50 @@
     return value
 
 
-def solve(source, store, tables, state, count, back, ey):
-    zt, y_on, y_back, x_on, x_back, recip = tables
+def solve(source, store, tables, state, count, back, ey, cx):
+    z_on, z_back, y_on, y_back, x_on, x_back, recip = tables
     s0, s1 = state
-    z_high, z_low = split(zt[...])
     modes = recip.shape[1]
     group = LANES // 8
     lane = lane_of((ey, LANES))
     octs = ey // 8
     nothing = jnp.zeros((ey, LANES), F32)
 
-    def times_y(table, core, side):
-        two = 2 * ey
-        first = dot(table[...], stack_rows(jnp.concatenate([core[:two], core[two : 2 * two]], axis=1)))
-        second = dot(table[...], stack_rows(jnp.concatenate([core[2 * two : 3 * two], core[3 * two :]], axis=1)))
-        third = dot(table[...], stack_rows(jnp.concatenate([side, nothing], axis=0)))
-        return jnp.concatenate([first[:, :LANES], first[:, LANES:], second[:, :LANES], second[:, LANES:]], axis=0), third[:ey]
-
-    def on(k, carry):
-        high, low = split(jnp.concatenate([source(8 * k + j) for j in range(8)], axis=0))
-        value = dot(high, z_high) + (dot(high, z_low) + dot(low, z_high))
-        side = nothing
-        for j in range(8):
-            turned = pltpu.roll(value[j * ey : (j + 1) * ey, LANES:], j * group, 1)
-            side = jnp.where(lane // group == j, turned, side)
-        core, side = times_y(y_on, value[:, :LANES], side)
-        s0[rows_of(k * 8 * ey, 8 * ey), :] = core
-        for q in range(octs):
-            s1[rows_of(q * count + k * 8, 8), :] = turn(side[q * 8 : (q + 1) * 8])
-        return carry
-
-    lax.fori_loop(0, count // 8, on, 0, unroll=3)
+    def times_y(table, core, sides):
+        planes = [core[j * ey : (j + 1) * ey] for j in range(cx)] + sides
+        planes += [nothing] * (-len(planes) % 4)
+        done = []
+        for j in range(0, len(planes), 4):
+            quad = jnp.concatenate([jnp.concatenate(planes[j + i : j + i + 2], axis=0) for i in (0, 2)], axis=1)
+            quad = dot(table[...], stack_rows(quad))
+            done += [quad[i * ey : (i + 1) * ey, k * LANES : (k + 1) * LANES] for k in range(2) for i in range(2)]
+        return done[:cx], done[cx : cx + len(sides)]
+
+    def on(part, carry):
+        rows = []
+        for j in range(cx):
+            value = source(part * cx + j)
+            high, low = split(value[:, :LANES])
+            near = value[:, LANES:].astype(BF16).astype(F32)
+            halo = near + pltpu.roll(value[:, LANES:] - near, group, 1) + pltpu.roll(near, 2 * group, 1)
+            rows.append((high, low, high, halo.astype(BF16)))
+        value = dot(jnp.concatenate([jnp.concatenate(piece, axis=0) for piece in zip(*rows)], axis=1), z_on[...])
+        sides = []
+        for k in range(cx // 8):
+            side = nothing
+            for j in range(8):
+                turned = pltpu.roll(value[(8 * k + j) * ey : (8 * k + j + 1) * ey, LANES:], j * group, 1)
+                side = jnp.where(lane // group == j, turned, side)
+            sides.append(side)
+        core, sides = times_y(y_on, value[:, :LANES], sides)
+        for j in range(cx):
+            s0[rows_of((part * cx + j) * ey, ey), :] = core[j]
+        for k in range(cx // 8):
+            for q in range(octs):
+                s1[rows_of(q * count + part * cx + k * 8, 8), :] = turn(sides[k][q * 8 : (q + 1) * 8])
+        return carry
+
+    lax.fori_loop(0, count // cx, on, 0, unroll=2)
 
     def times_x(value, factor):
         value = dot(x_on[...], stack_rows(value))
@@ -224,19 +233,28 @@
     for q in range(octs):
         value = times_x(s1[q * count : (q + 1) * count, :], recip[ey + q])
         s1[q * count : q * count + back, :] = value
-    lax.fori_loop(0, ey // 2, middle, 0, unroll=10)
-
-    def off(k, carry):
-        side = jnp.concatenate([turn(s1[rows_of(q * count + k * 8, 8), :]) for q in range(octs)], axis=0)
-        core, side = times_y(y_back, s0[rows_of(k * 8 * ey, 8 * ey), :], side)
-        side = jnp.concatenate([side] + [pltpu.roll(side, LANES - j * group, 1) for j in range(1, 8)], axis=0)
-        high, low = split(jnp.concatenate([core, side], axis=1))
-        value = dot_nt(high, z_high) + (dot_nt(high, z_low) + dot_nt(low, z_high))
-        for j in range(8):
-            store(8 * k + j, value[j * ey : (j + 1) * ey])
-        return carry
-
-    lax.fori_loop(0, back // 8, off, 0, unroll=2 if back % 16 == 0 else 3)
+    lax.fori_loop(0, ey // 2, middle, 0, unroll=20)
+
+    def off(part, carry):
+        sides = []
+        for k in range(cx // 8):
+            sides.append(jnp.concatenate([turn(s1[rows_of(q * count + part * cx + k * 8, 8), :]) for q in range(octs)], axis=0))
+        core, sides = times_y(y_back, s0[rows_of(part * cx * ey, cx * ey), :], sides)
+        rows = []
+        for k in range(cx // 8):
+            near = sides[k].astype(BF16).astype(F32)
+            far = sides[k] - near
+            for j in range(8):
+                high, low = split(core[8 * k + j])
+                halo = [pltpu.roll(piece, (i - j) * group % LANES, 1) for i, piece in enumerate((near, far, near))]
+                halo = jnp.where(lane < group, halo[0], jnp.where(lane < 2 * group, halo[1], halo[2]))
+                rows.append((high, low, high, halo.astype(BF16)))
+        value = dot(jnp.concatenate([jnp.concatenate(piece, axis=0) for piece in zip(*rows)], axis=1), z_back[...])
+        for j in range(cx):
+            store(part * cx + j, value[j * ey : (j + 1) * ey])
+        return carry
+
+    lax.fori_loop(0, back // cx, off, 0, unroll=2 if back > cx else 1)
 
 
 def merged(core, halo, low):
@@ -244,7 +262,7 @@
     return jnp.where((lane < LANES // 2) == low, core, halo)
 
 
-def first_solve(info, field, got_one, got_two, zt, y_on, y_back, x_on, x_back, recip, u, block, rest, one, two, s0, s1, *, nz, ov, ey, cz):
+def first_solve(info, field, got_one, got_two, z_on, z_back, y_on, y_back, x_on, x_back, recip, u, block, rest, one, two, s0, s1, *, nz, ov, ey, cx, cz):
     along = Side(info[2], nz)
     count = field.shape[0] // ey
     w = 2 * ov + 1
@@ -260,7 +278,7 @@
     def store(x, value):
         u[rows_of(x * ey, ey), :] = value
 
-    solve(source, store, (zt, y_on, y_back, x_on, x_back, recip), (s0, s1), count, count, ey)
+    solve(source, store, (z_on, z_back, y_on, y_back, x_on, x_back, recip), (s0, s1), count, count, ey, cx)
 
     for out, low in ((one, ~along.even), (two, along.even)):
 
@@ -329,7 +347,7 @@
         lax.fori_loop(0, cx, plane, 0, unroll=4)
 
 
-def second_solve(info, core_in, rest_in, got_one, got_two, block, coef, zt, y_on, y_back, x_on, x_back, recip, u, first, one, two, s0, s1, core_v, rest_v, far, *, ny, nz, ov, ey, cx, cz):
+def second_solve(info, core_in, rest_in, got_one, got_two, block, coef, z_on, z_back, y_on, y_back, x_on, x_back, recip, u, first, one, two, s0, s1, core_v, rest_v, far, *, ny, nz, ov, ey, cx, cz):
     side, along = Side(info[1], ny), Side(info[2], nz)
     count = coef.shape[0] // ey
     tall, halo = 2 * ov, 2 * (ov + 1)
@@ -395,7 +413,7 @@
         u[rows, :] = value[:, :LANES]
         far[rows, :] = value[:, LANES:]
 
-    solve(plane, store, (zt, y_on, y_back, x_on, x_back, recip), (s0, s1), count, cx, ey)
+    solve(plane, store, (z_on, z_back, y_on, y_back, x_on, x_back, recip), (s0, s1), count, cx, ey, cx)
 
     def load(x):
         return far[rows_of(x * ey, ey), :]
@@ -441,12 +459,34 @@
     lax.fori_loop(0, cx, add, 0, unroll=8)
 
 
-def reciprocals(eigen_x, rest, out):
+def make_tables(eigen_x, rest, zt, out, z_on, z_back, *, ov, ez):
     def row(q, carry):
         out[q] = 1.0 / (eigen_x[...] + rest[pl.ds(q, 1), :])
         return carry
 
     lax.fori_loop(0, out.shape[0], row, 0, unroll=5)
+
+    def fill(table, ref, halo):
+        high = table.astype(BF16).astype(F32)
+        low = table - high
+        ref[:LANES] = high[:LANES].astype(BF16)
+        ref[LANES : 2 * LANES] = high[:LANES].astype(BF16)
+        ref[2 * LANES : 3 * LANES] = low[:LANES].astype(BF16)
+        ref[3 * LANES :] = halo(high, low).astype(BF16)
+
+    def ring(high, low):
+        above, below = slice(LANES, LANES + ov), slice(RING - ov, RING)
+        parts = [high[above], high[below], high[above], low[below], low[above], jnp.zeros((LANES - 6 * ov, RING), F32), high[below]]
+        return jnp.concatenate(parts, axis=0)
+
+    def plain(high, low):
+        tail = slice(LANES, ez)
+        parts = [high[tail], high[tail], low[tail], jnp.zeros((LANES - 3 * (ez - LANES), RING), F32)]
+        return jnp.concatenate(parts, axis=0)
+
+    table = zt[...]
+    fill(table, z_on, ring)
+    fill(table.T, z_back, plain)
 
 
 def gather_x(block):
@@ -484,8 +524,11 @@
     zt = jnp.pad(zt, ((0, 0), (0, RING - ez)))
     rest = eigen_y[:, None] + eigen_z[None, :]
     rest = jnp.concatenate([rest[:, :LANES], rest[:, LANES:].reshape(-1, LANES)], axis=0)
-    recip = call(reciprocals, [(rest.shape[0], ex, LANES)], jnp.broadcast_to(eigen_x[:, None], (ex, LANES)), rest, smem=0)[0]
-    tables = (zt, columns(double.T), columns(double), columns(table), columns(table.T), recip)
+    recip, z_on, z_back = call(
+        functools.partial(make_tables, ov=ov, ez=ez), [(rest.shape[0], ex, LANES), (4 * LANES, RING, BF16), (4 * LANES, RING, BF16)],
+        jnp.broadcast_to(eigen_x[:, None], (ex, LANES)), rest, zt, smem=0,
+    )
+    tables = (z_on, z_back, columns(double.T), columns(double), columns(table), columns(table.T), recip)
 
     slabs = call(functools.partial(first_slabs, ny=ny, ov=ov), [(count + cx, ov, cz)] * 2, info, *f_parts, reaction)
     got = swap(*slabs, "gy")
@@ -499,7 +542,7 @@
     state = [pltpu.VMEM((count * ey, LANES), F32), pltpu.VMEM((ey // 8 * count, LANES), F32)]
     small = (group_of(count, w) * ey, LANES)
     u, block, rest, *slabs = call(
-        functools.partial(first_solve, nz=nz, **at), [(count * ey, RING)] * 2 + [(2 * edge, LANES), small, small], info, f, *got, *tables, scratch=state
+        functools.partial(first_solve, nz=nz, cx=cx, **at), [(count * ey, RING)] * 2 + [(2 * edge, LANES), small, small], info, f, *got, *tables, scratch=state
     )
     got = swap(*slabs, "gz")
     c_parts += gather_x(rest)

time: 87.8 us -> 82.1 us (0.935)
  the two profiles are of different devices: /device:TPU:1 before, /device:TPU:11 now
where the time goes in v2:
time: 82.1 us; the launch traced here: 81.6 us
  waiting for transfers between devices  29.3 us (36%)
  Pallas kernels  23.6 us (29%)
  starting transfers between devices  23.4 us (29%)
  local copies, waits for them, and re-layouts  2.87 us (3%)
  other arithmetic  2.22 us (3%)
    pallas_call x9, Pallas kernels, call(): pl.pallas_call(body, out_shape=[jax.ShapeDtypeStruct(s[:2], BF16) if BF16...  23.6 us
    ppermute x6, starting transfers between devices, swap(): lax.ppermute(two, axis, pairs(count, 1))  18.6 us
    ppermute x6, waiting for transfers between devices, swap(): lax.ppermute(two, axis, pairs(count, 1))  13.9 us
    ppermute x3, waiting for transfers between devices, gather_x(): lax.ppermute(block, 'gx', [((i + shift) % count, i) for i in range(count)])  11.6 us
    ppermute x6, waiting for transfers between devices, swap(): lax.ppermute(one, axis, pairs(count, 0))  3.78 us
    ppermute x6, starting transfers between devices, swap(): lax.ppermute(one, axis, pairs(count, 0))  2.97 us
    ppermute x3, starting transfers between devices, gather_x(): lax.ppermute(block, 'gx', [((i + shift) % count, i) for i in range(count)])  1.85 us
  transfers between devices with their start and end apart: 15, of which 9 were waited for; matrix products, arithmetic and copies ran while one was open for 6% of the time, Pallas kernels for 3%

profile of v2, /device:TPU:11, one launch (start us, length us, event | category | flops | bytes accessed | tf_op | source)
XLA Modules:
  0.0 81.6 jit_solution(12510369413461509349)
XLA Ops:
  0.0 0.0 copy-start
  0.0 0.0 copy-start.2
  0.0 0.0 copy-start.3
  0.0 0.0 copy-start.1
  0.0 0.3 collective-permute-start
  0.3 0.8 broadcast_add_fusion
  1.1 0.9 %slice.20 = f32[136,144]{1,0:T(8,128)S(1)} slice(f32[144,144]{1,0:T(8,128)} %param.12), slice={[8:144], [0:144]} | slice | bytes 156672 | tf_op jit(solution)/shard_map/slice | solution.py:523
  2.0 0.7 slice.21
  2.7 0.8 pad_slice_fusion.1
  3.5 0.1 fusion.3
  3.7 0.1 copy.14.refs_8_.refs_11_
  3.8 0.1 reshape.6
  3.8 0.1 pad.36.clone
  3.9 0.1 pad_maximum_fusion
  4.1 0.9 %fusion = (bf16[80,80]{0,1:T(8,128)(2,1)S(1)}, bf16[80,80]{0,1:T(8,128)(2,1)S(1)}) fusion(f32[40,40]{1,0:T(8,128)} %param.11), kind=kLoop, calls=%fused_computation.10 | loop fusion | flops 57600 | bytes 32000 | tf_op jit(solution)/shard_map/convert.10
  5.0 0.1 copy.13.refs_6_.refs_9_
  5.1 0.0 copy-done.3
  5.1 0.1 broadcast_in_dim.4.refs_0_
  5.2 0.3 shard_map.84
  5.5 0.1 pad_add_fusion.refs_0_
  5.6 0.0 copy-done.2
  5.6 0.1 fusion.1
  5.6 2.5 %collective-permute-done.refs_2_ = f32[24,24,128]{2,1,0:T(8,128)S(1)} collective-permute-done((f32[24,24,128]{2,1,0:T(8,128)}, f32[24,24,128]{2,1,0:T(8,128)S(1)}, u32[]{:S(2)}, u32[]{:S(2)}) %collective-permute-start) | collective-permute-done | bytes 294944 | tf_op jit(solution)/shard_map/ppermute | solution.py:496
  8.2 0.0 copy-done
  8.2 0.0 copy-done.1
  8.2 0.6 shard_map.82
  8.8 0.2 collective-permute-start.1
  9.0 4.3 %collective-permute-start.2 = (f32[72,8,128]{2,1,0:T(8,128)S(1)}, f32[72,8,128]{2,1,0:T(8,128)S(1)}, u32[]{:S(2)}, u32[]{:S(2)}) collective-permute-start(f32[72,8,128]{2,1,0:T(8,128)S(1)} %get-tuple-element.31), channel_id=1, source_target_pairs={{0,0},{4,8},{8,4},{12,12},{1,1},{5,9},{9,5},{13,13},{2,2},{6,10},{... | collective-permute-start | bytes 884744 | tf_op jit(solution)/shard_map/ppermute | solution.py:27
  13.4 0.1 pad_maximum_fusion.2.refs_7_.refs_10_
  13.5 2.4 %collective-permute-done.1.refs_4_ = f32[72,8,128]{2,1,0:T(8,128)S(1)} collective-permute-done((f32[72,8,128]{2,1,0:T(8,128)S(1)}, f32[72,8,128]{2,1,0:T(8,128)S(1)}, u32[]{:S(2)}, u32[]{:S(2)}) %collective-permute-start.1) | collective-permute-done | bytes 294944 | tf_op jit(solution)/shard_map/ppermute | solution.py:27
  15.9 3.0 %collective-permute-done.2.refs_5_ = f32[72,8,128]{2,1,0:T(8,128)S(1)} collective-permute-done((f32[72,8,128]{2,1,0:T(8,128)S(1)}, f32[72,8,128]{2,1,0:T(8,128)S(1)}, u32[]{:S(2)}, u32[]{:S(2)}) %collective-permute-start.2) | collective-permute-done | bytes 294944 | tf_op jit(solution)/shard_map/ppermute | solution.py:27
  18.9 1.5 %shard_map.83 = (f32[1920,128]{1,0:T(8,128)S(1)}, f32[960,128]{1,0:T(8,128)S(1)}, f32[200,128]{1,0:T(8,128)S(1)}, f32[200,128]{1,0:T(8,128)S(1)}) custom-call(s32[3]{0:T(128)S(1)} %pad_add_fusion.refs_0_, f32[24,24,128]{2,1,0:T(8,128)S(1)} %copy-done, f32[24,24,128]{2,1,0:T(8,128)S(1)} %collective-permute-done.refs_2_, f32[24,24,128]{2,1,0:T(8,128)S(1)} %copy-done.1, ...), custom_call_target="tpu_custom_call" | custom-call | tf_op jit(solution)/shard_map/pallas_call | solution.py:40
  20.4 2.5 %collective-permute-start.3 = (f32[200,128]{1,0:T(8,128)S(1)}, f32[200,128]{1,0:T(8,128)S(1)}, u32[]{:S(2)}, u32[]{:S(2)}) collective-permute-start(f32[200,128]{1,0:T(8,128)S(1)} %get-tuple-element.33), channel_id=1, source_target_pairs={{0,1},{1,0},{2,3},{3,2},{4,5},{5,4},{6,7},{7,6},{8,9},{9,8},{10,11... | collective-permute-start | bytes 307208 | tf_op jit(solution)/shard_map/ppermute | solution.py:27
  22.9 3.0 %collective-permute-start.4 = (f32[200,128]{1,0:T(8,128)S(1)}, f32[200,128]{1,0:T(8,128)S(1)}, u32[]{:S(2)}, u32[]{:S(2)}) collective-permute-start(f32[200,128]{1,0:T(8,128)S(1)} %get-tuple-element.34), channel_id=1, source_target_pairs={{0,0},{1,2},{2,1},{3,3},{4,4},{5,6},{6,5},{7,7},{8,8},{9,10},{10,9... | collective-permute-start | bytes 307208 | tf_op jit(solution)/shard_map/ppermute | solution.py:27
  25.9 0.1 pad_maximum_fusion.5.refs_9_.refs_12_
  26.0 0.0 collective-permute-done.3.refs_2_
  26.0 2.8 %collective-permute-done.4.refs_3_ = f32[200,128]{1,0:T(8,128)S(1)} collective-permute-done((f32[200,128]{1,0:T(8,128)S(1)}, f32[200,128]{1,0:T(8,128)S(1)}, u32[]{:S(2)}, u32[]{:S(2)}) %collective-permute-start.4) | collective-permute-done | bytes 102432 | tf_op jit(solution)/shard_map/ppermute | solution.py:27
  28.8 6.3 %shard_map.85 = (f32[1920,256]{1,0:T(8,128)S(1)}, f32[1920,256]{1,0:T(8,128)S(1)}, f32[160,128]{1,0:T(8,128)S(1)}, f32[280,128]{1,0:T(8,128)S(1)}, f32[280,128]{1,0:T(8,128)S(1)}) custom-call(s32[3]{0:T(128)S(1)} %pad_add_fusion.refs_0_, f32[1920,128]{1,0:T(8,128)S(1)} %get-tuple-element.32.refs_1_, f32[200,128]{1,0:T(8,128)S(1)} %collective-permute-done.3.refs_2_, ...), custom_call_target="tpu_custom_call" | custom-call | tf_op jit(solution)/shard_map/pallas_call | solution.py:40
  35.1 0.1 collective-permute-start.5
  35.2 3.1 %collective-permute-start.6 = (f32[280,128]{1,0:T(8,128)S(1)}, f32[280,128]{1,0:T(8,128)S(1)}, u32[]{:S(2)}, u32[]{:S(2)}) collective-permute-start(f32[280,128]{1,0:T(8,128)S(1)} %get-tuple-element.40), channel_id=1, source_target_pairs={{0,0},{1,2},{2,1},{3,3},{4,4},{5,6},{6,5},{7,7},{8,8},{9,10},{10,9... | collective-permute-start | bytes 430088 | tf_op jit(solution)/shard_map/ppermute | solution.py:27
  38.3 0.0 collective-permute-done.5.refs_2_
  38.3 3.3 %collective-permute-done.6.refs_3_ = f32[280,128]{1,0:T(8,128)S(1)} collective-permute-done((f32[280,128]{1,0:T(8,128)S(1)}, f32[280,128]{1,0:T(8,128)S(1)}, u32[]{:S(2)}, u32[]{:S(2)}) %collective-permute-start.6) | collective-permute-done | bytes 143392 | tf_op jit(solution)/shard_map/ppermute | solution.py:27
  41.6 2.1 %shard_map.86 = (f32[1920,128]{1,0:T(8,128)S(1)}, f32[1920,128]{1,0:T(8,128)S(1)}, f32[976,128]{1,0:T(8,128)S(1)}, f32[976,128]{1,0:T(8,128)S(1)}) custom-call(s32[3]{0:T(128)S(1)} %pad_add_fusion.refs_0_, f32[1920,256]{1,0:T(8,128)S(1)} %get-tuple-element.38.refs_1_, f32[280,128]{1,0:T(8,128)S(1)} %collective-permute-done.5.refs_2_, ...), custom_call_target="tpu_custom_call" | custom-call | tf_op jit(solution)/shard_map/pallas_call | solution.py:40
  43.8 0.1 collective-permute-start.7
  43.8 3.5 %collective-permute-start.8 = (f32[976,128]{1,0:T(8,128)S(1)}, f32[976,128]{1,0:T(8,128)S(1)}, u32[]{:S(2)}, u32[]{:S(2)}) collective-permute-start(f32[976,128]{1,0:T(8,128)S(1)} %get-tuple-element.44), channel_id=1, source_target_pairs={{0,0},{4,8},{8,4},{12,12},{1,1},{5,9},{9,5},{13,13},{2,2},{6,10},{... | collective-permute-start | bytes 1499144 | tf_op jit(solution)/shard_map/ppermute | solution.py:27
  47.4 0.3 collective-permute-start.9
  47.7 1.2 %collective-permute-start.10 = (f32[160,128]{1,0:T(8,128)S(1)}, f32[160,128]{1,0:T(8,128)S(1)}, u32[]{:S(2)}, u32[]{:S(2)}) collective-permute-start(f32[160,128]{1,0:T(8,128)S(1)} %get-tuple-element.47.refs_3_), channel_id=1, source_target_pairs={{16,0},{0,16},{17,1},{1,17},{18,2},{2,18},{19,3},{3,19},{20,4},{4,... | collective-permute-start | bytes 245768 | tf_op jit(solution)/shard_map/ppermute | solution.py:496
  48.9 9.1 %collective-permute-done.10.refs_4_ = f32[160,128]{1,0:T(8,128)S(1)} collective-permute-done((f32[160,128]{1,0:T(8,128)S(1)}, f32[160,128]{1,0:T(8,128)S(1)}, u32[]{:S(2)}, u32[]{:S(2)}) %collective-permute-start.10) | collective-permute-done | bytes 81952 | tf_op jit(solution)/shard_map/ppermute | solution.py:496
  58.0 0.0 collective-permute-done.9.refs_2_
  58.0 2.0 %shard_map.87.refs_6_ = f32[1920,256]{1,0:T(8,128)S(1)} custom-call(s32[3]{0:T(128)S(1)} %pad_add_fusion.refs_0_, f32[960,128]{1,0:T(8,128)S(1)} %get-tuple-element.46.refs_1_, f32[960,128]{1,0:T(8,128)S(1)} %collective-permute-done.9.refs_2_, f32[160,128]{1,0:T(8,128)S(1)} %get-tuple-element.47.refs_3_, f32[160,128]{1,0:T(8,128)S(1)} %collective-permute-done.10.refs_4_, ...), custom_call_target="tpu_custom_call" | custom-call | tf_op jit(solution)/shard_map/pallas_call | solution.py:40
  60.0 0.0 collective-permute-done.7.refs_3_
  60.0 0.0 collective-permute-done.8.refs_4_
  60.0 8.3 %shard_map.88 = (f32[960,128]{1,0:T(8,128)S(1)}, f32[576,128]{1,0:T(8,128)S(1)}, f32[80,128]{1,0:T(8,128)S(1)}, f32[80,128]{1,0:T(8,128)S(1)}) custom-call(s32[3]{0:T(128)S(1)} %pad_add_fusion.refs_0_, f32[1920,128]{1,0:T(8,128)S(1)} %get-tuple-element.41.refs_1_, f32[1920,128]{1,0:T(8,128)S(1)} %get-tuple-element.42.refs_2_, ...), custom_call_target="tpu_custom_call" | custom-call | tf_op jit(solution)/shard_map/pallas_call | solution.py:40
  68.4 0.1 collective-permute-start.11
  68.4 2.5 %collective-permute-start.12 = (f32[80,128]{1,0:T(8,128)S(1)}, f32[80,128]{1,0:T(8,128)S(1)}, u32[]{:S(2)}, u32[]{:S(2)}) collective-permute-start(f32[80,128]{1,0:T(8,128)S(1)} %get-tuple-element.50), channel_id=1, source_target_pairs={{0,0},{1,2},{2,1},{3,3},{4,4},{5,6},{6,5},{7,7},{8,8},{9,10},{10,9... | collective-permute-start | bytes 122888 | tf_op jit(solution)/shard_map/ppermute | solution.py:27
  71.0 0.0 collective-permute-done.11.refs_2_
  71.0 2.8 %collective-permute-done.12.refs_3_ = f32[80,128]{1,0:T(8,128)S(1)} collective-permute-done((f32[80,128]{1,0:T(8,128)S(1)}, f32[80,128]{1,0:T(8,128)S(1)}, u32[]{:S(2)}, u32[]{:S(2)}) %collective-permute-start.12) | collective-permute-done | bytes 40992 | tf_op jit(solution)/shard_map/ppermute | solution.py:27
  73.8 1.1 %shard_map.89 = (f32[960,128]{1,0:T(8,128)S(1)}, f32[192,128]{1,0:T(8,128)S(1)}, f32[192,128]{1,0:T(8,128)S(1)}) custom-call(s32[3]{0:T(128)S(1)} %pad_add_fusion.refs_0_, f32[960,128]{1,0:T(8,128)S(1)} %get-tuple-element.48.refs_1_, f32[80,128]{1,0:T(8,128)S(1)} %collective-permute-done.11.refs_2_, f32[80,128]{1,0:T(8,128)S(1)} %collective-permute-done.12.refs_3_), custom_call_target="tpu_custom_call" | custom-call | tf_op jit(solution)/shard_map/pallas_call | solution.py:40
  74.9 0.1 collective-permute-start.13
  75.0 2.1 %collective-permute-start.14 = (f32[192,128]{1,0:T(8,128)S(1)}, f32[192,128]{1,0:T(8,128)S(1)}, u32[]{:S(2)}, u32[]{:S(2)}) collective-permute-start(f32[192,128]{1,0:T(8,128)S(1)} %get-tuple-element.53), channel_id=1, source_target_pairs={{0,0},{4,8},{8,4},{12,12},{1,1},{5,9},{9,5},{13,13},{2,2},{6,10},{... | collective-permute-start | bytes 294920 | tf_op jit(solution)/shard_map/ppermute | solution.py:27
  77.1 1.3 %collective-permute-done.13.refs_2_ = f32[192,128]{1,0:T(8,128)S(1)} collective-permute-done((f32[192,128]{1,0:T(8,128)S(1)}, f32[192,128]{1,0:T(8,128)S(1)}, u32[]{:S(2)}, u32[]{:S(2)}) %collective-permute-start.13) | collective-permute-done | bytes 98336 | tf_op jit(solution)/shard_map/ppermute | solution.py:27
  78.4 1.9 %collective-permute-done.14.refs_3_ = f32[192,128]{1,0:T(8,128)S(1)} collective-permute-done((f32[192,128]{1,0:T(8,128)S(1)}, f32[192,128]{1,0:T(8,128)S(1)}, u32[]{:S(2)}, u32[]{:S(2)}) %collective-permute-start.14) | collective-permute-done | bytes 98336 | tf_op jit(solution)/shard_map/ppermute | solution.py:27
  80.3 1.3 %shard_map.90 = f32[24,24,128]{2,1,0:T(8,128)} custom-call(s32[3]{0:T(128)S(1)} %pad_add_fusion.refs_0_, f32[960,128]{1,0:T(8,128)S(1)} %get-tuple-element.51.refs_1_, f32[192,128]{1,0:T(8,128)S(1)} %collective-permute-done.13.refs_2_, f32[192,128]{1,0:T(8,128)S(1)} %collective-permute-done.14.refs_3_, f32[576,128]{1,0:T(8,128)S(1)} %get-tuple-element.54.refs_4_), custom_call_target="tpu_custom_call" | custom-call | tf_op jit(solution)/shard_map/pallas_call | solution.py:40
  (9 shorter events, 0.1 us)
Async XLA Ops:
  0.0 8.2 %copy-start = (f32[24,24,128]{2,1,0:T(8,128)S(1)}, f32[24,24,128]{2,1,0:T(8,128)}, u32[]{:S(2)}) copy-start(f32[24,24,128]{2,1,0:T(8,128)} %refs_1_.3) | copy-start | bytes 884740
  0.0 5.6 %copy-start.2 = (f32[40,40]{1,0:T(8,128)S(1)}, f32[40,40]{1,0:T(8,128)}, u32[]{:S(2)}) copy-start(f32[40,40]{1,0:T(8,128)} %param.11) | copy-start | bytes 19204
  0.0 5.1 %copy-start.3 = (f32[40]{0:T(128)S(1)}, f32[40]{0:T(128)}, u32[]{:S(2)}) copy-start(f32[40]{0:T(128)} %param.13) | copy-start | bytes 484
  0.0 8.2 %copy-start.1 = (f32[24,24,128]{2,1,0:T(8,128)S(1)}, f32[24,24,128]{2,1,0:T(8,128)}, u32[]{:S(2)}) copy-start(f32[24,24,128]{2,1,0:T(8,128)} %refs_3_.3) | copy-start | bytes 884740
  0.0 8.2 %collective-permute-start = (f32[24,24,128]{2,1,0:T(8,128)}, f32[24,24,128]{2,1,0:T(8,128)S(1)}, u32[]{:S(2)}, u32[]{:S(2)}) collective-permute-start(f32[24,24,128]{2,1,0:T(8,128)} %refs_1_.3), channel_id=1, source_target_pairs={{16,0},{0,16},{17,1},{1,17},{18,2},{2,18},{19,3},{3,19},{20,4},{4,... | collective-permute-start | bytes 884744 | tf_op jit(solution)/shard_map/ppermute | solution.py:496
  8.8 7.1 %collective-permute-start.1 = (f32[72,8,128]{2,1,0:T(8,128)S(1)}, f32[72,8,128]{2,1,0:T(8,128)S(1)}, u32[]{:S(2)}, u32[]{:S(2)}) collective-permute-start(f32[72,8,128]{2,1,0:T(8,128)S(1)} %get-tuple-element.30), channel_id=1, source_target_pairs={{0,4},{4,0},{8,12},{12,8},{1,5},{5,1},{9,13},{13,9},{2,6},{6,2},{1... | collective-permute-start | bytes 884744 | tf_op jit(solution)/shard_map/ppermute | solution.py:27
  9.0 9.9 %collective-permute-start.2 = (f32[72,8,128]{2,1,0:T(8,128)S(1)}, f32[72,8,128]{2,1,0:T(8,128)S(1)}, u32[]{:S(2)}, u32[]{:S(2)}) collective-permute-start(f32[72,8,128]{2,1,0:T(8,128)S(1)} %get-tuple-element.31), channel_id=1, source_target_pairs={{0,0},{4,8},{8,4},{12,12},{1,1},{5,9},{9,5},{13,13},{2,2},{6,10},{... | collective-permute-start | bytes 884744 | tf_op jit(solution)/shard_map/ppermute | solution.py:27
  20.4 5.6 %collective-permute-start.3 = (f32[200,128]{1,0:T(8,128)S(1)}, f32[200,128]{1,0:T(8,128)S(1)}, u32[]{:S(2)}, u32[]{:S(2)}) collective-permute-start(f32[200,128]{1,0:T(8,128)S(1)} %get-tuple-element.33), channel_id=1, source_target_pairs={{0,1},{1,0},{2,3},{3,2},{4,5},{5,4},{6,7},{7,6},{8,9},{9,8},{10,11... | collective-permute-start | bytes 307208 | tf_op jit(solution)/shard_map/ppermute | solution.py:27
  22.9 6.0 %collective-permute-start.4 = (f32[200,128]{1,0:T(8,128)S(1)}, f32[200,128]{1,0:T(8,128)S(1)}, u32[]{:S(2)}, u32[]{:S(2)}) collective-permute-start(f32[200,128]{1,0:T(8,128)S(1)} %get-tuple-element.34), channel_id=1, source_target_pairs={{0,0},{1,2},{2,1},{3,3},{4,4},{5,6},{6,5},{7,7},{8,8},{9,10},{10,9... | collective-permute-start | bytes 307208 | tf_op jit(solution)/shard_map/ppermute | solution.py:27
  35.1 3.1 %collective-permute-start.5 = (f32[280,128]{1,0:T(8,128)S(1)}, f32[280,128]{1,0:T(8,128)S(1)}, u32[]{:S(2)}, u32[]{:S(2)}) collective-permute-start(f32[280,128]{1,0:T(8,128)S(1)} %get-tuple-element.39), channel_id=1, source_target_pairs={{0,1},{1,0},{2,3},{3,2},{4,5},{5,4},{6,7},{7,6},{8,9},{9,8},{10,11... | collective-permute-start | bytes 430088 | tf_op jit(solution)/shard_map/ppermute | solution.py:27
  35.2 6.4 %collective-permute-start.6 = (f32[280,128]{1,0:T(8,128)S(1)}, f32[280,128]{1,0:T(8,128)S(1)}, u32[]{:S(2)}, u32[]{:S(2)}) collective-permute-start(f32[280,128]{1,0:T(8,128)S(1)} %get-tuple-element.40), channel_id=1, source_target_pairs={{0,0},{1,2},{2,1},{3,3},{4,4},{5,6},{6,5},{7,7},{8,8},{9,10},{10,9... | collective-permute-start | bytes 430088 | tf_op jit(solution)/shard_map/ppermute | solution.py:27
  43.8 16.3 %collective-permute-start.7 = (f32[976,128]{1,0:T(8,128)S(1)}, f32[976,128]{1,0:T(8,128)S(1)}, u32[]{:S(2)}, u32[]{:S(2)}) collective-permute-start(f32[976,128]{1,0:T(8,128)S(1)} %get-tuple-element.43.refs_5_), channel_id=1, source_target_pairs={{0,4},{4,0},{8,12},{12,8},{1,5},{5,1},{9,13},{13,9},{2,6},{6,2},{1... | collective-permute-start | bytes 1499144 | tf_op jit(solution)/shard_map/ppermute | solution.py:27
  43.8 16.2 %collective-permute-start.8 = (f32[976,128]{1,0:T(8,128)S(1)}, f32[976,128]{1,0:T(8,128)S(1)}, u32[]{:S(2)}, u32[]{:S(2)}) collective-permute-start(f32[976,128]{1,0:T(8,128)S(1)} %get-tuple-element.44), channel_id=1, source_target_pairs={{0,0},{4,8},{8,4},{12,12},{1,1},{5,9},{9,5},{13,13},{2,2},{6,10},{... | collective-permute-start | bytes 1499144 | tf_op jit(solution)/shard_map/ppermute | solution.py:27
  47.4 10.6 %collective-permute-start.9 = (f32[960,128]{1,0:T(8,128)S(1)}, f32[960,128]{1,0:T(8,128)S(1)}, u32[]{:S(2)}, u32[]{:S(2)}) collective-permute-start(f32[960,128]{1,0:T(8,128)S(1)} %get-tuple-element.46.refs_1_), channel_id=1, source_target_pairs={{16,0},{0,16},{17,1},{1,17},{18,2},{2,18},{19,3},{3,19},{20,4},{4,... | collective-permute-start | bytes 1474568 | tf_op jit(solution)/shard_map/ppermute | solution.py:496
  47.7 10.3 %collective-permute-start.10 = (f32[160,128]{1,0:T(8,128)S(1)}, f32[160,128]{1,0:T(8,128)S(1)}, u32[]{:S(2)}, u32[]{:S(2)}) collective-permute-start(f32[160,128]{1,0:T(8,128)S(1)} %get-tuple-element.47.refs_3_), channel_id=1, source_target_pairs={{16,0},{0,16},{17,1},{1,17},{18,2},{2,18},{19,3},{3,19},{20,4},{4,... | collective-permute-start | bytes 245768 | tf_op jit(solution)/shard_map/ppermute | solution.py:496
  68.4 2.6 %collective-permute-start.11 = (f32[80,128]{1,0:T(8,128)S(1)}, f32[80,128]{1,0:T(8,128)S(1)}, u32[]{:S(2)}, u32[]{:S(2)}) collective-permute-start(f32[80,128]{1,0:T(8,128)S(1)} %get-tuple-element.49), channel_id=1, source_target_pairs={{0,1},{1,0},{2,3},{3,2},{4,5},{5,4},{6,7},{7,6},{8,9},{9,8},{10,11... | collective-permute-start | bytes 122888 | tf_op jit(solution)/shard_map/ppermute | solution.py:27
  68.4 5.3 %collective-permute-start.12 = (f32[80,128]{1,0:T(8,128)S(1)}, f32[80,128]{1,0:T(8,128)S(1)}, u32[]{:S(2)}, u32[]{:S(2)}) collective-permute-start(f32[80,128]{1,0:T(8,128)S(1)} %get-tuple-element.50), channel_id=1, source_target_pairs={{0,0},{1,2},{2,1},{3,3},{4,4},{5,6},{6,5},{7,7},{8,8},{9,10},{10,9... | collective-permute-start | bytes 122888 | tf_op jit(solution)/shard_map/ppermute | solution.py:27
  74.9 3.5 %collective-permute-start.13 = (f32[192,128]{1,0:T(8,128)S(1)}, f32[192,128]{1,0:T(8,128)S(1)}, u32[]{:S(2)}, u32[]{:S(2)}) collective-permute-start(f32[192,128]{1,0:T(8,128)S(1)} %get-tuple-element.52), channel_id=1, source_target_pairs={{0,4},{4,0},{8,12},{12,8},{1,5},{5,1},{9,13},{13,9},{2,6},{6,2},{1... | collective-permute-start | bytes 294920 | tf_op jit(solution)/shard_map/ppermute | solution.py:27
  75.0 5.4 %collective-permute-start.14 = (f32[192,128]{1,0:T(8,128)S(1)}, f32[192,128]{1,0:T(8,128)S(1)}, u32[]{:S(2)}, u32[]{:S(2)}) collective-permute-start(f32[192,128]{1,0:T(8,128)S(1)} %get-tuple-element.53), channel_id=1, source_target_pairs={{0,0},{4,8},{8,4},{12,12},{1,1},{5,9},{9,5},{13,13},{2,2},{6,10},{... | collective-permute-start | bytes 294920 | tf_op jit(solution)/shard_map/ppermute | solution.py:27

commit v3 on v2

--- a/solution.py
+++ b/solution.py
@@ -15,16 +15,18 @@
 BF16 = jnp.bfloat16
 
 
-def pairs(count, first):
+def pairs(count, first, around):
     swaps = {}
     for low in range(first, count - 1, 2):
         swaps[low], swaps[low + 1] = low + 1, low
+    if around and first == 1 and count % 2 == 0 and count > 2:
+        swaps[0], swaps[count - 1] = count - 1, 0
     return [(i, swaps.get(i, i)) for i in range(count)]
 
 
-def swap(one, two, axis):
+def swap(one, two, axis, around=False):
     count = lax.axis_size(axis)
-    return lax.ppermute(one, axis, pairs(count, 0)), lax.ppermute(two, axis, pairs(count, 1))
+    return lax.ppermute(one, axis, pairs(count, 0, around)), lax.ppermute(two, axis, pairs(count, 1, around))
 
 
 def call(kernel, outs, *args, scratch=(), smem=1, after=()):
@@ -72,6 +74,10 @@
 
 def group_of(count, width):
     return -(-count // (LANES // width))
+
+
+def odd_group(count, width):
+    return next(n for n in range(8, count + 1, 8) if count % n == 0 and count // n * width <= LANES)
 
 
 def pack(load, count, rows, width, src, out):
@@ -141,7 +147,7 @@
             out[rows_of(row + ov + cy, ov), :] = jnp.where(side.has_above, above, 0.0)
             return carry
 
-        lax.fori_loop(0, cx, place, 0, unroll=8)
+        lax.fori_loop(0, cx, place, 0, unroll=24)
 
     edge = group_of(count, ov) * ey
     for ref, planes, first in ((field, count, 0), (coef, cx, edge)):
@@ -307,9 +313,9 @@
         rest_out[rows, :] = jnp.where(inside, rest, 0.0)
         return carry
 
-    lax.fori_loop(0, count, add, 0, unroll=8)
+    lax.fori_loop(0, count, add, 0, unroll=16)
     tall, halo = 2 * ov, 2 * (ov + 1)
-    each = group_of(count, halo)
+    wide = group_of(count, halo)
     for out, high in ((one, side.even), (two, ~side.even)):
         start = jnp.where(high, ey - tall, 0)
         odd = pl.ds(jnp.where(high, ey - tall - 1, tall), count, stride=ey)
@@ -318,16 +324,23 @@
             out[rows_of(x * tall, tall), :] = core_out[rows_of(x * ey + start, tall), :]
             return carry
 
-        lax.fori_loop(0, count, main, 0, unroll=8)
+        lax.fori_loop(0, count, main, 0, unroll=16)
         base = count * tall
 
         def load(x, start=start):
             return rest_out[rows_of(x * ey + start, tall), :]
 
-        pack(load, count, tall, halo, LANES - ov - 1, out.at[base : base + each * tall])
-        base = base + each * tall
+        pack(load, count, tall, halo, LANES - ov - 1, out.at[base : base + wide * tall])
+        base = base + wide * tall
         out[base : base + count, :] = core_out[odd, :]
-        out[base + count : base + 2 * count, :] = rest_out[odd, :]
+        rows = rest_out[odd, :]
+        each = odd_group(count, halo)
+        near = lane_of((each, LANES))
+        value = jnp.zeros((each, LANES), F32)
+        for g in range(count // each):
+            turned = pltpu.roll(rows[g * each : (g + 1) * each], (g * halo + ov + 1) % LANES, 1)
+            value = jnp.where((near >= g * halo) & (near < (g + 1) * halo), turned, value)
+        out[base + count :, :] = value
 
 
 def coefficients(info, *refs, nz, ov, ey):
@@ -381,9 +394,20 @@
             out[rows_of(x * room + ey, ov), :] = jnp.where(side.has_above, high[ov:], 0.0)
         return carry
 
-    lax.fori_loop(0, count, gather, 0, unroll=4)
-    for out, start in ((core_v, odd_rows), (rest_v, odd_rows + count)):
-        below, above = sides(got_one[start : start + count, :], got_two[start : start + count, :])
+    lax.fori_loop(0, count, gather, 0, unroll=8)
+    single = odd_group(count, halo)
+    near = lane_of((single, LANES))
+
+    def odd(ref):
+        value = ref[odd_rows + count :, :]
+        rows = [pltpu.roll(value, (2 * LANES - g * halo - ov - 1) % LANES, 1) for g in range(count // single)]
+        return jnp.concatenate([jnp.where((near <= ov) | (near >= LANES - ov - 1), row, 0.0) for row in rows], axis=0)
+
+    for out, a, b in (
+        (core_v, got_one[odd_rows : odd_rows + count, :], got_two[odd_rows : odd_rows + count, :]),
+        (rest_v, odd(got_one), odd(got_two)),
+    ):
+        below, above = sides(a, b)
         out[pl.ds(ov - 1, count, stride=room), :] = below
         out[pl.ds(ov + ey, count, stride=room), :] = above
 
@@ -441,7 +465,7 @@
         two[rows_of(x * ov, ov), :] = v[rows_of(x * ey + side.two(ey - ov, 0), ov), :]
         return carry
 
-    lax.fori_loop(0, cx, add, 0, unroll=8)
+    lax.fori_loop(0, cx, add, 0, unroll=24)
 
 
 def last_sum_y(info, v, got_one, got_two, first, out, *, ny, ov, ey, cx):
@@ -456,7 +480,7 @@
         out[x] = jnp.concatenate([value[:ov] + below, value[ov : cy - ov], value[cy - ov :] + above], axis=0)
         return carry
 
-    lax.fori_loop(0, cx, add, 0, unroll=8)
+    lax.fori_loop(0, cx, add, 0, unroll=24)
 
 
 def make_tables(eigen_x, rest, zt, out, z_on, z_back, *, ov, ez):
@@ -537,7 +561,7 @@
     f, c, *slabs = call(
         functools.partial(second_slabs, ny=ny, nz=nz, ov=ov), [(count * ey, cz), (cx * ey, cz), small, small], info, *f_parts, reaction, *got
     )
-    got = swap(*slabs, "gz")
+    got = swap(*slabs, "gz", around=True)
     c_parts = gather_x(c)
     state = [pltpu.VMEM((count * ey, LANES), F32), pltpu.VMEM((ey // 8 * count, LANES), F32)]
     small = (group_of(count, w) * ey, LANES)
@@ -546,7 +570,7 @@
     )
     got = swap(*slabs, "gz")
     c_parts += gather_x(rest)
-    tall_rows = (count * tall + group_of(count, halo) * tall + 2 * count, LANES)
+    tall_rows = (count * tall + group_of(count, halo) * tall + count + odd_group(count, halo), LANES)
     core, rest, *slabs = call(functools.partial(sum_z, ny=ny, nz=nz, **at), [(count * ey, LANES)] * 2 + [tall_rows, tall_rows], info, u, *got)
     got = swap(*slabs, "gy")
     c = call(functools.partial(coefficients, nz=nz, ov=ov, ey=ey), [(count * ey, RING)], info, *c_parts, after=slabs[:1])[0]
@@ -556,7 +580,7 @@
         functools.partial(second_solve, ny=ny, nz=nz, cx=cx, **at),
         [(cx * ey, LANES), (cx * cy, LANES), small, small], info, core, rest, *got, block, c, *tables, scratch=state,
     )
-    got = swap(*slabs, "gz")
+    got = swap(*slabs, "gz", around=True)
     v, *slabs = call(functools.partial(last_sum_z, ny=ny, nz=nz, cx=cx, **at), [(cx * ey, LANES)] + [(cx * ov, LANES)] * 2, info, u, *got)
     got = swap(*slabs, "gy")
     return call(functools.partial(last_sum_y, ny=ny, ov=ov, ey=ey, cx=cx), [(cx, cy, cz)], info, v, *got, first)[0]

time: 82.1 us -> 74.4 us (0.906)
  the two profiles are of different devices: /device:TPU:11 before, /device:TPU:16 now
where the time goes in v3:
time: 74.4 us; the launch traced here: 74 us
  waiting for transfers between devices  27.3 us (37%)
  Pallas kernels  22.6 us (30%)
  starting transfers between devices  18.8 us (25%)
  local copies, waits for them, and re-layouts  2.87 us (4%)
  other arithmetic  2.22 us (3%)
    pallas_call x9, Pallas kernels, call(): pl.pallas_call(body, out_shape=[jax.ShapeDtypeStruct(s[:2], BF16) if BF16...  22.6 us
    ppermute x6, waiting for transfers between devices, swap(): lax.ppermute(two, axis, pairs(count, 1, around))  10.7 us
    ppermute x6, starting transfers between devices, swap(): lax.ppermute(two, axis, pairs(count, 1, around))  9.6 us
    ppermute x3, waiting for transfers between devices, gather_x(): lax.ppermute(block, 'gx', [((i + shift) % count, i) for i in range(count)])  9.6 us
    ppermute x6, waiting for transfers between devices, swap(): lax.ppermute(one, axis, pairs(count, 0, around))  6.93 us
    ppermute x6, starting transfers between devices, swap(): lax.ppermute(one, axis, pairs(count, 0, around))  5.49 us
    ppermute x3, starting transfers between devices, gather_x(): lax.ppermute(block, 'gx', [((i + shift) % count, i) for i in range(count)])  3.72 us
  transfers between devices with their start and end apart: 15, of which 8 were waited for; matrix products, arithmetic and copies ran while one was open for 7% of the time, Pallas kernels for 6%

profile of v3, /device:TPU:16, one launch (start us, length us, event | category | flops | bytes accessed | tf_op | source)
XLA Modules:
  0.0 74.0 jit_solution(17989419035170464946)
XLA Ops:
  0.0 0.0 copy-start
  0.0 0.0 copy-start.2
  0.0 0.0 copy-start.3
  0.0 0.0 copy-start.1
  0.0 1.6 %collective-permute-start = (f32[24,24,128]{2,1,0:T(8,128)}, f32[24,24,128]{2,1,0:T(8,128)S(1)}, u32[]{:S(2)}, u32[]{:S(2)}) collective-permute-start(f32[24,24,128]{2,1,0:T(8,128)} %refs_1_.3), channel_id=1, source_target_pairs={{16,0},{0,16},{17,1},{1,17},{18,2},{2,18},{19,3},{3,19},{20,4},{4,... | collective-permute-start | bytes 884744 | tf_op jit(solution)/shard_map/ppermute | solution.py:520
  1.6 0.8 %broadcast_add_fusion = f32[40,144]{1,0:T(8,128)S(1)} fusion(f32[144]{0:T(256)} %param.15, f32[40]{0:T(128)} %param.14), kind=kLoop, calls=%fused_computation.30 | loop fusion | flops 5760 | bytes 23776 | tf_op jit(solution)/shard_map/add | solution.py:549
  2.3 0.9 %slice.20 = f32[136,144]{1,0:T(8,128)S(1)} slice(f32[144,144]{1,0:T(8,128)} %param.12), slice={[8:144], [0:144]} | slice | bytes 156672 | tf_op jit(solution)/shard_map/slice | solution.py:547
  3.3 0.7 slice.21
  4.0 0.8 %pad_slice_fusion.1 = (f32[40,48]{0,1:T(8,128)S(1)}, f32[40,48]{0,1:T(8,128)S(1)}) fusion(f32[40,40]{0,1:T(8,128)} %bitcast.10), kind=kLoop, calls=%fused_computation.22 | loop fusion | bytes 21760 | tf_op jit(solution)/shard_map/slice | solution.py:542
  4.8 0.1 fusion.3
  4.9 0.1 copy.14.refs_8_.refs_11_
  5.0 0.1 reshape.6
  5.1 0.1 pad.36.clone
  5.2 0.1 pad_maximum_fusion
  5.3 0.9 %fusion = (bf16[80,80]{0,1:T(8,128)(2,1)S(1)}, bf16[80,80]{0,1:T(8,128)(2,1)S(1)}) fusion(f32[40,40]{1,0:T(8,128)} %param.11), kind=kLoop, calls=%fused_computation.10 | loop fusion | flops 57600 | bytes 32000 | tf_op jit(solution)/shard_map/convert.10
  6.2 0.1 copy.13.refs_6_.refs_9_
  6.3 0.0 copy-done.3
  6.3 0.1 broadcast_in_dim.4.refs_0_
  6.4 0.3 shard_map.84
  6.7 0.1 pad_add_fusion.refs_0_
  6.8 0.0 copy-done.2
  6.8 0.1 fusion.1
  6.9 2.2 %collective-permute-done.refs_2_ = f32[24,24,128]{2,1,0:T(8,128)S(1)} collective-permute-done((f32[24,24,128]{2,1,0:T(8,128)}, f32[24,24,128]{2,1,0:T(8,128)S(1)}, u32[]{:S(2)}, u32[]{:S(2)}) %collective-permute-start) | collective-permute-done | bytes 294944 | tf_op jit(solution)/shard_map/ppermute | solution.py:520
  9.0 0.0 copy-done
  9.0 0.0 copy-done.1
  9.0 0.6 shard_map.82
  9.6 1.6 %collective-permute-start.1 = (f32[72,8,128]{2,1,0:T(8,128)S(1)}, f32[72,8,128]{2,1,0:T(8,128)S(1)}, u32[]{:S(2)}, u32[]{:S(2)}) collective-permute-start(f32[72,8,128]{2,1,0:T(8,128)S(1)} %get-tuple-element.30), channel_id=1, source_target_pairs={{0,4},{4,0},{8,12},{12,8},{1,5},{5,1},{9,13},{13,9},{2,6},{6,2},{1... | collective-permute-start | bytes 884744 | tf_op jit(solution)/shard_map/ppermute | solution.py:29
  11.3 1.9 %collective-permute-start.2 = (f32[72,8,128]{2,1,0:T(8,128)S(1)}, f32[72,8,128]{2,1,0:T(8,128)S(1)}, u32[]{:S(2)}, u32[]{:S(2)}) collective-permute-start(f32[72,8,128]{2,1,0:T(8,128)S(1)} %get-tuple-element.31), channel_id=1, source_target_pairs={{0,0},{4,8},{8,4},{12,12},{1,1},{5,9},{9,5},{13,13},{2,2},{6,10},{... | collective-permute-start | bytes 884744 | tf_op jit(solution)/shard_map/ppermute | solution.py:29
  13.2 0.1 pad_maximum_fusion.2.refs_7_.refs_10_
  13.3 4.3 %collective-permute-done.1.refs_4_ = f32[72,8,128]{2,1,0:T(8,128)S(1)} collective-permute-done((f32[72,8,128]{2,1,0:T(8,128)S(1)}, f32[72,8,128]{2,1,0:T(8,128)S(1)}, u32[]{:S(2)}, u32[]{:S(2)}) %collective-permute-start.1) | collective-permute-done | bytes 294944 | tf_op jit(solution)/shard_map/ppermute | solution.py:29
  17.6 3.2 %collective-permute-done.2.refs_5_ = f32[72,8,128]{2,1,0:T(8,128)S(1)} collective-permute-done((f32[72,8,128]{2,1,0:T(8,128)S(1)}, f32[72,8,128]{2,1,0:T(8,128)S(1)}, u32[]{:S(2)}, u32[]{:S(2)}) %collective-permute-start.2) | collective-permute-done | bytes 294944 | tf_op jit(solution)/shard_map/ppermute | solution.py:29
  20.8 1.4 %shard_map.83 = (f32[1920,128]{1,0:T(8,128)S(1)}, f32[960,128]{1,0:T(8,128)S(1)}, f32[200,128]{1,0:T(8,128)S(1)}, f32[200,128]{1,0:T(8,128)S(1)}) custom-call(s32[3]{0:T(128)S(1)} %pad_add_fusion.refs_0_, f32[24,24,128]{2,1,0:T(8,128)S(1)} %copy-done, f32[24,24,128]{2,1,0:T(8,128)S(1)} %collective-permute-done.refs_2_, f32[24,24,128]{2,1,0:T(8,128)S(1)} %copy-done.1, ...), custom_call_target="tpu_custom_call" | custom-call | tf_op jit(solution)/shard_map/pallas_call | solution.py:42
  22.2 0.1 collective-permute-start.3
  22.3 1.6 %collective-permute-start.4 = (f32[200,128]{1,0:T(8,128)S(1)}, f32[200,128]{1,0:T(8,128)S(1)}, u32[]{:S(2)}, u32[]{:S(2)}) collective-permute-start(f32[200,128]{1,0:T(8,128)S(1)} %get-tuple-element.34), channel_id=1, source_target_pairs={{0,3},{1,2},{2,1},{3,0},{4,7},{5,6},{6,5},{7,4},{8,11},{9,10},{10,... | collective-permute-start | bytes 307208 | tf_op jit(solution)/shard_map/ppermute | solution.py:29
  23.9 0.1 pad_maximum_fusion.5.refs_9_.refs_12_
  24.0 0.0 collective-permute-done.3.refs_2_
  24.0 2.9 %collective-permute-done.4.refs_3_ = f32[200,128]{1,0:T(8,128)S(1)} collective-permute-done((f32[200,128]{1,0:T(8,128)S(1)}, f32[200,128]{1,0:T(8,128)S(1)}, u32[]{:S(2)}, u32[]{:S(2)}) %collective-permute-start.4) | collective-permute-done | bytes 102432 | tf_op jit(solution)/shard_map/ppermute | solution.py:29
  26.9 6.3 %shard_map.85 = (f32[1920,256]{1,0:T(8,128)S(1)}, f32[1920,256]{1,0:T(8,128)S(1)}, f32[160,128]{1,0:T(8,128)S(1)}, f32[280,128]{1,0:T(8,128)S(1)}, f32[280,128]{1,0:T(8,128)S(1)}) custom-call(s32[3]{0:T(128)S(1)} %pad_add_fusion.refs_0_, f32[1920,128]{1,0:T(8,128)S(1)} %get-tuple-element.32.refs_1_, f32[200,128]{1,0:T(8,128)S(1)} %collective-permute-done.3.refs_2_, ...), custom_call_target="tpu_custom_call" | custom-call | tf_op jit(solution)/shard_map/pallas_call | solution.py:42
  33.2 0.5 collective-permute-start.5
  33.7 0.7 collective-permute-start.6
  34.3 1.6 %collective-permute-start.9 = (f32[960,128]{1,0:T(8,128)S(1)}, f32[960,128]{1,0:T(8,128)S(1)}, u32[]{:S(2)}, u32[]{:S(2)}) collective-permute-start(f32[960,128]{1,0:T(8,128)S(1)} %get-tuple-element.46.refs_1_), channel_id=1, source_target_pairs={{16,0},{0,16},{17,1},{1,17},{18,2},{2,18},{19,3},{3,19},{20,4},{4,... | collective-permute-start | bytes 1474568 | tf_op jit(solution)/shard_map/ppermute | solution.py:520
  35.9 0.0 collective-permute-done.5.refs_2_
  35.9 0.0 collective-permute-done.6.refs_3_
  35.9 1.9 %shard_map.86 = (f32[1920,128]{1,0:T(8,128)S(1)}, f32[1920,128]{1,0:T(8,128)S(1)}, f32[936,128]{1,0:T(8,128)S(1)}, f32[936,128]{1,0:T(8,128)S(1)}) custom-call(s32[3]{0:T(128)S(1)} %pad_add_fusion.refs_0_, f32[1920,256]{1,0:T(8,128)S(1)} %get-tuple-element.38.refs_1_, f32[280,128]{1,0:T(8,128)S(1)} %collective-permute-done.5.refs_2_, ...), custom_call_target="tpu_custom_call" | custom-call | tf_op jit(solution)/shard_map/pallas_call | solution.py:42
  37.8 0.1 collective-permute-start.7
  37.9 2.4 %collective-permute-start.8 = (f32[936,128]{1,0:T(8,128)S(1)}, f32[936,128]{1,0:T(8,128)S(1)}, u32[]{:S(2)}, u32[]{:S(2)}) collective-permute-start(f32[936,128]{1,0:T(8,128)S(1)} %get-tuple-element.44), channel_id=1, source_target_pairs={{0,0},{4,8},{8,4},{12,12},{1,1},{5,9},{9,5},{13,13},{2,2},{6,10},{... | collective-permute-start | bytes 1437704 | tf_op jit(solution)/shard_map/ppermute | solution.py:29
  40.3 0.6 collective-permute-start.10
  40.9 7.4 %collective-permute-done.10.refs_4_ = f32[160,128]{1,0:T(8,128)S(1)} collective-permute-done((f32[160,128]{1,0:T(8,128)S(1)}, f32[160,128]{1,0:T(8,128)S(1)}, u32[]{:S(2)}, u32[]{:S(2)}) %collective-permute-start.10) | collective-permute-done | bytes 81952 | tf_op jit(solution)/shard_map/ppermute | solution.py:520
  48.3 0.0 collective-permute-done.9.refs_2_
  48.3 2.0 %shard_map.87.refs_6_ = f32[1920,256]{1,0:T(8,128)S(1)} custom-call(s32[3]{0:T(128)S(1)} %pad_add_fusion.refs_0_, f32[960,128]{1,0:T(8,128)S(1)} %get-tuple-element.46.refs_1_, f32[960,128]{1,0:T(8,128)S(1)} %collective-permute-done.9.refs_2_, f32[160,128]{1,0:T(8,128)S(1)} %get-tuple-element.47.refs_3_, f32[160,128]{1,0:T(8,128)S(1)} %collective-permute-done.10.refs_4_, ...), custom_call_target="tpu_custom_call" | custom-call | tf_op jit(solution)/shard_map/pallas_call | solution.py:42
  50.4 0.0 collective-permute-done.7.refs_3_
  50.4 0.0 collective-permute-done.8.refs_4_
  50.4 7.8 %shard_map.88 = (f32[960,128]{1,0:T(8,128)S(1)}, f32[576,128]{1,0:T(8,128)S(1)}, f32[80,128]{1,0:T(8,128)S(1)}, f32[80,128]{1,0:T(8,128)S(1)}) custom-call(s32[3]{0:T(128)S(1)} %pad_add_fusion.refs_0_, f32[1920,128]{1,0:T(8,128)S(1)} %get-tuple-element.41.refs_1_, f32[1920,128]{1,0:T(8,128)S(1)} %get-tuple-element.42.refs_2_, ...), custom_call_target="tpu_custom_call" | custom-call | tf_op jit(solution)/shard_map/pallas_call | solution.py:42
  58.2 3.1 %collective-permute-start.11 = (f32[80,128]{1,0:T(8,128)S(1)}, f32[80,128]{1,0:T(8,128)S(1)}, u32[]{:S(2)}, u32[]{:S(2)}) collective-permute-start(f32[80,128]{1,0:T(8,128)S(1)} %get-tuple-element.49), channel_id=1, source_target_pairs={{0,1},{1,0},{2,3},{3,2},{4,5},{5,4},{6,7},{7,6},{8,9},{9,8},{10,11... | collective-permute-start | bytes 122888 | tf_op jit(solution)/shard_map/ppermute | solution.py:29
  61.4 0.9 %collective-permute-start.12 = (f32[80,128]{1,0:T(8,128)S(1)}, f32[80,128]{1,0:T(8,128)S(1)}, u32[]{:S(2)}, u32[]{:S(2)}) collective-permute-start(f32[80,128]{1,0:T(8,128)S(1)} %get-tuple-element.50), channel_id=1, source_target_pairs={{0,3},{1,2},{2,1},{3,0},{4,7},{5,6},{6,5},{7,4},{8,11},{9,10},{10,... | collective-permute-start | bytes 122888 | tf_op jit(solution)/shard_map/ppermute | solution.py:29
  62.2 0.0 collective-permute-done.11.refs_2_
  62.2 2.7 %collective-permute-done.12.refs_3_ = f32[80,128]{1,0:T(8,128)S(1)} collective-permute-done((f32[80,128]{1,0:T(8,128)S(1)}, f32[80,128]{1,0:T(8,128)S(1)}, u32[]{:S(2)}, u32[]{:S(2)}) %collective-permute-start.12) | collective-permute-done | bytes 40992 | tf_op jit(solution)/shard_map/ppermute | solution.py:29
  65.0 0.9 %shard_map.89 = (f32[960,128]{1,0:T(8,128)S(1)}, f32[192,128]{1,0:T(8,128)S(1)}, f32[192,128]{1,0:T(8,128)S(1)}) custom-call(s32[3]{0:T(128)S(1)} %pad_add_fusion.refs_0_, f32[960,128]{1,0:T(8,128)S(1)} %get-tuple-element.48.refs_1_, f32[80,128]{1,0:T(8,128)S(1)} %collective-permute-done.11.refs_2_, f32[80,128]{1,0:T(8,128)S(1)} %collective-permute-done.12.refs_3_), custom_call_target="tpu_custom_call" | custom-call | tf_op jit(solution)/shard_map/pallas_call | solution.py:42
  65.9 0.1 collective-permute-start.13
  65.9 2.2 %collective-permute-start.14 = (f32[192,128]{1,0:T(8,128)S(1)}, f32[192,128]{1,0:T(8,128)S(1)}, u32[]{:S(2)}, u32[]{:S(2)}) collective-permute-start(f32[192,128]{1,0:T(8,128)S(1)} %get-tuple-element.53), channel_id=1, source_target_pairs={{0,0},{4,8},{8,4},{12,12},{1,1},{5,9},{9,5},{13,13},{2,2},{6,10},{... | collective-permute-start | bytes 294920 | tf_op jit(solution)/shard_map/ppermute | solution.py:29
  68.1 2.6 %collective-permute-done.13.refs_2_ = f32[192,128]{1,0:T(8,128)S(1)} collective-permute-done((f32[192,128]{1,0:T(8,128)S(1)}, f32[192,128]{1,0:T(8,128)S(1)}, u32[]{:S(2)}, u32[]{:S(2)}) %collective-permute-start.13) | collective-permute-done | bytes 98336 | tf_op jit(solution)/shard_map/ppermute | solution.py:29
  70.7 1.9 %collective-permute-done.14.refs_3_ = f32[192,128]{1,0:T(8,128)S(1)} collective-permute-done((f32[192,128]{1,0:T(8,128)S(1)}, f32[192,128]{1,0:T(8,128)S(1)}, u32[]{:S(2)}, u32[]{:S(2)}) %collective-permute-start.14) | collective-permute-done | bytes 98336 | tf_op jit(solution)/shard_map/ppermute | solution.py:29
  72.7 1.3 %shard_map.90 = f32[24,24,128]{2,1,0:T(8,128)} custom-call(s32[3]{0:T(128)S(1)} %pad_add_fusion.refs_0_, f32[960,128]{1,0:T(8,128)S(1)} %get-tuple-element.51.refs_1_, f32[192,128]{1,0:T(8,128)S(1)} %collective-permute-done.13.refs_2_, f32[192,128]{1,0:T(8,128)S(1)} %collective-permute-done.14.refs_3_, f32[576,128]{1,0:T(8,128)S(1)} %get-tuple-element.54.refs_4_), custom_call_target="tpu_custom_call" | custom-call | tf_op jit(solution)/shard_map/pallas_call | solution.py:42
  (9 shorter events, 0.1 us)
Async XLA Ops:
  0.0 9.0 %copy-start = (f32[24,24,128]{2,1,0:T(8,128)S(1)}, f32[24,24,128]{2,1,0:T(8,128)}, u32[]{:S(2)}) copy-start(f32[24,24,128]{2,1,0:T(8,128)} %refs_1_.3) | copy-start | bytes 884740
  0.0 6.8 %copy-start.2 = (f32[40,40]{1,0:T(8,128)S(1)}, f32[40,40]{1,0:T(8,128)}, u32[]{:S(2)}) copy-start(f32[40,40]{1,0:T(8,128)} %param.11) | copy-start | bytes 19204
  0.0 6.3 %copy-start.3 = (f32[40]{0:T(128)S(1)}, f32[40]{0:T(128)}, u32[]{:S(2)}) copy-start(f32[40]{0:T(128)} %param.13) | copy-start | bytes 484
  0.0 9.0 %copy-start.1 = (f32[24,24,128]{2,1,0:T(8,128)S(1)}, f32[24,24,128]{2,1,0:T(8,128)}, u32[]{:S(2)}) copy-start(f32[24,24,128]{2,1,0:T(8,128)} %refs_3_.3) | copy-start | bytes 884740
  0.0 9.0 %collective-permute-start = (f32[24,24,128]{2,1,0:T(8,128)}, f32[24,24,128]{2,1,0:T(8,128)S(1)}, u32[]{:S(2)}, u32[]{:S(2)}) collective-permute-start(f32[24,24,128]{2,1,0:T(8,128)} %refs_1_.3), channel_id=1, source_target_pairs={{16,0},{0,16},{17,1},{1,17},{18,2},{2,18},{19,3},{3,19},{20,4},{4,... | collective-permute-start | bytes 884744 | tf_op jit(solution)/shard_map/ppermute | solution.py:520
  9.6 8.0 %collective-permute-start.1 = (f32[72,8,128]{2,1,0:T(8,128)S(1)}, f32[72,8,128]{2,1,0:T(8,128)S(1)}, u32[]{:S(2)}, u32[]{:S(2)}) collective-permute-start(f32[72,8,128]{2,1,0:T(8,128)S(1)} %get-tuple-element.30), channel_id=1, source_target_pairs={{0,4},{4,0},{8,12},{12,8},{1,5},{5,1},{9,13},{13,9},{2,6},{6,2},{1... | collective-permute-start | bytes 884744 | tf_op jit(solution)/shard_map/ppermute | solution.py:29
  11.3 9.5 %collective-permute-start.2 = (f32[72,8,128]{2,1,0:T(8,128)S(1)}, f32[72,8,128]{2,1,0:T(8,128)S(1)}, u32[]{:S(2)}, u32[]{:S(2)}) collective-permute-start(f32[72,8,128]{2,1,0:T(8,128)S(1)} %get-tuple-element.31), channel_id=1, source_target_pairs={{0,0},{4,8},{8,4},{12,12},{1,1},{5,9},{9,5},{13,13},{2,2},{6,10},{... | collective-permute-start | bytes 884744 | tf_op jit(solution)/shard_map/ppermute | solution.py:29
  22.2 1.8 %collective-permute-start.3 = (f32[200,128]{1,0:T(8,128)S(1)}, f32[200,128]{1,0:T(8,128)S(1)}, u32[]{:S(2)}, u32[]{:S(2)}) collective-permute-start(f32[200,128]{1,0:T(8,128)S(1)} %get-tuple-element.33), channel_id=1, source_target_pairs={{0,1},{1,0},{2,3},{3,2},{4,5},{5,4},{6,7},{7,6},{8,9},{9,8},{10,11... | collective-permute-start | bytes 307208 | tf_op jit(solution)/shard_map/ppermute | solution.py:29
  22.3 4.6 %collective-permute-start.4 = (f32[200,128]{1,0:T(8,128)S(1)}, f32[200,128]{1,0:T(8,128)S(1)}, u32[]{:S(2)}, u32[]{:S(2)}) collective-permute-start(f32[200,128]{1,0:T(8,128)S(1)} %get-tuple-element.34), channel_id=1, source_target_pairs={{0,3},{1,2},{2,1},{3,0},{4,7},{5,6},{6,5},{7,4},{8,11},{9,10},{10,... | collective-permute-start | bytes 307208 | tf_op jit(solution)/shard_map/ppermute | solution.py:29
  33.2 2.7 %collective-permute-start.5 = (f32[280,128]{1,0:T(8,128)S(1)}, f32[280,128]{1,0:T(8,128)S(1)}, u32[]{:S(2)}, u32[]{:S(2)}) collective-permute-start(f32[280,128]{1,0:T(8,128)S(1)} %get-tuple-element.39), channel_id=1, source_target_pairs={{0,1},{1,0},{2,3},{3,2},{4,5},{5,4},{6,7},{7,6},{8,9},{9,8},{10,11... | collective-permute-start | bytes 430088 | tf_op jit(solution)/shard_map/ppermute | solution.py:29
  33.7 2.2 %collective-permute-start.6 = (f32[280,128]{1,0:T(8,128)S(1)}, f32[280,128]{1,0:T(8,128)S(1)}, u32[]{:S(2)}, u32[]{:S(2)}) collective-permute-start(f32[280,128]{1,0:T(8,128)S(1)} %get-tuple-element.40), channel_id=1, source_target_pairs={{0,0},{1,2},{2,1},{3,3},{4,4},{5,6},{6,5},{7,7},{8,8},{9,10},{10,9... | collective-permute-start | bytes 430088 | tf_op jit(solution)/shard_map/ppermute | solution.py:29
  34.3 14.0 %collective-permute-start.9 = (f32[960,128]{1,0:T(8,128)S(1)}, f32[960,128]{1,0:T(8,128)S(1)}, u32[]{:S(2)}, u32[]{:S(2)}) collective-permute-start(f32[960,128]{1,0:T(8,128)S(1)} %get-tuple-element.46.refs_1_), channel_id=1, source_target_pairs={{16,0},{0,16},{17,1},{1,17},{18,2},{2,18},{19,3},{3,19},{20,4},{4,... | collective-permute-start | bytes 1474568 | tf_op jit(solution)/shard_map/ppermute | solution.py:520
  37.8 12.5 %collective-permute-start.7 = (f32[936,128]{1,0:T(8,128)S(1)}, f32[936,128]{1,0:T(8,128)S(1)}, u32[]{:S(2)}, u32[]{:S(2)}) collective-permute-start(f32[936,128]{1,0:T(8,128)S(1)} %get-tuple-element.43.refs_5_), channel_id=1, source_target_pairs={{0,4},{4,0},{8,12},{12,8},{1,5},{5,1},{9,13},{13,9},{2,6},{6,2},{1... | collective-permute-start | bytes 1437704 | tf_op jit(solution)/shard_map/ppermute | solution.py:29
  37.9 12.5 %collective-permute-start.8 = (f32[936,128]{1,0:T(8,128)S(1)}, f32[936,128]{1,0:T(8,128)S(1)}, u32[]{:S(2)}, u32[]{:S(2)}) collective-permute-start(f32[936,128]{1,0:T(8,128)S(1)} %get-tuple-element.44), channel_id=1, source_target_pairs={{0,0},{4,8},{8,4},{12,12},{1,1},{5,9},{9,5},{13,13},{2,2},{6,10},{... | collective-permute-start | bytes 1437704 | tf_op jit(solution)/shard_map/ppermute | solution.py:29
  40.3 8.0 %collective-permute-start.10 = (f32[160,128]{1,0:T(8,128)S(1)}, f32[160,128]{1,0:T(8,128)S(1)}, u32[]{:S(2)}, u32[]{:S(2)}) collective-permute-start(f32[160,128]{1,0:T(8,128)S(1)} %get-tuple-element.47.refs_3_), channel_id=1, source_target_pairs={{16,0},{0,16},{17,1},{1,17},{18,2},{2,18},{19,3},{3,19},{20,4},{4,... | collective-permute-start | bytes 245768 | tf_op jit(solution)/shard_map/ppermute | solution.py:520
  58.2 4.0 %collective-permute-start.11 = (f32[80,128]{1,0:T(8,128)S(1)}, f32[80,128]{1,0:T(8,128)S(1)}, u32[]{:S(2)}, u32[]{:S(2)}) collective-permute-start(f32[80,128]{1,0:T(8,128)S(1)} %get-tuple-element.49), channel_id=1, source_target_pairs={{0,1},{1,0},{2,3},{3,2},{4,5},{5,4},{6,7},{7,6},{8,9},{9,8},{10,11... | collective-permute-start | bytes 122888 | tf_op jit(solution)/shard_map/ppermute | solution.py:29
  61.4 3.6 %collective-permute-start.12 = (f32[80,128]{1,0:T(8,128)S(1)}, f32[80,128]{1,0:T(8,128)S(1)}, u32[]{:S(2)}, u32[]{:S(2)}) collective-permute-start(f32[80,128]{1,0:T(8,128)S(1)} %get-tuple-element.50), channel_id=1, source_target_pairs={{0,3},{1,2},{2,1},{3,0},{4,7},{5,6},{6,5},{7,4},{8,11},{9,10},{10,... | collective-permute-start | bytes 122888 | tf_op jit(solution)/shard_map/ppermute | solution.py:29
  65.9 4.9 %collective-permute-start.13 = (f32[192,128]{1,0:T(8,128)S(1)}, f32[192,128]{1,0:T(8,128)S(1)}, u32[]{:S(2)}, u32[]{:S(2)}) collective-permute-start(f32[192,128]{1,0:T(8,128)S(1)} %get-tuple-element.52), channel_id=1, source_target_pairs={{0,4},{4,0},{8,12},{12,8},{1,5},{5,1},{9,13},{13,9},{2,6},{6,2},{1... | collective-permute-start | bytes 294920 | tf_op jit(solution)/shard_map/ppermute | solution.py:29
  65.9 6.7 %collective-permute-start.14 = (f32[192,128]{1,0:T(8,128)S(1)}, f32[192,128]{1,0:T(8,128)S(1)}, u32[]{:S(2)}, u32[]{:S(2)}) collective-permute-start(f32[192,128]{1,0:T(8,128)S(1)} %get-tuple-element.53), channel_id=1, source_target_pairs={{0,0},{4,8},{8,4},{12,12},{1,1},{5,9},{9,5},{13,13},{2,2},{6,10},{... | collective-permute-start | bytes 294920 | tf_op jit(solution)/shard_map/ppermute | solution.py:29

commit v4 on v3

--- a/solution.py
+++ b/solution.py
@@ -29,15 +29,19 @@
     return lax.ppermute(one, axis, pairs(count, 0, around)), lax.ppermute(two, axis, pairs(count, 1, around))
 
 
-def call(kernel, outs, *args, scratch=(), smem=1, after=()):
+class Place:
+    def __getitem__(self, axis):
+        return lax.axis_index(("gx", "gy", "gz")[axis])
+
+
+def call(kernel, outs, *args, scratch=(), after=()):
     vmem = pl.BlockSpec(memory_space=pltpu.VMEM)
-    specs = [pl.BlockSpec(memory_space=pltpu.SMEM)] * smem + [vmem] * (len(args) - smem)
-    specs += [pl.BlockSpec(memory_space=pl.ANY)] * len(after)
+    specs = [vmem] * len(args) + [pl.BlockSpec(memory_space=pl.ANY)] * len(after)
     used = len(args)
     held = sum(math.prod(s.shape) * 4 for s in scratch)
 
     def body(*refs):
-        kernel(*refs[:used], *refs[used + len(after) :])
+        kernel(Place(), *refs[:used], *refs[used + len(after) :])
 
     return pl.pallas_call(
         body,
@@ -226,7 +230,7 @@
     def times_x(value, factor):
         value = dot(x_on[...], stack_rows(value))
         value = jnp.concatenate([value[i * modes : (i + 1) * modes] * factor for i in range(value.shape[0] // modes)], axis=0)
-        return dot(x_back[...], stack_rows(value))[:back]
+        return dot(x_back[:back], stack_rows(value))
 
     def middle(h, carry):
         q = 2 * h
@@ -357,7 +361,7 @@
             out[rows_of((k * cx + x) * ey, ey), :] = value + 5.0
             return carry
 
-        lax.fori_loop(0, cx, plane, 0, unroll=4)
+        lax.fori_loop(0, cx, plane, 0, unroll=12)
 
 
 def second_solve(info, core_in, rest_in, got_one, got_two, block, coef, z_on, z_back, y_on, y_back, x_on, x_back, recip, u, first, one, two, s0, s1, core_v, rest_v, far, *, ny, nz, ov, ey, cx, cz):
@@ -394,7 +398,7 @@
             out[rows_of(x * room + ey, ov), :] = jnp.where(side.has_above, high[ov:], 0.0)
         return carry
 
-    lax.fori_loop(0, count, gather, 0, unroll=8)
+    lax.fori_loop(0, count, gather, 0, unroll=16)
     single = odd_group(count, halo)
     near = lane_of((single, LANES))
 
@@ -449,7 +453,7 @@
         first[rows_of(x * cy, cy), :] = core_v[rows_of(x * room + 2 * ov, cy), :]
         return carry
 
-    lax.fori_loop(0, cx, keep, 0, unroll=8)
+    lax.fori_loop(0, cx, keep, 0, unroll=24)
 
 
 def last_sum_z(info, u, got_one, got_two, v, one, two, *, ny, nz, ov, ey, cx, cz):
@@ -483,7 +487,7 @@
     lax.fori_loop(0, cx, add, 0, unroll=24)
 
 
-def make_tables(eigen_x, rest, zt, out, z_on, z_back, *, ov, ez):
+def make_tables(info, eigen_x, rest, zt, out, z_on, z_back, *, ov, ez):
     def row(q, carry):
         out[q] = 1.0 / (eigen_x[...] + rest[pl.ds(q, 1), :])
         return carry
@@ -531,9 +535,8 @@
     ex, ey, ez = basis_x.shape[0], basis_y.shape[0], basis_z.shape[0]
     ov = (ex - cx) // 2
     nx, ny, nz = lax.axis_size("gx"), lax.axis_size("gy"), lax.axis_size("gz")
-    ix, iy, iz = lax.axis_index("gx"), lax.axis_index("gy"), lax.axis_index("gz")
+    ix = lax.axis_index("gx")
     count = nx * cx
-    info = jnp.stack([ix, iy, iz]).astype(jnp.int32)
     w, tall, halo = 2 * ov + 1, 2 * ov, 2 * (ov + 1)
     at = dict(ov=ov, ey=ey, cz=cz)
 
@@ -550,40 +553,40 @@
     rest = jnp.concatenate([rest[:, :LANES], rest[:, LANES:].reshape(-1, LANES)], axis=0)
     recip, z_on, z_back = call(
         functools.partial(make_tables, ov=ov, ez=ez), [(rest.shape[0], ex, LANES), (4 * LANES, RING, BF16), (4 * LANES, RING, BF16)],
-        jnp.broadcast_to(eigen_x[:, None], (ex, LANES)), rest, zt, smem=0,
+        jnp.broadcast_to(eigen_x[:, None], (ex, LANES)), rest, zt,
     )
     tables = (z_on, z_back, columns(double.T), columns(double), columns(table), columns(table.T), recip)
 
-    slabs = call(functools.partial(first_slabs, ny=ny, ov=ov), [(count + cx, ov, cz)] * 2, info, *f_parts, reaction)
+    slabs = call(functools.partial(first_slabs, ny=ny, ov=ov), [(count + cx, ov, cz)] * 2, *f_parts, reaction)
     got = swap(*slabs, "gy")
     edge = group_of(cx, ov) * ey
     small = (group_of(count, ov) * ey + edge, LANES)
     f, c, *slabs = call(
-        functools.partial(second_slabs, ny=ny, nz=nz, ov=ov), [(count * ey, cz), (cx * ey, cz), small, small], info, *f_parts, reaction, *got
+        functools.partial(second_slabs, ny=ny, nz=nz, ov=ov), [(count * ey, cz), (cx * ey, cz), small, small], *f_parts, reaction, *got
     )
     got = swap(*slabs, "gz", around=True)
     c_parts = gather_x(c)
     state = [pltpu.VMEM((count * ey, LANES), F32), pltpu.VMEM((ey // 8 * count, LANES), F32)]
     small = (group_of(count, w) * ey, LANES)
     u, block, rest, *slabs = call(
-        functools.partial(first_solve, nz=nz, cx=cx, **at), [(count * ey, RING)] * 2 + [(2 * edge, LANES), small, small], info, f, *got, *tables, scratch=state
+        functools.partial(first_solve, nz=nz, cx=cx, **at), [(count * ey, RING)] * 2 + [(2 * edge, LANES), small, small], f, *got, *tables, scratch=state
     )
     got = swap(*slabs, "gz")
     c_parts += gather_x(rest)
     tall_rows = (count * tall + group_of(count, halo) * tall + count + odd_group(count, halo), LANES)
-    core, rest, *slabs = call(functools.partial(sum_z, ny=ny, nz=nz, **at), [(count * ey, LANES)] * 2 + [tall_rows, tall_rows], info, u, *got)
+    core, rest, *slabs = call(functools.partial(sum_z, ny=ny, nz=nz, **at), [(count * ey, LANES)] * 2 + [tall_rows, tall_rows], u, *got)
     got = swap(*slabs, "gy")
-    c = call(functools.partial(coefficients, nz=nz, ov=ov, ey=ey), [(count * ey, RING)], info, *c_parts, after=slabs[:1])[0]
+    c = call(functools.partial(coefficients, nz=nz, ov=ov, ey=ey), [(count * ey, RING)], *c_parts, after=slabs[:1])[0]
     small = (group_of(cx, ov) * ey, LANES)
     state += [pltpu.VMEM((count * (ey + 2 * ov), LANES), F32)] * 2 + [pltpu.VMEM((cx * ey, LANES), F32)]
     u, first, *slabs = call(
         functools.partial(second_solve, ny=ny, nz=nz, cx=cx, **at),
-        [(cx * ey, LANES), (cx * cy, LANES), small, small], info, core, rest, *got, block, c, *tables, scratch=state,
+        [(cx * ey, LANES), (cx * cy, LANES), small, small], core, rest, *got, block, c, *tables, scratch=state,
     )
     got = swap(*slabs, "gz", around=True)
-    v, *slabs = call(functools.partial(last_sum_z, ny=ny, nz=nz, cx=cx, **at), [(cx * ey, LANES)] + [(cx * ov, LANES)] * 2, info, u, *got)
+    v, *slabs = call(functools.partial(last_sum_z, ny=ny, nz=nz, cx=cx, **at), [(cx * ey, LANES)] + [(cx * ov, LANES)] * 2, u, *got)
     got = swap(*slabs, "gy")
-    return call(functools.partial(last_sum_y, ny=ny, ov=ov, ey=ey, cx=cx), [(cx, cy, cz)], info, v, *got, first)[0]
+    return call(functools.partial(last_sum_y, ny=ny, ov=ov, ey=ey, cx=cx), [(cx, cy, cz)], v, *got, first)[0]
 
 
 def solution(mesh):

time: 74.4 us -> 70.5 us (0.948)
  Pallas kernels: 22.6 us -> 17.5 us
  waiting for transfers between devices: 27.3 us -> 28.1 us
    pallas_call x9, Pallas kernels: 22.6 us -> 17.5 us  [call(): pl.pallas_call(body, out_shape=[jax.ShapeDtypeStruct(s[:2], BF16) if BF16...]
  transfers between devices with their start and end apart: 15 -> 15, of which waited for: 8 -> 9; matrix products, arithmetic and copies ran while one was open for 7% -> 7% of each run, Pallas kernels for 6% -> 4%
where the time goes in v4:
time: 70.5 us; the launch traced here: 70 us
  waiting for transfers between devices  28.1 us (40%)
  starting transfers between devices  19.1 us (27%)
  Pallas kernels  17.5 us (25%)
  local copies, waits for them, and re-layouts  2.87 us (4%)
  other arithmetic  2.14 us (3%)
    pallas_call x9, Pallas kernels, call(): pl.pallas_call(body, out_shape=[jax.ShapeDtypeStruct(s[:2], BF16) if BF16...  17.5 us
    ppermute x6, waiting for transfers between devices, swap(): lax.ppermute(two, axis, pairs(count, 1, around))  10.9 us
    ppermute x3, waiting for transfers between devices, gather_x(): lax.ppermute(block, 'gx', [((i + shift) % count, i) for i in range(count)])  10.2 us
    ppermute x6, starting transfers between devices, swap(): lax.ppermute(two, axis, pairs(count, 1, around))  9.61 us
    ppermute x6, waiting for transfers between devices, swap(): lax.ppermute(one, axis, pairs(count, 0, around))  6.92 us
    ppermute x6, starting transfers between devices, swap(): lax.ppermute(one, axis, pairs(count, 0, around))  5.81 us
    ppermute x3, starting transfers between devices, gather_x(): lax.ppermute(block, 'gx', [((i + shift) % count, i) for i in range(count)])  3.7 us
  transfers between devices with their start and end apart: 15, of which 9 were waited for; matrix products, arithmetic and copies ran while one was open for 7% of the time, Pallas kernels for 4%

profile of v4, /device:TPU:16, one launch (start us, length us, event | category | flops | bytes accessed | tf_op | source)
XLA Modules:
  0.0 70.0 jit_solution(15856268236072510357)
XLA Ops:
  0.0 0.0 copy-start
  0.0 0.0 copy-start.2
  0.0 0.0 copy-start.3
  0.0 0.0 copy-start.1
  0.0 1.6 %collective-permute-start = (f32[24,24,128]{2,1,0:T(8,128)}, f32[24,24,128]{2,1,0:T(8,128)S(1)}, u32[]{:S(2)}, u32[]{:S(2)}) collective-permute-start(f32[24,24,128]{2,1,0:T(8,128)} %refs_0_.3), channel_id=1, source_target_pairs={{16,0},{0,16},{17,1},{1,17},{18,2},{2,18},{19,3},{3,19},{20,4},{4,... | collective-permute-start | bytes 884744 | tf_op jit(solution)/shard_map/ppermute | solution.py:524
  1.6 0.8 %broadcast_add_fusion = f32[40,144]{1,0:T(8,128)S(1)} fusion(f32[144]{0:T(256)} %param.15, f32[40]{0:T(128)} %param.14), kind=kLoop, calls=%fused_computation.30 | loop fusion | flops 5760 | bytes 23776 | tf_op jit(solution)/shard_map/add | solution.py:552
  2.3 0.9 %slice.20 = f32[136,144]{1,0:T(8,128)S(1)} slice(f32[144,144]{1,0:T(8,128)} %param.12), slice={[8:144], [0:144]} | slice | bytes 156672 | tf_op jit(solution)/shard_map/slice | solution.py:550
  3.3 0.7 %slice.21 = f32[8,144]{1,0:T(8,128)S(1)} slice(f32[144,144]{1,0:T(8,128)} %param.12), slice={[0:8], [0:144]} | slice | bytes 9216 | tf_op jit(solution)/shard_map/slice | solution.py:550
  4.0 0.8 %pad_slice_fusion.1 = (f32[40,48]{0,1:T(8,128)S(1)}, f32[40,48]{0,1:T(8,128)S(1)}) fusion(f32[40,40]{0,1:T(8,128)} %bitcast.7), kind=kLoop, calls=%fused_computation.22 | loop fusion | bytes 21760 | tf_op jit(solution)/shard_map/slice | solution.py:545
  4.8 0.1 fusion.3
  4.9 0.1 copy.14.refs_7_.refs_10_
  5.0 0.1 reshape.6
  5.1 0.1 pad.36.clone
  5.2 0.1 pad_maximum_fusion
  5.3 0.9 %fusion = (bf16[80,80]{0,1:T(8,128)(2,1)S(1)}, bf16[80,80]{0,1:T(8,128)(2,1)S(1)}) fusion(f32[40,40]{1,0:T(8,128)} %param.11), kind=kLoop, calls=%fused_computation.10 | loop fusion | flops 57600 | bytes 32000 | tf_op jit(solution)/shard_map/convert.10
  6.2 0.1 copy.13.refs_5_.refs_8_
  6.3 0.0 copy-done.3
  6.3 0.1 broadcast_in_dim.4.refs_0_
  6.4 0.3 shard_map.84
  6.7 0.0 copy-done.2
  6.7 0.1 fusion.1
  6.8 2.2 %collective-permute-done.refs_1_ = f32[24,24,128]{2,1,0:T(8,128)S(1)} collective-permute-done((f32[24,24,128]{2,1,0:T(8,128)}, f32[24,24,128]{2,1,0:T(8,128)S(1)}, u32[]{:S(2)}, u32[]{:S(2)}) %collective-permute-start) | collective-permute-done | bytes 294944 | tf_op jit(solution)/shard_map/ppermute | solution.py:524
  9.0 0.0 copy-done
  9.0 0.0 copy-done.1
  9.1 1.6 %collective-permute-start.1 = (f32[72,8,128]{2,1,0:T(8,128)S(1)}, f32[72,8,128]{2,1,0:T(8,128)S(1)}, u32[]{:S(2)}, u32[]{:S(2)}) collective-permute-start(f32[72,8,128]{2,1,0:T(8,128)S(1)} %get-tuple-element.30), channel_id=1, source_target_pairs={{0,4},{4,0},{8,12},{12,8},{1,5},{5,1},{9,13},{13,9},{2,6},{6,2},{1... | collective-permute-start | bytes 884744 | tf_op jit(solution)/shard_map/ppermute | solution.py:29
  10.7 1.9 %collective-permute-start.2 = (f32[72,8,128]{2,1,0:T(8,128)S(1)}, f32[72,8,128]{2,1,0:T(8,128)S(1)}, u32[]{:S(2)}, u32[]{:S(2)}) collective-permute-start(f32[72,8,128]{2,1,0:T(8,128)S(1)} %get-tuple-element.31), channel_id=1, source_target_pairs={{0,0},{4,8},{8,4},{12,12},{1,1},{5,9},{9,5},{13,13},{2,2},{6,10},{... | collective-permute-start | bytes 884744 | tf_op jit(solution)/shard_map/ppermute | solution.py:29
  12.7 0.1 pad_maximum_fusion.2.refs_6_.refs_9_
  12.8 4.3 %collective-permute-done.1.refs_3_ = f32[72,8,128]{2,1,0:T(8,128)S(1)} collective-permute-done((f32[72,8,128]{2,1,0:T(8,128)S(1)}, f32[72,8,128]{2,1,0:T(8,128)S(1)}, u32[]{:S(2)}, u32[]{:S(2)}) %collective-permute-start.1) | collective-permute-done | bytes 294944 | tf_op jit(solution)/shard_map/ppermute | solution.py:29
  17.1 3.2 %collective-permute-done.2.refs_4_ = f32[72,8,128]{2,1,0:T(8,128)S(1)} collective-permute-done((f32[72,8,128]{2,1,0:T(8,128)S(1)}, f32[72,8,128]{2,1,0:T(8,128)S(1)}, u32[]{:S(2)}, u32[]{:S(2)}) %collective-permute-start.2) | collective-permute-done | bytes 294944 | tf_op jit(solution)/shard_map/ppermute | solution.py:29
  20.2 0.9 %shard_map.83 = (f32[1920,128]{1,0:T(8,128)S(1)}, f32[960,128]{1,0:T(8,128)S(1)}, f32[200,128]{1,0:T(8,128)S(1)}, f32[200,128]{1,0:T(8,128)S(1)}) custom-call(f32[24,24,128]{2,1,0:T(8,128)S(1)} %copy-done, f32[24,24,128]{2,1,0:T(8,128)S(1)} %collective-permute-done.refs_1_, f32[24,24,128]{2,1,0:T(8,128)S(1)} %copy-done.1, ...), custom_call_target="tpu_custom_call" | custom-call | tf_op jit(solution)/shard_map/pallas_call | solution.py:46
  21.1 0.1 collective-permute-start.3
  21.2 1.6 %collective-permute-start.4 = (f32[200,128]{1,0:T(8,128)S(1)}, f32[200,128]{1,0:T(8,128)S(1)}, u32[]{:S(2)}, u32[]{:S(2)}) collective-permute-start(f32[200,128]{1,0:T(8,128)S(1)} %get-tuple-element.34), channel_id=1, source_target_pairs={{0,3},{1,2},{2,1},{3,0},{4,7},{5,6},{6,5},{7,4},{8,11},{9,10},{10,... | collective-permute-start | bytes 307208 | tf_op jit(solution)/shard_map/ppermute | solution.py:29
  22.8 0.1 pad_maximum_fusion.5.refs_8_.refs_11_
  22.9 0.0 collective-permute-done.3.refs_1_
  22.9 2.9 %collective-permute-done.4.refs_2_ = f32[200,128]{1,0:T(8,128)S(1)} collective-permute-done((f32[200,128]{1,0:T(8,128)S(1)}, f32[200,128]{1,0:T(8,128)S(1)}, u32[]{:S(2)}, u32[]{:S(2)}) %collective-permute-start.4) | collective-permute-done | bytes 102432 | tf_op jit(solution)/shard_map/ppermute | solution.py:29
  25.8 5.7 %shard_map.85 = (f32[1920,256]{1,0:T(8,128)S(1)}, f32[1920,256]{1,0:T(8,128)S(1)}, f32[160,128]{1,0:T(8,128)S(1)}, f32[280,128]{1,0:T(8,128)S(1)}, f32[280,128]{1,0:T(8,128)S(1)}) custom-call(f32[1920,128]{1,0:T(8,128)S(1)} %get-tuple-element.32.refs_0_, f32[200,128]{1,0:T(8,128)S(1)} %collective-permute-done.3.refs_1_, ...), custom_call_target="tpu_custom_call" | custom-call | tf_op jit(solution)/shard_map/pallas_call | solution.py:46
  31.6 0.5 collective-permute-start.5
  32.1 0.7 collective-permute-start.6
  32.7 1.6 %collective-permute-start.9 = (f32[960,128]{1,0:T(8,128)S(1)}, f32[960,128]{1,0:T(8,128)S(1)}, u32[]{:S(2)}, u32[]{:S(2)}) collective-permute-start(f32[960,128]{1,0:T(8,128)S(1)} %get-tuple-element.46.refs_0_), channel_id=1, source_target_pairs={{16,0},{0,16},{17,1},{1,17},{18,2},{2,18},{19,3},{3,19},{20,4},{4,... | collective-permute-start | bytes 1474568 | tf_op jit(solution)/shard_map/ppermute | solution.py:524
  34.3 0.0 collective-permute-done.5.refs_1_
  34.3 0.0 collective-permute-done.6.refs_2_
  34.3 1.4 %shard_map.86 = (f32[1920,128]{1,0:T(8,128)S(1)}, f32[1920,128]{1,0:T(8,128)S(1)}, f32[936,128]{1,0:T(8,128)S(1)}, f32[936,128]{1,0:T(8,128)S(1)}) custom-call(f32[1920,256]{1,0:T(8,128)S(1)} %get-tuple-element.38.refs_0_, f32[280,128]{1,0:T(8,128)S(1)} %collective-permute-done.5.refs_1_, f32[280,128]{1,0:T(8,128)S(1)} %collective-permute-done.6.refs_2_), custom_call_target="tpu_custom_call" | custom-call | tf_op jit(solution)/shard_map/pallas_call | solution.py:46
  35.7 0.1 collective-permute-start.7
  35.8 2.4 %collective-permute-start.8 = (f32[936,128]{1,0:T(8,128)S(1)}, f32[936,128]{1,0:T(8,128)S(1)}, u32[]{:S(2)}, u32[]{:S(2)}) collective-permute-start(f32[936,128]{1,0:T(8,128)S(1)} %get-tuple-element.44), channel_id=1, source_target_pairs={{0,0},{4,8},{8,4},{12,12},{1,1},{5,9},{9,5},{13,13},{2,2},{6,10},{... | collective-permute-start | bytes 1437704 | tf_op jit(solution)/shard_map/ppermute | solution.py:29
  38.2 0.6 collective-permute-start.10
  38.8 8.0 %collective-permute-done.10.refs_3_ = f32[160,128]{1,0:T(8,128)S(1)} collective-permute-done((f32[160,128]{1,0:T(8,128)S(1)}, f32[160,128]{1,0:T(8,128)S(1)}, u32[]{:S(2)}, u32[]{:S(2)}) %collective-permute-start.10) | collective-permute-done | bytes 81952 | tf_op jit(solution)/shard_map/ppermute | solution.py:524
  46.7 0.0 collective-permute-done.9.refs_1_
  46.7 1.0 %shard_map.87.refs_5_ = f32[1920,256]{1,0:T(8,128)S(1)} custom-call(f32[960,128]{1,0:T(8,128)S(1)} %get-tuple-element.46.refs_0_, f32[960,128]{1,0:T(8,128)S(1)} %collective-permute-done.9.refs_1_, f32[160,128]{1,0:T(8,128)S(1)} %get-tuple-element.47.refs_2_, f32[160,128]{1,0:T(8,128)S(1)} %collective-permute-done.10.refs_3_, ...), custom_call_target="tpu_custom_call" | custom-call | tf_op jit(solution)/shard_map/pallas_call | solution.py:46
  47.7 0.0 collective-permute-done.7.refs_2_
  47.7 0.2 collective-permute-done.8.refs_3_
  47.9 7.1 %shard_map.88 = (f32[960,128]{1,0:T(8,128)S(1)}, f32[576,128]{1,0:T(8,128)S(1)}, f32[80,128]{1,0:T(8,128)S(1)}, f32[80,128]{1,0:T(8,128)S(1)}) custom-call(f32[1920,128]{1,0:T(8,128)S(1)} %get-tuple-element.41.refs_0_, f32[1920,128]{1,0:T(8,128)S(1)} %get-tuple-element.42.refs_1_, f32[936,128]{1,0:T(8,128)S(1)} %collective-permute-done.7.refs_2_, ...), custom_call_target="tpu_custom_call" | custom-call | tf_op jit(solution)/shard_map/pallas_call | solution.py:46
  55.0 3.5 %collective-permute-start.11 = (f32[80,128]{1,0:T(8,128)S(1)}, f32[80,128]{1,0:T(8,128)S(1)}, u32[]{:S(2)}, u32[]{:S(2)}) collective-permute-start(f32[80,128]{1,0:T(8,128)S(1)} %get-tuple-element.49), channel_id=1, source_target_pairs={{0,1},{1,0},{2,3},{3,2},{4,5},{5,4},{6,7},{7,6},{8,9},{9,8},{10,11... | collective-permute-start | bytes 122888 | tf_op jit(solution)/shard_map/ppermute | solution.py:29
  58.5 0.8 %collective-permute-start.12 = (f32[80,128]{1,0:T(8,128)S(1)}, f32[80,128]{1,0:T(8,128)S(1)}, u32[]{:S(2)}, u32[]{:S(2)}) collective-permute-start(f32[80,128]{1,0:T(8,128)S(1)} %get-tuple-element.50), channel_id=1, source_target_pairs={{0,3},{1,2},{2,1},{3,0},{4,7},{5,6},{6,5},{7,4},{8,11},{9,10},{10,... | collective-permute-start | bytes 122888 | tf_op jit(solution)/shard_map/ppermute | solution.py:29
  59.3 0.0 collective-permute-done.11.refs_1_
  59.3 2.7 %collective-permute-done.12.refs_2_ = f32[80,128]{1,0:T(8,128)S(1)} collective-permute-done((f32[80,128]{1,0:T(8,128)S(1)}, f32[80,128]{1,0:T(8,128)S(1)}, u32[]{:S(2)}, u32[]{:S(2)}) %collective-permute-start.12) | collective-permute-done | bytes 40992 | tf_op jit(solution)/shard_map/ppermute | solution.py:29
  62.1 0.4 shard_map.89
  62.4 0.1 collective-permute-start.13
  62.5 2.2 %collective-permute-start.14 = (f32[192,128]{1,0:T(8,128)S(1)}, f32[192,128]{1,0:T(8,128)S(1)}, u32[]{:S(2)}, u32[]{:S(2)}) collective-permute-start(f32[192,128]{1,0:T(8,128)S(1)} %get-tuple-element.53), channel_id=1, source_target_pairs={{0,0},{4,8},{8,4},{12,12},{1,1},{5,9},{9,5},{13,13},{2,2},{6,10},{... | collective-permute-start | bytes 294920 | tf_op jit(solution)/shard_map/ppermute | solution.py:29
  64.7 2.6 %collective-permute-done.13.refs_1_ = f32[192,128]{1,0:T(8,128)S(1)} collective-permute-done((f32[192,128]{1,0:T(8,128)S(1)}, f32[192,128]{1,0:T(8,128)S(1)}, u32[]{:S(2)}, u32[]{:S(2)}) %collective-permute-start.13) | collective-permute-done | bytes 98336 | tf_op jit(solution)/shard_map/ppermute | solution.py:29
  67.3 1.9 %collective-permute-done.14.refs_2_ = f32[192,128]{1,0:T(8,128)S(1)} collective-permute-done((f32[192,128]{1,0:T(8,128)S(1)}, f32[192,128]{1,0:T(8,128)S(1)}, u32[]{:S(2)}, u32[]{:S(2)}) %collective-permute-start.14) | collective-permute-done | bytes 98336 | tf_op jit(solution)/shard_map/ppermute | solution.py:29
  69.2 0.8 %shard_map.90 = f32[24,24,128]{2,1,0:T(8,128)} custom-call(f32[960,128]{1,0:T(8,128)S(1)} %get-tuple-element.51.refs_0_, f32[192,128]{1,0:T(8,128)S(1)} %collective-permute-done.13.refs_1_, f32[192,128]{1,0:T(8,128)S(1)} %collective-permute-done.14.refs_2_, f32[576,128]{1,0:T(8,128)S(1)} %get-tuple-element.54.refs_3_), custom_call_target="tpu_custom_call" | custom-call | tf_op jit(solution)/shard_map/pallas_call | solution.py:46
  (10 shorter events, 0.1 us)
Async XLA Ops:
  0.0 9.0 %copy-start = (f32[24,24,128]{2,1,0:T(8,128)S(1)}, f32[24,24,128]{2,1,0:T(8,128)}, u32[]{:S(2)}) copy-start(f32[24,24,128]{2,1,0:T(8,128)} %refs_0_.3) | copy-start | bytes 884740
  0.0 6.7 %copy-start.2 = (f32[40,40]{1,0:T(8,128)S(1)}, f32[40,40]{1,0:T(8,128)}, u32[]{:S(2)}) copy-start(f32[40,40]{1,0:T(8,128)} %param.11) | copy-start | bytes 19204
  0.0 6.3 %copy-start.3 = (f32[40]{0:T(128)S(1)}, f32[40]{0:T(128)}, u32[]{:S(2)}) copy-start(f32[40]{0:T(128)} %param.13) | copy-start | bytes 484
  0.0 9.0 %copy-start.1 = (f32[24,24,128]{2,1,0:T(8,128)S(1)}, f32[24,24,128]{2,1,0:T(8,128)}, u32[]{:S(2)}) copy-start(f32[24,24,128]{2,1,0:T(8,128)} %refs_2_.3) | copy-start | bytes 884740
  0.0 9.0 %collective-permute-start = (f32[24,24,128]{2,1,0:T(8,128)}, f32[24,24,128]{2,1,0:T(8,128)S(1)}, u32[]{:S(2)}, u32[]{:S(2)}) collective-permute-start(f32[24,24,128]{2,1,0:T(8,128)} %refs_0_.3), channel_id=1, source_target_pairs={{16,0},{0,16},{17,1},{1,17},{18,2},{2,18},{19,3},{3,19},{20,4},{4,... | collective-permute-start | bytes 884744 | tf_op jit(solution)/shard_map/ppermute | solution.py:524
  9.1 8.0 %collective-permute-start.1 = (f32[72,8,128]{2,1,0:T(8,128)S(1)}, f32[72,8,128]{2,1,0:T(8,128)S(1)}, u32[]{:S(2)}, u32[]{:S(2)}) collective-permute-start(f32[72,8,128]{2,1,0:T(8,128)S(1)} %get-tuple-element.30), channel_id=1, source_target_pairs={{0,4},{4,0},{8,12},{12,8},{1,5},{5,1},{9,13},{13,9},{2,6},{6,2},{1... | collective-permute-start | bytes 884744 | tf_op jit(solution)/shard_map/ppermute | solution.py:29
  10.7 9.5 %collective-permute-start.2 = (f32[72,8,128]{2,1,0:T(8,128)S(1)}, f32[72,8,128]{2,1,0:T(8,128)S(1)}, u32[]{:S(2)}, u32[]{:S(2)}) collective-permute-start(f32[72,8,128]{2,1,0:T(8,128)S(1)} %get-tuple-element.31), channel_id=1, source_target_pairs={{0,0},{4,8},{8,4},{12,12},{1,1},{5,9},{9,5},{13,13},{2,2},{6,10},{... | collective-permute-start | bytes 884744 | tf_op jit(solution)/shard_map/ppermute | solution.py:29
  21.1 1.8 %collective-permute-start.3 = (f32[200,128]{1,0:T(8,128)S(1)}, f32[200,128]{1,0:T(8,128)S(1)}, u32[]{:S(2)}, u32[]{:S(2)}) collective-permute-start(f32[200,128]{1,0:T(8,128)S(1)} %get-tuple-element.33), channel_id=1, source_target_pairs={{0,1},{1,0},{2,3},{3,2},{4,5},{5,4},{6,7},{7,6},{8,9},{9,8},{10,11... | collective-permute-start | bytes 307208 | tf_op jit(solution)/shard_map/ppermute | solution.py:29
  21.2 4.6 %collective-permute-start.4 = (f32[200,128]{1,0:T(8,128)S(1)}, f32[200,128]{1,0:T(8,128)S(1)}, u32[]{:S(2)}, u32[]{:S(2)}) collective-permute-start(f32[200,128]{1,0:T(8,128)S(1)} %get-tuple-element.34), channel_id=1, source_target_pairs={{0,3},{1,2},{2,1},{3,0},{4,7},{5,6},{6,5},{7,4},{8,11},{9,10},{10,... | collective-permute-start | bytes 307208 | tf_op jit(solution)/shard_map/ppermute | solution.py:29
  31.6 2.7 %collective-permute-start.5 = (f32[280,128]{1,0:T(8,128)S(1)}, f32[280,128]{1,0:T(8,128)S(1)}, u32[]{:S(2)}, u32[]{:S(2)}) collective-permute-start(f32[280,128]{1,0:T(8,128)S(1)} %get-tuple-element.39), channel_id=1, source_target_pairs={{0,1},{1,0},{2,3},{3,2},{4,5},{5,4},{6,7},{7,6},{8,9},{9,8},{10,11... | collective-permute-start | bytes 430088 | tf_op jit(solution)/shard_map/ppermute | solution.py:29
  32.1 2.2 %collective-permute-start.6 = (f32[280,128]{1,0:T(8,128)S(1)}, f32[280,128]{1,0:T(8,128)S(1)}, u32[]{:S(2)}, u32[]{:S(2)}) collective-permute-start(f32[280,128]{1,0:T(8,128)S(1)} %get-tuple-element.40), channel_id=1, source_target_pairs={{0,0},{1,2},{2,1},{3,3},{4,4},{5,6},{6,5},{7,7},{8,8},{9,10},{10,9... | collective-permute-start | bytes 430088 | tf_op jit(solution)/shard_map/ppermute | solution.py:29
  32.7 14.0 %collective-permute-start.9 = (f32[960,128]{1,0:T(8,128)S(1)}, f32[960,128]{1,0:T(8,128)S(1)}, u32[]{:S(2)}, u32[]{:S(2)}) collective-permute-start(f32[960,128]{1,0:T(8,128)S(1)} %get-tuple-element.46.refs_0_), channel_id=1, source_target_pairs={{16,0},{0,16},{17,1},{1,17},{18,2},{2,18},{19,3},{3,19},{20,4},{4,... | collective-permute-start | bytes 1474568 | tf_op jit(solution)/shard_map/ppermute | solution.py:524
  35.7 12.0 %collective-permute-start.7 = (f32[936,128]{1,0:T(8,128)S(1)}, f32[936,128]{1,0:T(8,128)S(1)}, u32[]{:S(2)}, u32[]{:S(2)}) collective-permute-start(f32[936,128]{1,0:T(8,128)S(1)} %get-tuple-element.43.refs_4_), channel_id=1, source_target_pairs={{0,4},{4,0},{8,12},{12,8},{1,5},{5,1},{9,13},{13,9},{2,6},{6,2},{1... | collective-permute-start | bytes 1437704 | tf_op jit(solution)/shard_map/ppermute | solution.py:29
  35.8 12.2 %collective-permute-start.8 = (f32[936,128]{1,0:T(8,128)S(1)}, f32[936,128]{1,0:T(8,128)S(1)}, u32[]{:S(2)}, u32[]{:S(2)}) collective-permute-start(f32[936,128]{1,0:T(8,128)S(1)} %get-tuple-element.44), channel_id=1, source_target_pairs={{0,0},{4,8},{8,4},{12,12},{1,1},{5,9},{9,5},{13,13},{2,2},{6,10},{... | collective-permute-start | bytes 1437704 | tf_op jit(solution)/shard_map/ppermute | solution.py:29
  38.2 8.6 %collective-permute-start.10 = (f32[160,128]{1,0:T(8,128)S(1)}, f32[160,128]{1,0:T(8,128)S(1)}, u32[]{:S(2)}, u32[]{:S(2)}) collective-permute-start(f32[160,128]{1,0:T(8,128)S(1)} %get-tuple-element.47.refs_2_), channel_id=1, source_target_pairs={{16,0},{0,16},{17,1},{1,17},{18,2},{2,18},{19,3},{3,19},{20,4},{4,... | collective-permute-start | bytes 245768 | tf_op jit(solution)/shard_map/ppermute | solution.py:524
  55.0 4.3 %collective-permute-start.11 = (f32[80,128]{1,0:T(8,128)S(1)}, f32[80,128]{1,0:T(8,128)S(1)}, u32[]{:S(2)}, u32[]{:S(2)}) collective-permute-start(f32[80,128]{1,0:T(8,128)S(1)} %get-tuple-element.49), channel_id=1, source_target_pairs={{0,1},{1,0},{2,3},{3,2},{4,5},{5,4},{6,7},{7,6},{8,9},{9,8},{10,11... | collective-permute-start | bytes 122888 | tf_op jit(solution)/shard_map/ppermute | solution.py:29
  58.5 3.6 %collective-permute-start.12 = (f32[80,128]{1,0:T(8,128)S(1)}, f32[80,128]{1,0:T(8,128)S(1)}, u32[]{:S(2)}, u32[]{:S(2)}) collective-permute-start(f32[80,128]{1,0:T(8,128)S(1)} %get-tuple-element.50), channel_id=1, source_target_pairs={{0,3},{1,2},{2,1},{3,0},{4,7},{5,6},{6,5},{7,4},{8,11},{9,10},{10,... | collective-permute-start | bytes 122888 | tf_op jit(solution)/shard_map/ppermute | solution.py:29
  62.4 4.9 %collective-permute-start.13 = (f32[192,128]{1,0:T(8,128)S(1)}, f32[192,128]{1,0:T(8,128)S(1)}, u32[]{:S(2)}, u32[]{:S(2)}) collective-permute-start(f32[192,128]{1,0:T(8,128)S(1)} %get-tuple-element.52), channel_id=1, source_target_pairs={{0,4},{4,0},{8,12},{12,8},{1,5},{5,1},{9,13},{13,9},{2,6},{6,2},{1... | collective-permute-start | bytes 294920 | tf_op jit(solution)/shard_map/ppermute | solution.py:29
  62.5 6.7 %collective-permute-start.14 = (f32[192,128]{1,0:T(8,128)S(1)}, f32[192,128]{1,0:T(8,128)S(1)}, u32[]{:S(2)}, u32[]{:S(2)}) collective-permute-start(f32[192,128]{1,0:T(8,128)S(1)} %get-tuple-element.53), channel_id=1, source_target_pairs={{0,0},{4,8},{8,4},{12,12},{1,1},{5,9},{9,5},{13,13},{2,2},{6,10},{... | collective-permute-start | bytes 294920 | tf_op jit(solution)/shard_map/ppermute | solution.py:29
